TPU v7x, 32 devices: a whole 2x2x4 slice. The times are simulated.
32 devices in a mesh: gx: 2 (over x), gy: 4 (over z), gz: 4 (over y, core).
Axes of the slice: x: 2, y: 2, z: 4, core: 2. Of those that a mesh axis runs over, the one named last changes fastest.
Arguments:
- fields: bfloat16 [7, 16, 32, 64], P(None, 'gx', 'gy', 'gz'), may hold values from -6 to 6
- grain_ids: int32 [16, 32, 64], P('gx', 'gy', 'gz'), may hold values from 0 to 127
- material_table: bfloat16 [128, 64], replicated, may hold values from -6 to 6
- input_weight: bfloat16 [64, 7], replicated, may hold values from -2 to 2
- kernel_fine: bfloat16 [64, 1728], replicated, may hold values from -0.15625 to 0.15625
- kernel_down: bfloat16 [128, 1728], replicated, may hold values from -0.15625 to 0.15625
- kernel_bottle: bfloat16 [256, 3456], P('gx'), may hold values from -0.109375 to 0.109375
- cotangent: bfloat16 [256, 8, 16, 32], P('gx', None, 'gy', 'gz'), may hold values from -6 to 6
Outputs:
- bottle: bfloat16 [256, 8, 16, 32], P('gx', None, 'gy', 'gz')
- grad_down: float32 [128, 1728], P('gx', ('gy', 'gz'))
- grad_bottle: float32 [256, 3456], P('gx', ('gy', 'gz'))
Inputs may be any that keep to these rules, and one draw needn't show every extreme that they name: `grain_ids`: each voxel's grain, a row of material_table.
All inputs are finite; a program needn't handle non-finite values.
Results may differ from a plain program's by a relative error of at most 0.028.
Values may be sent and summed in bfloat16 or wider, within the bound.
No kernel may reach another device: no remote copies, remote signals or barrier semaphores. Data moves between devices by JAX's collectives and lax.ppermute only.
A program may use at most 64 MiB of HBM per device.

v0:
```python
import math

import jax
import jax.numpy as jnp
from jax import lax
from jax.sharding import PartitionSpec as P


def with_halo(block, sides, width):
    for axis, dim in sides:
        count = lax.axis_size(axis)
        forward = [(i, i + 1) for i in range(count - 1)]
        backward = [(target, source) for source, target in forward]
        low = lax.ppermute(
            lax.slice_in_dim(block, block.shape[dim] - width, None, axis=dim), axis, forward
        )
        high = lax.ppermute(lax.slice_in_dim(block, 0, width, axis=dim), axis, backward)
        block = jnp.concatenate([low, block, high], axis=dim)
    return block


def tap_offsets():
    offsets = []
    for along_x in range(3):
        for along_y in range(3):
            for along_z in range(3):
                offsets.append((along_x, along_y, along_z))
    return offsets


def silu_grad(values):
    sigmoid = jax.nn.sigmoid(values)
    return sigmoid * (1.0 + values * (1.0 - sigmoid))


def take_window(padded, offset, out_shape, stride):
    limits = (
        padded.shape[0],
        offset[0] + stride * (out_shape[0] - 1) + 1,
        offset[1] + stride * (out_shape[1] - 1) + 1,
        offset[2] + stride * (out_shape[2] - 1) + 1,
    )
    sliced = lax.slice(
        padded, (0, offset[0], offset[1], offset[2]), limits, (1, stride, stride, stride)
    )
    return sliced.reshape(padded.shape[0], -1)


def correlate(padded, kernel, out_shape, stride):
    channels = padded.shape[0]
    outputs = kernel.shape[0]
    kernel_taps = kernel.reshape(outputs, 27, channels)
    running = jnp.zeros((outputs, out_shape[0] * out_shape[1] * out_shape[2]), jnp.float32)
    for number, offset in enumerate(tap_offsets()):
        sliced = take_window(padded, offset, out_shape, stride)
        running = running + jnp.dot(
            kernel_taps[:, number], sliced, preferred_element_type=jnp.float32
        )
    return running.reshape((outputs,) + tuple(out_shape))


def transpose_correlate(padded, kernel, out_shape):
    outputs = kernel.shape[0]
    channels = kernel.shape[1] // 27
    kernel_taps = kernel.reshape(outputs, 27, channels)
    running = jnp.zeros((channels, out_shape[0] * out_shape[1] * out_shape[2]), jnp.float32)
    for number, offset in enumerate(tap_offsets()):
        flipped = (2 - offset[0], 2 - offset[1], 2 - offset[2])
        sliced = take_window(padded, flipped, out_shape, 1)
        running = running + lax.dot_general(
            kernel_taps[:, number],
            sliced,
            (((0,), (0,)), ((), ())),
            preferred_element_type=jnp.float32,
        )
    return running.reshape((channels,) + tuple(out_shape))


def kernel_gradient(padded, grad_out, stride):
    outputs = grad_out.shape[0]
    channels = padded.shape[0]
    out_shape = grad_out.shape[1:]
    grad_flat = grad_out.reshape(outputs, -1)
    per_tap = []
    for offset in tap_offsets():
        sliced = take_window(padded, offset, out_shape, stride)
        per_tap.append(
            lax.dot_general(
                grad_flat, sliced, (((1,), (1,)), ((), ())), preferred_element_type=jnp.float32
            )
        )
    return jnp.stack(per_tap, axis=1).reshape(outputs, 27 * channels)


def interior_mask(out_shape):
    along_x = lax.broadcasted_iota(jnp.int32, out_shape, 0)
    along_y = lax.broadcasted_iota(jnp.int32, out_shape, 1)
    along_z = lax.broadcasted_iota(jnp.int32, out_shape, 2)
    keep_cells = (along_x > 0) | (lax.axis_index("gx") > 0)
    keep_cells = keep_cells & ((along_y > 0) | (lax.axis_index("gy") > 0))
    keep_cells = keep_cells & ((along_z > 0) | (lax.axis_index("gz") > 0))
    return keep_cells


def per_device(
    fields,
    grain_ids,
    material_table,
    input_weight,
    kernel_fine,
    kernel_down,
    kernel_bottle,
    cotangent,
):
    grains = material_table.shape[0]
    brick_shape = grain_ids.shape
    onehot = (grain_ids.reshape(1, -1) == lax.broadcasted_iota(jnp.int32, (grains, 1), 0)).astype(
        jnp.bfloat16
    )
    material = jnp.dot(material_table.T, onehot, preferred_element_type=jnp.float32)
    mixture = (
        jnp.dot(
            input_weight, fields.reshape(fields.shape[0], -1), preferred_element_type=jnp.float32
        )
        + material
    )
    embedded = jax.nn.silu(mixture).astype(jnp.bfloat16).reshape((-1,) + tuple(brick_shape))
    rimmed = with_halo(embedded, (("gx", 1), ("gy", 2), ("gz", 3)), 2)
    extended_shape = (brick_shape[0] + 1, brick_shape[1] + 1, brick_shape[2] + 1)
    fine_values = jax.nn.silu(correlate(rimmed, kernel_fine, extended_shape, 1))
    fine_ext = jnp.where(interior_mask(extended_shape)[None], fine_values, 0.0).astype(jnp.bfloat16)
    coarse_shape = (brick_shape[0] // 2, brick_shape[1] // 2, brick_shape[2] // 2)
    pre_down = correlate(fine_ext, kernel_down, coarse_shape, 2)
    coarse = jax.nn.silu(pre_down).astype(jnp.bfloat16)
    voxel_count = (
        coarse_shape[0]
        * lax.axis_size("gx")
        * coarse_shape[1]
        * lax.axis_size("gy")
        * coarse_shape[2]
        * lax.axis_size("gz")
    )
    grad_scale = 1.0 / math.sqrt(voxel_count)
    slab_plain = lax.all_gather(coarse, "gx", axis=1, tiled=True)
    slab_input = with_halo(slab_plain, (("gy", 2), ("gz", 3)), 1)
    slab_input = jnp.pad(slab_input, ((0, 0), (1, 1), (0, 0), (0, 0)))
    slab_shape = (slab_input.shape[1] - 2, coarse_shape[1], coarse_shape[2])
    pre_slab = correlate(slab_input, kernel_bottle, slab_shape, 1)
    bottle = jax.nn.silu(pre_slab).astype(jnp.bfloat16)
    grad_pre_bottle = (cotangent.astype(jnp.float32) * silu_grad(pre_slab)).astype(jnp.bfloat16)
    grad_padded = with_halo(grad_pre_bottle, (("gy", 2), ("gz", 3)), 1)
    grad_padded = jnp.pad(grad_padded, ((0, 0), (1, 1), (0, 0), (0, 0)))
    partial_act = transpose_correlate(grad_padded, kernel_bottle, slab_shape)
    grad_down_act = lax.psum_scatter(
        partial_act.astype(jnp.bfloat16), "gx", scatter_dimension=1, tiled=True
    ).astype(jnp.float32)
    bottle_part = kernel_gradient(slab_input, grad_pre_bottle, 1) * grad_scale
    grad_pre_down = (grad_down_act * silu_grad(pre_down)).astype(jnp.bfloat16)
    down_part = kernel_gradient(fine_ext, grad_pre_down, 2) * grad_scale
    down_part = lax.psum_scatter(
        down_part.astype(jnp.bfloat16), "gx", scatter_dimension=0, tiled=True
    ).astype(jnp.float32)
    grad_down, grad_bottle = (
        lax.psum_scatter(
            down_part.astype(jnp.bfloat16), ("gy", "gz"), scatter_dimension=1, tiled=True
        ).astype(jnp.float32),
        lax.psum_scatter(
            bottle_part.astype(jnp.bfloat16), ("gy", "gz"), scatter_dimension=1, tiled=True
        ).astype(jnp.float32),
    )
    return (bottle, grad_down, grad_bottle)


def solution(mesh):
    placed = (
        P(None, "gx", "gy", "gz"),
        P("gx", "gy", "gz"),
        P(),
        P(),
        P(),
        P(),
        P("gx", None),
        P("gx", None, "gy", "gz"),
    )
    return jax.shard_map(
        per_device,
        mesh=mesh,
        in_specs=placed,
        out_specs=(P("gx", None, "gy", "gz"), P("gx", ("gy", "gz")), P("gx", ("gy", "gz"))),
        check_vma=False,
    )
```

profile of v0, /device:TPU:0, one launch (start us, length us, event | category | flops | bytes accessed | tf_op | source)
XLA Modules:
  0.0 368.0 jit_solution(15244783112159213757)
XLA Ops:
  7.2 1.1 reshape.425
  10.6 4.9 %collective-permute-start = (bf16[64,2,8,16]{0,3,2,1:T(8,128)(2,1)S(1)}, bf16[64,2,8,16]{0,3,2,1:T(8,128)(2,1)S(1)}, u32[]{:S(2)}, u32[]{:S(2)}) collective-permute-start(bf16[64,2,8,16]{0,3,2,1:T(8,128)(2,1)S(1)} %get-tuple-element.63), channel_id=1, source_target_pairs={{0,16},{1,17},{2,18},{3,19},{4,20},{5,21},{6,22},{7,23},{8,24},{9,... | collective-permute-start | bytes 98312 | tf_op jit(solution)/shard_map/ppermute | solution.py:14
  15.4 1.3 collective-permute-start.1
  18.1 1.3 fusion.191
  19.4 2.2 collective-permute-done.1
  21.7 3.5 collective-permute-start.2
  25.1 1.3 collective-permute-start.3
  27.3 4.3 %collective-permute-done.3 = bf16[64,12,2,16]{0,3,2,1:T(8,128)(2,1)S(1)} collective-permute-done((bf16[64,12,2,16]{0,3,2,1:T(8,128)(2,1)S(1)}, bf16[64,12,2,16]{0,3,2,1:T(8,128)(2,1)S(1)}, u32[]{:S(2)}, u32[]{:S(2)}) %collective-permute-start.3) | collective-permute-done | bytes 49184 | tf_op jit(solution)/shard_map/ppermute | solution.py:17
  31.8 1.3 collective-permute-start.4
  33.1 1.5 collective-permute-start.5
  35.3 2.7 collective-permute-done.5
  38.5 3.5 fusion.189
  42.1 1.9 reshape.429
  44.0 1.9 reshape.427
  46.0 2.2 fusion.190
  48.1 1.9 reshape.430
  50.1 2.0 reshape.431
  52.1 1.9 reshape.432
  54.0 2.0 reshape.433
  56.0 1.9 reshape.434
  58.8 2.0 reshape.436
  60.8 2.0 reshape.437
  62.8 2.0 reshape.438
  64.7 1.9 reshape.439
  67.6 2.0 reshape.441
  69.6 2.0 reshape.442
  71.6 1.2 reshape.443
  72.8 1.9 reshape.453
  79.3 2.0 reshape.454
  83.6 1.1 fusion.166
  84.7 1.3 convolution_bitcast_fusion.1
  86.0 1.1 convolution_bitcast_fusion.2
  87.1 1.1 convolution_bitcast_fusion.4
  114.2 4.6 %all_gather.3 = bf16[128,8,4,8]{0,3,2,1:T(8,128)(2,1)S(1)} all-gather(bf16[128,4,4,8]{0,3,2,1:T(8,128)(2,1)S(1)} %multiply_convert_fusion.6), channel_id=1, replica_groups=mesh['gx'=2,'gy'=4,'gz'=4] {'gx'}, dimensions={1}, use_global_device_ids=true | all-gather | bytes 98304 | tf_op jit(solution)/shard_map/all_gather | solution.py:144
  118.8 3.5 collective-permute-start.6
  122.3 1.0 copy.47
  123.3 1.3 collective-permute-start.7
  124.6 4.3 %collective-permute-done.7 = bf16[128,8,1,8]{0,3,2,1:T(8,128)(2,1)S(1)} collective-permute-done((bf16[128,8,1,8]{0,3,2,1:T(8,128)(2,1)S(1)}, bf16[128,8,1,8]{0,3,2,1:T(8,128)(2,1)S(1)}, u32[]{:S(2)}, u32[]{:S(2)}) %collective-permute-start.7) | collective-permute-done | bytes 16416 | tf_op jit(solution)/shard_map/ppermute | solution.py:17
  129.0 2.3 collective-permute-start.8
  131.4 1.3 collective-permute-start.9
  132.8 3.7 collective-permute-done.9
  146.4 3.5 collective-permute-start.10
  149.9 1.3 collective-permute-start.11
  151.4 4.1 %collective-permute-done.11 = bf16[128,8,1,8]{0,3,2,1:T(8,128)(2,1)S(1)} collective-permute-done((bf16[128,8,1,8]{0,3,2,1:T(8,128)(2,1)S(1)}, bf16[128,8,1,8]{0,3,2,1:T(8,128)(2,1)S(1)}, u32[]{:S(2)}, u32[]{:S(2)}) %collective-permute-start.11) | collective-permute-done | bytes 16416 | tf_op jit(solution)/shard_map/ppermute | solution.py:17
  155.6 3.0 collective-permute-start.12
  158.6 1.3 collective-permute-start.13
  160.0 2.7 collective-permute-done.13
  168.8 8.3 %reduce-scatter.7.cloned.1.call-done = bf16[128,4,4,8]{0,3,2,1:T(8,128)(2,1)} async-done(((bf16[128,8,4,8]{0,3,2,1:T(8,128)(2,1)}), bf16[128,4,4,8]{0,3,2,1:T(8,128)(2,1)}) %reduce-scatter.7.cloned.1.call-update) | async-done | bytes 32784 | tf_op jit(solution)/shard_map/reduce_scatter | solution.py:154
  178.1 1.0 fusion.101
  179.0 1.0 fusion.100
  180.0 1.0 fusion.99
  181.0 1.0 fusion.98
  181.9 1.0 fusion.97
  182.9 1.0 fusion.96
  183.8 1.0 fusion.95
  186.7 1.0 fusion.92
  187.7 1.0 fusion.91
  192.5 1.0 copy.75
  194.4 13.2 %reduce-scatter.9.cloned.1.call-done = bf16[64,1728]{1,0:T(8,128)(2,1)} async-done(((bf16[128,1728]{1,0:T(8,128)(2,1)}), bf16[64,1728]{1,0:T(8,128)(2,1)}) %reduce-scatter.9.cloned.1.call-update) | async-done | bytes 221200 | tf_op jit(solution)/shard_map/reduce_scatter | solution.py:160
  207.7 1.1 multiply_convert_fusion
  210.1 90.2 %all-reduce.6.cloned.1.call-done = bf16[64,1728]{1,0:T(8,128)(2,1)} async-done(((bf16[64,1728]{1,0:T(8,128)(2,1)}), bf16[64,1728]{1,0:T(8,128)(2,1)}) %all-reduce.6.cloned.1.call-update) | async-done | bytes 221200
  300.4 1.4 dynamic-slice_convert_fusion
  301.8 58.2 %reduce-scatter.11.cloned.1.call-done = bf16[128,216]{0,1:T(8,128)(2,1)} async-done(((bf16[128,3456]{0,1:T(8,128)(2,1)}), bf16[128,216]{0,1:T(8,128)(2,1)}) %reduce-scatter.11.cloned.1.call-update) | async-done | bytes 55312
  360.0 1.5 convert_element_type.69
  (389 shorter events, 63.9 us)
Async XLA Ops:
  7.2 2.9 copy-start
  7.2 9.6 %copy-start.48 = (bf16[64,1728]{1,0:T(8,128)(2,1)S(1)}, bf16[64,1728]{1,0:T(8,128)(2,1)}, u32[]{:S(2)}) copy-start(bf16[64,1728]{1,0:T(8,128)(2,1)} %param.12) | copy-start | bytes 663556
  7.2 169.9 %reduce-scatter.7.cloned.1.call-start = ((), (), s32[]{:S(2)}) async-start(), calls=%async_computation.3 | async-start | bytes 98304 | tf_op jit(solution)/shard_map/reduce_scatter | solution.py:154
  10.6 8.9 %collective-permute-start = (bf16[64,2,8,16]{0,3,2,1:T(8,128)(2,1)S(1)}, bf16[64,2,8,16]{0,3,2,1:T(8,128)(2,1)S(1)}, u32[]{:S(2)}, u32[]{:S(2)}) collective-permute-start(bf16[64,2,8,16]{0,3,2,1:T(8,128)(2,1)S(1)} %get-tuple-element.63), channel_id=1, source_target_pairs={{0,16},{1,17},{2,18},{3,19},{4,20},{5,21},{6,22},{7,23},{8,24},{9,... | collective-permute-start | bytes 98312 | tf_op jit(solution)/shard_map/ppermute | solution.py:14
  15.4 6.2 %collective-permute-start.1 = (bf16[64,2,8,16]{0,3,2,1:T(8,128)(2,1)S(1)}, bf16[64,2,8,16]{0,3,2,1:T(8,128)(2,1)S(1)}, u32[]{:S(2)}, u32[]{:S(2)}) collective-permute-start(bf16[64,2,8,16]{0,3,2,1:T(8,128)(2,1)S(1)} %get-tuple-element.64), channel_id=1, source_target_pairs={{16,0},{17,1},{18,2},{19,3},{20,4},{21,5},{22,6},{23,7},{24,8},{25... | collective-permute-start | bytes 98312 | tf_op jit(solution)/shard_map/ppermute | solution.py:17
  21.7 5.7 %collective-permute-start.2 = (bf16[64,12,2,16]{0,3,2,1:T(8,128)(2,1)S(1)}, bf16[64,12,2,16]{0,3,2,1:T(8,128)(2,1)S(1)}, u32[]{:S(2)}, u32[]{:S(2)}) collective-permute-start(bf16[64,12,2,16]{0,3,2,1:T(8,128)(2,1)S(1)} %get-tuple-element.61), channel_id=1, source_target_pairs={{0,4},{4,8},{8,12},{1,5},{5,9},{9,13},{2,6},{6,10},{10,14},{3,7},{... | collective-permute-start | bytes 147464 | tf_op jit(solution)/shard_map/ppermute | solution.py:14
  25.1 6.5 %collective-permute-start.3 = (bf16[64,12,2,16]{0,3,2,1:T(8,128)(2,1)S(1)}, bf16[64,12,2,16]{0,3,2,1:T(8,128)(2,1)S(1)}, u32[]{:S(2)}, u32[]{:S(2)}) collective-permute-start(bf16[64,12,2,16]{0,3,2,1:T(8,128)(2,1)S(1)} %get-tuple-element.62), channel_id=1, source_target_pairs={{4,0},{8,4},{12,8},{5,1},{9,5},{13,9},{6,2},{10,6},{14,10},{7,3},{... | collective-permute-start | bytes 147464 | tf_op jit(solution)/shard_map/ppermute | solution.py:17
  31.8 3.5 collective-permute-start.4
  33.1 4.9 %collective-permute-start.5 = (bf16[64,12,12,2]{0,3,2,1:T(2,128)(2,1)S(1)}, bf16[64,12,12,2]{0,3,2,1:T(2,128)(2,1)S(1)}, u32[]{:S(2)}, u32[]{:S(2)}) collective-permute-start(bf16[64,12,12,2]{0,3,2,1:T(2,128)(2,1)S(1)} %get-tuple-element.33), channel_id=1, source_target_pairs={{1,0},{2,1},{3,2},{5,4},{6,5},{7,6},{9,8},{10,9},{11,10},{13,12},{... | collective-permute-start | bytes 110600 | tf_op jit(solution)/shard_map/ppermute | solution.py:17
  50.1 7.9 %copy-start.3 = (bf16[64,9,9,17]{0,3,2,1:T(8,128)(2,1)S(1)}, bf16[64,9,9,17]{0,3,2,1:T(8,128)(2,1)}, u32[]{:S(2)}) copy-start(bf16[64,9,9,17]{0,3,2,1:T(8,128)(2,1)} %get-tuple-element.15) | copy-start | bytes 528772
  58.8 7.9 %copy-start.2 = (bf16[64,9,9,17]{0,3,2,1:T(8,128)(2,1)S(1)}, bf16[64,9,9,17]{0,3,2,1:T(8,128)(2,1)}, u32[]{:S(2)}) copy-start(bf16[64,9,9,17]{0,3,2,1:T(8,128)(2,1)} %get-tuple-element.12) | copy-start | bytes 528772
  67.6 7.1 %copy-start.1 = (bf16[64,9,9,17]{0,3,2,1:T(8,128)(2,1)S(1)}, bf16[64,9,9,17]{0,3,2,1:T(8,128)(2,1)}, u32[]{:S(2)}) copy-start(bf16[64,9,9,17]{0,3,2,1:T(8,128)(2,1)} %get-tuple-element.5) | copy-start | bytes 528772
  76.6 4.7 %copy-start.6 = (bf16[64,9,9,17]{0,3,2,1:T(8,128)(2,1)S(1)}, bf16[64,9,9,17]{0,3,2,1:T(8,128)(2,1)}, u32[]{:S(2)}) copy-start(bf16[64,9,9,17]{0,3,2,1:T(8,128)(2,1)} %get-tuple-element.23) | copy-start | bytes 528772
  77.5 4.7 %copy-start.5 = (bf16[64,9,9,17]{0,3,2,1:T(8,128)(2,1)S(1)}, bf16[64,9,9,17]{0,3,2,1:T(8,128)(2,1)}, u32[]{:S(2)}) copy-start(bf16[64,9,9,17]{0,3,2,1:T(8,128)(2,1)} %get-tuple-element.24) | copy-start | bytes 528772
  78.4 4.0 %copy-start.4 = (bf16[64,9,9,17]{0,3,2,1:T(8,128)(2,1)S(1)}, bf16[64,9,9,17]{0,3,2,1:T(8,128)(2,1)}, u32[]{:S(2)}) copy-start(bf16[64,9,9,17]{0,3,2,1:T(8,128)(2,1)} %get-tuple-element.25) | copy-start | bytes 528772
  81.3 2.3 copy-start.21
  82.4 3.6 copy-start.28
  82.4 4.6 %copy-start.27 = (bf16[64,1377]{0,1:T(8,128)(2,1)S(1)}, bf16[64,1377]{0,1:T(8,128)(2,1)}, u32[]{:S(2)}) copy-start(bf16[64,1377]{0,1:T(8,128)(2,1)} %reshape.450) | copy-start | bytes 528772
  82.6 5.5 %copy-start.26 = (bf16[64,1377]{0,1:T(8,128)(2,1)S(1)}, bf16[64,1377]{0,1:T(8,128)(2,1)}, u32[]{:S(2)}) copy-start(bf16[64,1377]{0,1:T(8,128)(2,1)} %reshape.449) | copy-start | bytes 528772
  82.6 5.5 %copy-start.71 = (bf16[64,1,64]{2,1,0:T(2,128)(2,1)S(1)}, bf16[64,1,64]{2,1,0:T(2,128)(2,1)}, u32[]{:S(2)}) copy-start(bf16[64,1,64]{2,1,0:T(2,128)(2,1)} %get-tuple-element.40) | copy-start | bytes 24580
  83.6 4.8 %copy-start.25 = (bf16[64,1377]{0,1:T(8,128)(2,1)S(1)}, bf16[64,1377]{0,1:T(8,128)(2,1)}, u32[]{:S(2)}) copy-start(bf16[64,1377]{0,1:T(8,128)(2,1)} %reshape.447) | copy-start | bytes 528772
  83.6 4.9 %copy-start.70 = (bf16[64,1,64]{2,1,0:T(2,128)(2,1)S(1)}, bf16[64,1,64]{2,1,0:T(2,128)(2,1)}, u32[]{:S(2)}) copy-start(bf16[64,1,64]{2,1,0:T(2,128)(2,1)} %get-tuple-element.42) | copy-start | bytes 24580
  84.6 4.1 %copy-start.24 = (bf16[64,1377]{0,1:T(8,128)(2,1)S(1)}, bf16[64,1377]{0,1:T(8,128)(2,1)}, u32[]{:S(2)}) copy-start(bf16[64,1377]{0,1:T(8,128)(2,1)} %reshape.446) | copy-start | bytes 528772
  84.6 4.1 %copy-start.69 = (bf16[64,1,64]{2,1,0:T(2,128)(2,1)S(1)}, bf16[64,1,64]{2,1,0:T(2,128)(2,1)}, u32[]{:S(2)}) copy-start(bf16[64,1,64]{2,1,0:T(2,128)(2,1)} %get-tuple-element.43) | copy-start | bytes 24580
  85.9 3.1 copy-start.23
  86.0 3.1 copy-start.68
  87.0 2.3 copy-start.22
  87.1 2.3 copy-start.67
  88.1 1.4 copy-start.66
  88.4 1.4 copy-start.65
  88.7 1.4 copy-start.15
  88.7 1.4 copy-start.64
  89.3 1.2 copy-start.20
  89.3 1.2 copy-start.63
  96.2 14.4 %copy-start.31 = (bf16[128,1728]{0,1:T(8,128)(2,1)S(1)}, bf16[128,1728]{0,1:T(8,128)(2,1)}, u32[]{:S(2)}) copy-start(bf16[128,1728]{0,1:T(8,128)(2,1)} %param.13) | copy-start | bytes 1327108
  97.5 14.4 %copy-start.47 = (bf16[64,4,4,8]{0,3,2,1:T(8,128)(2,1)}, bf16[64,4,4,8]{0,3,2,1:T(8,128)(2,1)S(1)}, u32[]{:S(2)}) copy-start(bf16[64,4,4,8]{0,3,2,1:T(8,128)(2,1)S(1)} %slice.815) | copy-start | bytes 49156
  98.0 14.1 %copy-start.46 = (bf16[64,4,4,8]{0,3,2,1:T(8,128)(2,1)}, bf16[64,4,4,8]{0,3,2,1:T(8,128)(2,1)S(1)}, u32[]{:S(2)}) copy-start(bf16[64,4,4,8]{0,3,2,1:T(8,128)(2,1)S(1)} %slice.817) | copy-start | bytes 49156
  98.4 13.7 %copy-start.45 = (bf16[64,4,4,8]{0,3,2,1:T(8,128)(2,1)}, bf16[64,4,4,8]{0,3,2,1:T(8,128)(2,1)S(1)}, u32[]{:S(2)}) copy-start(bf16[64,4,4,8]{0,3,2,1:T(8,128)(2,1)S(1)} %slice.819) | copy-start | bytes 49156
  98.8 13.3 %copy-start.44 = (bf16[64,4,4,8]{0,3,2,1:T(8,128)(2,1)}, bf16[64,4,4,8]{0,3,2,1:T(8,128)(2,1)S(1)}, u32[]{:S(2)}) copy-start(bf16[64,4,4,8]{0,3,2,1:T(8,128)(2,1)S(1)} %slice.821) | copy-start | bytes 49156
  99.2 13.0 %copy-start.43 = (bf16[64,4,4,8]{0,3,2,1:T(8,128)(2,1)}, bf16[64,4,4,8]{0,3,2,1:T(8,128)(2,1)S(1)}, u32[]{:S(2)}) copy-start(bf16[64,4,4,8]{0,3,2,1:T(8,128)(2,1)S(1)} %slice.823) | copy-start | bytes 49156
  99.9 12.4 %copy-start.42 = (bf16[64,4,4,8]{0,3,2,1:T(8,128)(2,1)}, bf16[64,4,4,8]{0,3,2,1:T(8,128)(2,1)S(1)}, u32[]{:S(2)}) copy-start(bf16[64,4,4,8]{0,3,2,1:T(8,128)(2,1)S(1)} %slice.825) | copy-start | bytes 49156
  100.5 11.8 %copy-start.41 = (bf16[64,4,4,8]{0,3,2,1:T(8,128)(2,1)}, bf16[64,4,4,8]{0,3,2,1:T(8,128)(2,1)S(1)}, u32[]{:S(2)}) copy-start(bf16[64,4,4,8]{0,3,2,1:T(8,128)(2,1)S(1)} %slice.827) | copy-start | bytes 49156
  101.3 11.1 %copy-start.40 = (bf16[64,4,4,8]{0,3,2,1:T(8,128)(2,1)}, bf16[64,4,4,8]{0,3,2,1:T(8,128)(2,1)S(1)}, u32[]{:S(2)}) copy-start(bf16[64,4,4,8]{0,3,2,1:T(8,128)(2,1)S(1)} %slice.829) | copy-start | bytes 49156
  101.7 10.7 %copy-start.39 = (bf16[64,4,4,8]{0,3,2,1:T(8,128)(2,1)}, bf16[64,4,4,8]{0,3,2,1:T(8,128)(2,1)S(1)}, u32[]{:S(2)}) copy-start(bf16[64,4,4,8]{0,3,2,1:T(8,128)(2,1)S(1)} %slice.831) | copy-start | bytes 49156
  102.1 10.4 %copy-start.38 = (bf16[64,4,4,8]{0,3,2,1:T(8,128)(2,1)}, bf16[64,4,4,8]{0,3,2,1:T(8,128)(2,1)S(1)}, u32[]{:S(2)}) copy-start(bf16[64,4,4,8]{0,3,2,1:T(8,128)(2,1)S(1)} %slice.833) | copy-start | bytes 49156
  102.6 10.0 %copy-start.37 = (bf16[64,4,4,8]{0,3,2,1:T(8,128)(2,1)}, bf16[64,4,4,8]{0,3,2,1:T(8,128)(2,1)S(1)}, u32[]{:S(2)}) copy-start(bf16[64,4,4,8]{0,3,2,1:T(8,128)(2,1)S(1)} %slice.835) | copy-start | bytes 49156
  103.0 9.6 %copy-start.36 = (bf16[64,4,4,8]{0,3,2,1:T(8,128)(2,1)}, bf16[64,4,4,8]{0,3,2,1:T(8,128)(2,1)S(1)}, u32[]{:S(2)}) copy-start(bf16[64,4,4,8]{0,3,2,1:T(8,128)(2,1)S(1)} %slice.837) | copy-start | bytes 49156
  103.4 9.3 %copy-start.34 = (bf16[64,4,4,8]{0,3,2,1:T(8,128)(2,1)}, bf16[64,4,4,8]{0,3,2,1:T(8,128)(2,1)S(1)}, u32[]{:S(2)}) copy-start(bf16[64,4,4,8]{0,3,2,1:T(8,128)(2,1)S(1)} %slice.839) | copy-start | bytes 49156
  103.9 8.8 %copy-start.32 = (bf16[64,4,4,8]{0,3,2,1:T(8,128)(2,1)}, bf16[64,4,4,8]{0,3,2,1:T(8,128)(2,1)S(1)}, u32[]{:S(2)}) copy-start(bf16[64,4,4,8]{0,3,2,1:T(8,128)(2,1)S(1)} %slice.841) | copy-start | bytes 49156
  111.7 10.6 %copy-start.30 = (bf16[128,3456]{1,0:T(8,128)(2,1)S(1)}, bf16[128,3456]{1,0:T(8,128)(2,1)}, u32[]{:S(2)}) copy-start(bf16[128,3456]{1,0:T(8,128)(2,1)} %param.14) | copy-start | bytes 2654212
  118.8 5.8 %collective-permute-start.6 = (bf16[128,8,1,8]{0,3,2,1:T(8,128)(2,1)S(1)}, bf16[128,8,1,8]{0,3,2,1:T(8,128)(2,1)S(1)}, u32[]{:S(2)}, u32[]{:S(2)}) collective-permute-start(bf16[128,8,1,8]{0,3,2,1:T(8,128)(2,1)S(1)} %get-tuple-element.132), channel_id=1, source_target_pairs={{0,4},{4,8},{8,12},{1,5},{5,9},{9,13},{2,6},{6,10},{10,14},{3,7},{... | collective-permute-start | bytes 49160 | tf_op jit(solution)/shard_map/ppermute | solution.py:14
  123.3 5.6 %collective-permute-start.7 = (bf16[128,8,1,8]{0,3,2,1:T(8,128)(2,1)S(1)}, bf16[128,8,1,8]{0,3,2,1:T(8,128)(2,1)S(1)}, u32[]{:S(2)}, u32[]{:S(2)}) collective-permute-start(bf16[128,8,1,8]{0,3,2,1:T(8,128)(2,1)S(1)} %get-tuple-element.131), channel_id=1, source_target_pairs={{4,0},{8,4},{12,8},{5,1},{9,5},{13,9},{6,2},{10,6},{14,10},{7,3},{... | collective-permute-start | bytes 49160 | tf_op jit(solution)/shard_map/ppermute | solution.py:17
  129.0 3.8 %collective-permute-start.8 = (bf16[128,8,6,1]{0,3,2,1:T(2,128)(2,1)S(1)}, bf16[128,8,6,1]{0,3,2,1:T(2,128)(2,1)S(1)}, u32[]{:S(2)}, u32[]{:S(2)}) collective-permute-start(bf16[128,8,6,1]{0,3,2,1:T(2,128)(2,1)S(1)} %get-tuple-element.122), channel_id=1, source_target_pairs={{0,1},{1,2},{2,3},{4,5},{5,6},{6,7},{8,9},{9,10},{10,11},{12,13},{... | collective-permute-start | bytes 36872 | tf_op jit(solution)/shard_map/ppermute | solution.py:14
  131.4 5.1 %collective-permute-start.9 = (bf16[128,8,6,1]{0,3,2,1:T(2,128)(2,1)S(1)}, bf16[128,8,6,1]{0,3,2,1:T(2,128)(2,1)S(1)}, u32[]{:S(2)}, u32[]{:S(2)}) collective-permute-start(bf16[128,8,6,1]{0,3,2,1:T(2,128)(2,1)S(1)} %get-tuple-element.123), channel_id=1, source_target_pairs={{1,0},{2,1},{3,2},{5,4},{6,5},{7,6},{9,8},{10,9},{11,10},{13,12},{... | collective-permute-start | bytes 36872 | tf_op jit(solution)/shard_map/ppermute | solution.py:17
  146.4 5.0 %collective-permute-start.10 = (bf16[128,8,1,8]{0,3,2,1:T(8,128)(2,1)S(1)}, bf16[128,8,1,8]{0,3,2,1:T(8,128)(2,1)S(1)}, u32[]{:S(2)}, u32[]{:S(2)}) collective-permute-start(bf16[128,8,1,8]{0,3,2,1:T(8,128)(2,1)S(1)} %get-tuple-element.126), channel_id=1, source_target_pairs={{0,4},{4,8},{8,12},{1,5},{5,9},{9,13},{2,6},{6,10},{10,14},{3,7},{... | collective-permute-start | bytes 49160 | tf_op jit(solution)/shard_map/ppermute | solution.py:14
  149.9 5.6 %collective-permute-start.11 = (bf16[128,8,1,8]{0,3,2,1:T(8,128)(2,1)S(1)}, bf16[128,8,1,8]{0,3,2,1:T(8,128)(2,1)S(1)}, u32[]{:S(2)}, u32[]{:S(2)}) collective-permute-start(bf16[128,8,1,8]{0,3,2,1:T(8,128)(2,1)S(1)} %get-tuple-element.127), channel_id=1, source_target_pairs={{4,0},{8,4},{12,8},{5,1},{9,5},{13,9},{6,2},{10,6},{14,10},{7,3},{... | collective-permute-start | bytes 49160 | tf_op jit(solution)/shard_map/ppermute | solution.py:17
  155.6 4.4 %collective-permute-start.12 = (bf16[128,8,6,1]{0,3,2,1:T(2,128)(2,1)S(1)}, bf16[128,8,6,1]{0,3,2,1:T(2,128)(2,1)S(1)}, u32[]{:S(2)}, u32[]{:S(2)}) collective-permute-start(bf16[128,8,6,1]{0,3,2,1:T(2,128)(2,1)S(1)} %get-tuple-element.117), channel_id=1, source_target_pairs={{0,1},{1,2},{2,3},{4,5},{5,6},{6,7},{8,9},{9,10},{10,11},{12,13},{... | collective-permute-start | bytes 36872 | tf_op jit(solution)/shard_map/ppermute | solution.py:14
  158.6 4.0 %collective-permute-start.13 = (bf16[128,8,6,1]{0,3,2,1:T(2,128)(2,1)S(1)}, bf16[128,8,6,1]{0,3,2,1:T(2,128)(2,1)S(1)}, u32[]{:S(2)}, u32[]{:S(2)}) collective-permute-start(bf16[128,8,6,1]{0,3,2,1:T(2,128)(2,1)S(1)} %get-tuple-element.118), channel_id=1, source_target_pairs={{1,0},{2,1},{3,2},{5,4},{6,5},{7,6},{9,8},{10,9},{11,10},{13,12},{... | collective-permute-start | bytes 36872 | tf_op jit(solution)/shard_map/ppermute | solution.py:17
  167.4 22.1 %copy-start.35 = (bf16[64,4,4,8]{0,3,2,1:T(8,128)(2,1)S(1)}, bf16[64,4,4,8]{0,3,2,1:T(8,128)(2,1)}, u32[]{:S(2)}) copy-start(bf16[64,4,4,8]{0,3,2,1:T(8,128)(2,1)} %copy-done.34) | copy-start | bytes 49156
  167.4 22.3 %copy-start.33 = (bf16[64,4,4,8]{0,3,2,1:T(8,128)(2,1)S(1)}, bf16[64,4,4,8]{0,3,2,1:T(8,128)(2,1)}, u32[]{:S(2)}) copy-start(bf16[64,4,4,8]{0,3,2,1:T(8,128)(2,1)} %copy-done.32) | copy-start | bytes 49156
  168.5 39.1 %reduce-scatter.9.cloned.1.call-start = ((), (), s32[]{:S(2)}) async-start(), calls=%async_computation.4 | async-start | bytes 688128 | tf_op jit(solution)/shard_map/reduce_scatter | solution.py:160
  193.5 106.9 %all-reduce.6.cloned.1.call-start = ((), (), s32[]{:S(2)}) async-start(), calls=%async_computation.5 | async-start | bytes 458752
  207.7 1.2 copy-start.74
  207.7 152.3 %reduce-scatter.11.cloned.1.call-start = ((), (), s32[]{:S(2)}) async-start(), calls=%async_computation.6 | async-start | bytes 940032
  (29 other events, 30.2 us)
Sparse Core Ops, SparseCore 0:
  168.6 8.4 reduce-scatter.6
  193.6 13.9 reduce-scatter.8
  211.0 89.2 all-reduce.5
  303.8 56.1 reduce-scatter.10
where the time goes:
time: 370 us; the launch traced here: 368 us
  waiting for transfers between devices  195 us (53%)
  local copies, waits for them, and re-layouts  68.2 us (18%)
  matrix products  44.4 us (12%)
  starting transfers between devices  31.4 us (8%)
  between operations  16.5 us (4%)
  other arithmetic  8.08 us (2%)
  blocking collectives  4.58 us (1%)
    unnamed x6, waiting for transfers between devices  148 us
    reshape x27, local copies, waits for them, and re-layouts, take_window(): return sliced.reshape(padded.shape[0], -1)  39.2 us
    ppermute x7, waiting for transfers between devices, with_halo(): lax.ppermute(lax.slice_in_dim(block, 0, width, axis=dim), axis, backward)  24 us
    ppermute x7, starting transfers between devices, with_halo(): lax.ppermute(lax.slice_in_dim(block, block.shape[dim] - width, None, axis...  22 us
    dot_general x54, matrix products, kernel_gradient(): lax.dot_general(grad_flat, sliced, (((1,), (1,)), ((), ())), preferred_el...  20.2 us
    slice x33, local copies, waits for them, and re-layouts, take_window(): lax.slice(padded, (0, offset[0], offset[1], offset[2]), limits, (1, strid...  19.8 us
    dot_general x81, matrix products, correlate(): jnp.dot(kernel_taps[:, number], sliced, preferred_element_type=jnp.float32)  17.9 us
    reduce_scatter x1, waiting for transfers between devices, per_device(): lax.psum_scatter(down_part.astype(jnp.bfloat16), 'gx', scatter_dimension=...  13.2 us
  transfers between devices with their start and end apart: 18, of which 12 were waited for; matrix products, arithmetic and copies ran while one was open for 2% of the time, Pallas kernels for 0%

commit v1 on v0

v1 whole, which is shorter than its diff:
```python
import math

import jax
import jax.numpy as jnp
from jax import lax
from jax.experimental import pallas as pl
from jax.experimental.pallas import tpu as pltpu
from jax.sharding import PartitionSpec as P

F32 = jnp.float32
BF16 = jnp.bfloat16
CONTRACT_LANES = (((1,), (1,)), ((), ()))
CONTRACT_PLAIN = (((1,), (0,)), ((), ()))
TAPS_XY = [(kx, ky) for kx in range(3) for ky in range(3)]


def silu(values):
    return values / (1.0 + jnp.exp(-values))


def silu_grad(values):
    sigmoid = 1.0 / (1.0 + jnp.exp(-values))
    return sigmoid * (1.0 + values * (1.0 - sigmoid))


def flat(values):
    return values.reshape(-1, values.shape[-1])


def next_row(values):
    return pltpu.roll(values, values.shape[0] - 1, 0)


def previous_row(values):
    return pltpu.roll(values, 1, 0)


def shift_rows(values, forward):
    rows = flat(values)
    return (next_row(rows) if forward else previous_row(rows)).reshape(values.shape)


def forward_kernel(
    place, feat, wide_weight, wide_table, band_fine, band_down, kernel_bottle, cotangent,
    bottle_out, act_out, grad_out, fine_out, slope_out,
    emb, fine, coarse, grads, pre, fine_mask, coarse_mask, *, dims,
):
    nx, by, bz, c1, c2, outs, grains, limits = dims
    total_y, total_z = limits
    ny_emb, ny_fine, ny_mid, ny_bot, ny_own = by + 11, by + 9, by // 2 + 4, by // 2 + 2, by // 2
    quad = feat.shape[1] // 4
    nq = emb.shape[2]
    coarse_x = nx // 2
    own_x = slope_out.shape[0] // (ny_own * nq)
    lanes = 4 * c1
    half = lanes // 2

    shape = (ny_fine * nq, lanes)
    row = lax.broadcasted_iota(jnp.int32, shape, 0)
    lane = lax.broadcasted_iota(jnp.int32, shape, 1)
    y = place[0] * by - 5 + row // nq
    z = place[1] * bz - 5 + 4 * (row % nq) + lane // c1
    inside = (y >= 0) & (y < total_y) & (z >= 0) & (z < total_z)
    fine_mask[...] = jnp.where(inside, 1.0, 0.0)
    shape = (ny_mid * nq, 2 * c2)
    row = lax.broadcasted_iota(jnp.int32, shape, 0)
    lane = lax.broadcasted_iota(jnp.int32, shape, 1)
    y = place[0] * (by // 2) - 2 + row // nq
    z = place[1] * (bz // 2) - 2 + 2 * (row % nq) + lane // c2
    inside = (y >= 0) & (y < total_y // 2) & (z >= 0) & (z < total_z // 2)
    coarse_mask[...] = jnp.where(inside, 1.0, 0.0)

    emb[0] = jnp.zeros(emb.shape[1:], F32)
    emb[nx + 1] = jnp.zeros(emb.shape[1:], F32)
    fine[0, 0] = jnp.zeros(fine.shape[2:], F32)
    coarse[0] = jnp.zeros(coarse.shape[1:], F32)
    coarse[coarse_x + 1] = jnp.zeros(coarse.shape[1:], F32)
    grads[0] = jnp.zeros(grads.shape[1:], F32)
    grads[coarse_x + 1] = jnp.zeros(grads.shape[1:], F32)

    emb_rows = ny_emb * nq

    def embed(step, carry):
        start = pl.multiple_of(step * 2 * emb_rows, 16)
        values = feat[pl.ds(start, 2 * emb_rows), :]
        wide = values.astype(F32)
        grain = lax.broadcasted_iota(jnp.int32, (1, grains), 1).astype(F32) + 1.0
        picks = [
            jnp.where(wide[:, quad * k + quad - 1 : quad * k + quad] == grain, 1.0, 0.0).astype(BF16)
            for k in range(4)
        ]
        mixture = jnp.dot(values, wide_weight[...], preferred_element_type=F32) + jnp.dot(
            jnp.concatenate(picks, axis=1), wide_table[...], preferred_element_type=F32
        )
        out = silu(mixture).astype(BF16).astype(F32)
        emb[pl.ds(1 + 2 * step, 2), :, :, :lanes] = out.reshape(2, ny_emb, nq, lanes)
        following = next_row(out[:, :half])
        emb[pl.ds(1 + 2 * step, 2), :, :, lanes:] = following.reshape(2, ny_emb, nq, half)
        return carry

    lax.fori_loop(0, nx // 2, embed, 0)

    fine_step = 4

    def fine_conv(step, carry):
        x0 = step * fine_step
        patches = jnp.concatenate(
            [
                flat(emb[pl.ds(x0 + kx, fine_step), ky : ky + ny_fine]).astype(BF16)
                for kx, ky in TAPS_XY
            ],
            axis=1,
        )
        values = lax.dot_general(
            patches, band_fine[...], CONTRACT_LANES, preferred_element_type=F32
        )
        rows = ny_fine * nq
        for i in range(fine_step):
            layer = silu(values[i * rows : (i + 1) * rows]) * fine_mask[...]
            layer = layer.astype(BF16).astype(F32)
            following = next_row(layer[:, :half])
            for j in range(ny_fine):
                target = (x0 // 2 + (1 + i) // 2, (1 + i) % 2, j // 2, j % 2)
                fine[target + (slice(None), slice(0, lanes))] = layer[j * nq : (j + 1) * nq]
                fine[target + (slice(None), slice(lanes, None))] = following[j * nq : (j + 1) * nq]
        return carry

    lax.fori_loop(0, nx // fine_step, fine_conv, 0)

    mid_step = 4

    def down_conv(step, carry):
        x0 = step * mid_step
        taps = [
            flat(
                fine[pl.ds(x0 + kx // 2, mid_step), kx % 2, ky // 2 : ky // 2 + ny_mid, ky % 2]
            ).astype(BF16)
            for kx, ky in TAPS_XY
        ]
        parts = []
        for k in range(2):
            patches = jnp.concatenate(
                [tap[:, 2 * k * c1 : 2 * k * c1 + lanes] for tap in taps], axis=1
            )
            parts.append(
                lax.dot_general(
                    patches, band_down[...], CONTRACT_LANES, preferred_element_type=F32
                )
            )
        values = jnp.concatenate(parts, axis=1)
        pre[pl.ds(x0, mid_step)] = values.reshape(mid_step, ny_mid, nq, 2 * c2)
        inside = coarse_mask[...]
        inside = jnp.concatenate([inside] * mid_step, axis=0)
        act = (silu(values) * inside).astype(BF16).astype(F32)
        where = pl.ds(1 + x0, mid_step)
        whole = (mid_step, ny_mid, nq)
        coarse[where, :, :, :c2] = previous_row(act[:, c2:]).reshape(whole + (c2,))
        coarse[where, :, :, c2 : 3 * c2] = act.reshape(whole + (2 * c2,))
        coarse[where, :, :, 3 * c2 :] = next_row(act[:, :c2]).reshape(whole + (c2,))
        return carry

    lax.fori_loop(0, coarse_x // mid_step, down_conv, 0)

    bot_rows = ny_bot * nq

    def bottle_conv(step, carry):
        x0 = step * mid_step
        taps = [
            flat(coarse[pl.ds(x0 + kx, mid_step), ky : ky + ny_bot]).astype(BF16)
            for kx, ky in TAPS_XY
        ]
        parts = []
        for k in range(2):
            patches = jnp.concatenate([tap[:, k * c2 : (k + 3) * c2] for tap in taps], axis=1)
            parts.append(
                lax.dot_general(
                    patches, kernel_bottle[...], CONTRACT_LANES, preferred_element_type=F32
                )
            )
        values = jnp.concatenate(parts, axis=1)
        start = pl.multiple_of(x0 * bot_rows, 16)
        grad = cotangent[pl.ds(start, mid_step * bot_rows), :].astype(F32) * silu_grad(values)
        grad = grad.astype(BF16).astype(F32)
        where = pl.ds(1 + x0, mid_step)
        whole = (mid_step, ny_bot, nq)
        grads[where, :, :, :outs] = previous_row(grad[:, outs:]).reshape(whole + (outs,))
        grads[where, :, :, outs : 3 * outs] = grad.reshape(whole + (2 * outs,))
        grads[where, :, :, 3 * outs :] = next_row(grad[:, :outs]).reshape(whole + (outs,))
        act = silu(values).reshape(whole + (2 * outs,))[:, 1 : 1 + ny_own]
        start = pl.multiple_of(x0 * ny_own * nq, 16)
        bottle_out[pl.ds(start, mid_step * ny_own * nq), :] = flat(act).astype(BF16)
        return carry

    lax.fori_loop(0, coarse_x // mid_step, bottle_conv, 0)

    stacked = jnp.concatenate(
        [kernel_bottle[:, t * c2 : (t + 1) * c2] for t in range(27)], axis=0
    )
    own_rows = ny_own * nq

    def transpose_conv(step, carry):
        x0 = step * mid_step
        taps = [
            flat(grads[pl.ds(x0 + 2 - kx, mid_step), 2 - ky : 2 - ky + ny_own]).astype(BF16)
            for kx, ky in TAPS_XY
        ]
        parts = []
        for k in range(2):
            patches = jnp.concatenate(
                [
                    tap[:, (k + 2 - kz) * outs : (k + 3 - kz) * outs]
                    for tap in taps
                    for kz in range(3)
                ],
                axis=1,
            )
            parts.append(
                lax.dot_general(patches, stacked, CONTRACT_PLAIN, preferred_element_type=F32)
            )
        values = jnp.concatenate(parts, axis=1)
        start = pl.multiple_of(x0 * own_rows, 16)
        act_out[pl.ds(start, mid_step * own_rows), :] = values.astype(BF16)
        return carry

    lax.fori_loop(0, coarse_x // mid_step, transpose_conv, 0)

    scale = 1.0 / math.sqrt(coarse_x * (total_y // 2) * (total_z // 2))
    own = flat(grads[1 : 1 + coarse_x, 1 : 1 + ny_own, :, outs : 3 * outs])
    place_row = lax.broadcasted_iota(jnp.int32, own.shape, 0) % nq
    own = jnp.where((place_row >= 1) & (place_row <= bz // 4), own, 0.0)
    turned = jnp.transpose(own, (1, 0)).astype(BF16)
    for number, (kx, ky) in enumerate(TAPS_XY):
        rows = flat(coarse[kx : kx + coarse_x, ky + 1 : ky + 1 + ny_own]).astype(BF16)
        product = jnp.dot(turned, rows, preferred_element_type=F32)
        total = product[:outs, : 3 * c2] + product[outs:, c2:]
        total = jnp.transpose(total * scale, (1, 0)).astype(BF16)
        grad_out[number * 3 * c2 : (number + 1) * 3 * c2, :] = total

    first = place[2] * own_x
    fine_out[...] = fine[pl.ds(first, own_x + 1), :, 2 : 3 + ny_own]
    slope = silu_grad(pre[pl.ds(first, own_x), 2 : 2 + ny_own])
    slope_out[...] = flat(slope)


def down_kernel(mine, other, slope, fine, grad_out, *, dims):
    bz, c1, c2, nq, scale = dims
    own_x, ny_own = fine.shape[0] - 1, fine.shape[2] - 1
    grad = jnp.sum(other[...].astype(F32), axis=0) + mine[...].astype(F32)
    grad = (grad * slope[...]).astype(BF16).astype(F32)
    place_row = lax.broadcasted_iota(jnp.int32, grad.shape, 0) % nq
    grad = jnp.where((place_row >= 1) & (place_row <= bz // 4), grad, 0.0)
    turned = jnp.transpose(grad, (1, 0)).astype(BF16)
    for number, (kx, ky) in enumerate(TAPS_XY):
        rows = flat(
            fine[kx // 2 : kx // 2 + own_x, kx % 2, ky // 2 : ky // 2 + ny_own, ky % 2]
        ).astype(BF16)
        product = jnp.dot(turned, rows, preferred_element_type=F32)
        total = product[:c2, : 4 * c1] + product[c2:, 2 * c1 : 6 * c1]
        total = jnp.transpose(total * scale, (1, 0))[: 3 * c1].astype(BF16)
        grad_out[number * 3 * c1 : (number + 1) * 3 * c1, :] = total


def shifted(block, axis, step):
    count = lax.axis_size(axis)
    pairs = [(i, i + step) for i in range(count) if 0 <= i + step < count]
    return lax.ppermute(block, axis, pairs)


def with_halo(block, axis, dim, low, high):
    size = block.shape[dim]
    before = shifted(lax.slice_in_dim(block, size - low, size, axis=dim), axis, 1)
    after = shifted(lax.slice_in_dim(block, 0, high, axis=dim), axis, -1)
    return jnp.concatenate([before, block, after], axis=dim)


def scatter_sum(block, axis, distance):
    count = lax.axis_size(axis)
    index = lax.axis_index(axis)
    rest = block.shape[1:]
    bit = 1
    while bit < count:
        split = block.reshape((-1, 2) + rest)
        mine = (index // bit) % 2
        keep = lax.dynamic_index_in_dim(split, mine, 1, keepdims=False)
        send = lax.dynamic_index_in_dim(split, 1 - mine, 1, keepdims=False)
        got = lax.ppermute(send, axis, [(i, i ^ bit) for i in range(count)])
        block = (keep.astype(F32) + got.astype(F32)).astype(BF16)
        bit *= 2
    return block[0]


def per_device(
    fields, grain_ids, material_table, input_weight, kernel_fine, kernel_down, kernel_bottle,
    cotangent,
):
    comps, bx, by, bz = fields.shape
    grains, c1 = material_table.shape
    c2 = kernel_down.shape[0]
    outs_true = kernel_bottle.shape[0]
    gx, gy, gz = lax.axis_size("gx"), lax.axis_size("gy"), lax.axis_size("gz")
    nx, total_y, total_z = bx * gx, by * gy, bz * gz
    coarse_x = nx // 2
    nq = -(-(bz + 12) // 32) * 8
    outs = -(-outs_true // 128) * 128
    if outs != outs_true:
        kernel_bottle = jnp.pad(kernel_bottle, ((0, outs - outs_true), (0, 0)))
        cotangent = jnp.pad(cotangent, ((0, outs - outs_true), (0, 0), (0, 0), (0, 0)))

    quad = comps + 1
    feat = jnp.concatenate([fields, (grain_ids + 1).astype(BF16)[None]], axis=0)
    feat = jnp.transpose(feat, (1, 2, 3, 0)).reshape(bx, by, bz * quad)
    feat = lax.all_gather(feat, "gx", axis=0, tiled=True)
    feat = with_halo(feat, "gy", 1, 6, 5)
    feat = with_halo(feat, "gz", 2, 6 * quad, 6 * quad)
    feat = feat.reshape(nx, by + 11, (bz + 12) // 4, 4 * quad)
    feat = jnp.pad(feat, ((0, 0), (0, 0), (0, nq - feat.shape[2]), (0, 0)))
    feat = feat.reshape(-1, 4 * quad)

    cot = jnp.transpose(cotangent, (1, 2, 3, 0))
    cot = with_halo(cot, "gy", 1, 1, 1)
    cot = with_halo(cot, "gz", 2, 1, 1)
    cot = jnp.pad(cot, ((0, 0), (0, 0), (1, 2 * nq - bz // 2 - 3), (0, 0)))
    cot = cot.reshape(-1, 2 * outs)

    eye = jnp.eye(4, dtype=BF16)
    tall = jnp.pad(input_weight.T, ((0, 1), (0, 0)))
    wide_weight = jnp.kron(eye, tall)
    wide_table = jnp.kron(eye, material_table)
    split = kernel_fine.reshape(c1, 9, 3 * c1)
    band_fine = jnp.concatenate(
        [jnp.pad(split, ((0, 0), (0, 0), (k * c1, (3 - k) * c1))) for k in range(4)], axis=0
    ).reshape(4 * c1, 9 * 6 * c1)
    band_down = jnp.pad(kernel_down.reshape(c2, 9, 3 * c1), ((0, 0), (0, 0), (0, c1)))
    band_down = band_down.reshape(c2, 9 * 4 * c1)
    place = jnp.stack([lax.axis_index("gy"), lax.axis_index("gz"), lax.axis_index("gx")])

    ny_own, ny_mid, ny_bot = by // 2, by // 2 + 4, by // 2 + 2
    own_x = bx // 2
    lanes = 6 * c1
    vmem = pl.BlockSpec(memory_space=pltpu.VMEM)
    bottle_rows, act, bottle_part, fine_own, slope = pl.pallas_call(
        lambda *refs: forward_kernel(
            *refs, dims=(nx, by, bz, c1, c2, outs, grains, (total_y, total_z))
        ),
        out_shape=(
            jax.ShapeDtypeStruct((coarse_x * ny_own * nq, 2 * outs), BF16),
            jax.ShapeDtypeStruct((coarse_x * ny_own * nq, 2 * c2), BF16),
            jax.ShapeDtypeStruct((27 * c2, outs), BF16),
            jax.ShapeDtypeStruct((own_x + 1, 2, ny_own + 1, 2, nq, lanes), F32),
            jax.ShapeDtypeStruct((own_x * ny_own * nq, 2 * c2), F32),
        ),
        in_specs=[pl.BlockSpec(memory_space=pltpu.SMEM)] + [vmem] * 7,
        out_specs=(vmem,) * 5,
        scratch_shapes=[
            pltpu.VMEM((nx + 2, by + 11, nq, lanes), F32),
            pltpu.VMEM((coarse_x + 1, 2, (by + 10) // 2, 2, nq, lanes), F32),
            pltpu.VMEM((coarse_x + 2, ny_mid, nq, 4 * c2), F32),
            pltpu.VMEM((coarse_x + 2, ny_bot, nq, 4 * outs), F32),
            pltpu.VMEM((coarse_x, ny_mid, nq, 2 * c2), F32),
            pltpu.VMEM(((by + 9) * nq, 4 * c1), F32),
            pltpu.VMEM((ny_mid * nq, 2 * c2), F32),
        ],
        compiler_params=pltpu.CompilerParams(vmem_limit_bytes=60 * 1024 * 1024),
        name="forward",
    )(place, feat, wide_weight, wide_table, band_fine, band_down, kernel_bottle, cot)

    bottle = bottle_rows.reshape(coarse_x, ny_own, 2 * nq, outs)[:, :, 2 : 2 + bz // 2]
    bottle = jnp.transpose(bottle, (3, 0, 1, 2))[:outs_true]

    act = act.reshape(gx, own_x * ny_own * nq, 2 * c2)
    index = lax.axis_index("gx")
    mine = lax.dynamic_index_in_dim(act, index, 0, keepdims=False)
    if gx == 2:
        other = lax.dynamic_index_in_dim(act, 1 - index, 0, keepdims=True)
        other = lax.ppermute(other, "gx", [(0, 1), (1, 0)])
    else:
        spread = lax.all_to_all(act, "gx", 0, 0, tiled=True)
        others = [(index + k) % gx for k in range(1, gx)]
        other = jnp.concatenate([lax.dynamic_slice_in_dim(spread, k, 1, 0) for k in others], axis=0)

    scale = 1.0 / math.sqrt(coarse_x * (total_y // 2) * (total_z // 2))
    down_part = pl.pallas_call(
        lambda *refs: down_kernel(*refs, dims=(bz, c1, c2, nq, scale)),
        out_shape=jax.ShapeDtypeStruct((27 * c1, c2), BF16),
        in_specs=[vmem] * 4,
        out_specs=vmem,
        name="down_gradient",
    )(mine, other, slope, fine_own)

    def reduce_chunks(part):
        rows, width = part.shape
        part = part.reshape(gy, gz, rows // (gy * gz), width)
        part = jnp.transpose(part, (1, 0, 2, 3))
        part = scatter_sum(part, "gz", 1)
        return scatter_sum(part, "gy", 1)

    grad_bottle = reduce_chunks(bottle_part)[:, :outs_true].astype(F32).T
    down_part = down_part.reshape(27 * c1, gx, c2 // gx)
    down_part = scatter_sum(jnp.transpose(down_part, (1, 0, 2)), "gx", 1)
    grad_down = reduce_chunks(down_part).astype(F32).T
    return (bottle, grad_down, grad_bottle)


def solution(mesh):
    placed = (
        P(None, "gx", "gy", "gz"),
        P("gx", "gy", "gz"),
        P(),
        P(),
        P(),
        P(),
        P("gx", None),
        P("gx", None, "gy", "gz"),
    )
    return jax.shard_map(
        per_device,
        mesh=mesh,
        in_specs=placed,
        out_specs=(P("gx", None, "gy", "gz"), P("gx", ("gy", "gz")), P("gx", ("gy", "gz"))),
        check_vma=False,
    )
```

time: 370 us -> 118 us (0.32)
  waiting for transfers between devices: 195 us -> 21.7 us
  matrix products: 44.4 us -> 0 us
  local copies, waits for them, and re-layouts: 68.2 us -> 24.2 us
  Pallas kernels: 0 us -> 20.5 us
  between operations: 16.5 us -> 0.96 us
    unnamed x6 -> x0, waiting for transfers between devices: 148 us -> none
    dot_general x164 -> x0, matrix products: 44.4 us -> none  [the longest x54 20.2 us: kernel_gradient(): lax.dot_general(grad_flat, sliced, (((1,), (1,)), ((), ())), preferred_el...]
    reshape x30 -> x8, local copies, waits for them, and re-layouts: 40.9 us -> 8.53 us  [the longest x1 3.93 us: per_device(): band_fine = jnp.concatenate([jnp.pad(split, ((0, 0), (0, 0), (k * c1, (3...]
    reduce_scatter x2 -> x0, waiting for transfers between devices: 21.5 us -> none  [the longest x1 13.2 us: per_device(): lax.psum_scatter(down_part.astype(jnp.bfloat16), 'gx', scatter_dimension=...]
    pallas_call x0 -> x2, Pallas kernels: none -> 20.5 us  [the longest x1 17.5 us: per_device(): pl.pallas_call(lambda *refs: forward_kernel(*refs, dims=(nx, by, bz, c1,...]
    slice x39 -> x3, local copies, waits for them, and re-layouts: 22 us -> 2.07 us  [with_halo(): lax.slice_in_dim(block, size - low, size, axis=dim)]
    convert_element_type x8, other arithmetic: 6.05 us -> 0.37 us  [the longest x7 0.37 us: scatter_sum(): block = (keep.astype(F32) + got.astype(F32)).astype(BF16)]
    ppermute x14 -> x18, starting transfers between devices: 31.2 us -> 34.9 us  [the longest x8 22.3 us: shifted(): return lax.ppermute(block, axis, pairs)]
  transfers between devices with their start and end apart: 18 -> 18, of which waited for: 12 -> 9; matrix products, arithmetic and copies ran while one was open for 2% -> 22% of each run, Pallas kernels for 0% -> 0%
where the time goes in v1:
time: 118 us; the launch traced here: 117 us
  starting transfers between devices  34.9 us (30%)
  local copies, waits for them, and re-layouts  24.2 us (21%)
  waiting for transfers between devices  21.7 us (18%)
  Pallas kernels  20.5 us (17%)
  other arithmetic  9.25 us (8%)
  blocking collectives  5.33 us (5%)
    ppermute x8, starting transfers between devices, shifted(): return lax.ppermute(block, axis, pairs)  22.3 us
    ppermute x9, waiting for transfers between devices, scatter_sum(): got = lax.ppermute(send, axis, [(i, i ^ bit) for i in range(count)])  18.9 us
    pallas_call x1, Pallas kernels, per_device(): pl.pallas_call(lambda *refs: forward_kernel(*refs, dims=(nx, by, bz, c1,...  17.5 us
    ppermute x9, starting transfers between devices, scatter_sum(): got = lax.ppermute(send, axis, [(i, i ^ bit) for i in range(count)])  11.1 us
    all_gather x1, blocking collectives, per_device(): feat = lax.all_gather(feat, 'gx', axis=0, tiled=True)  5.33 us
    reshape x1, local copies, waits for them, and re-layouts, per_device(): band_fine = jnp.concatenate([jnp.pad(split, ((0, 0), (0, 0), (k * c1, (3...  3.93 us
    concatenate x1, local copies, waits for them, and re-layouts, per_device(): jnp.concatenate([jnp.pad(split, ((0, 0), (0, 0), (k * c1, (3 - k) * c1)))...  3.05 us
    pallas_call x1, Pallas kernels, per_device(): pl.pallas_call(lambda *refs: down_kernel(*refs, dims=(bz, c1, c2, nq, sca...  2.97 us
  transfers between devices with their start and end apart: 18, of which 9 were waited for; matrix products, arithmetic and copies ran while one was open for 22% of the time, Pallas kernels for 0%

profile of v1, /device:TPU:0, one launch (start us, length us, event | category | flops | bytes accessed | tf_op | source)
XLA Modules:
  0.0 116.8 jit_solution(9486071897402207422)
XLA Ops:
  0.6 0.8 fusion.21
  1.4 0.9 maximum_bitcast_fusion
  2.3 0.2 copy.36
  2.6 0.2 reshape.128
  2.8 5.3 %all_gather.3 = bf16[16,8,128]{2,1,0:T(8,128)(2,1)S(1)} all-gather(bf16[8,8,128]{2,1,0:T(8,128)(2,1)S(1)} %reshape.128), channel_id=1, replica_groups=mesh['gx'=2,'gy'=4,'gz'=4] {'gx'}, dimensions={0}, use_global_device_ids=true | all-gather | bytes 49152 | tf_op jit(solution)/shard_map/all_gather | solution.py:312
  8.1 1.3 %collective-permute-start.1 = (bf16[16,5,128]{2,1,0:T(8,128)(2,1)S(1)}, bf16[16,5,128]{2,1,0:T(8,128)(2,1)S(1)}, u32[]{:S(2)}, u32[]{:S(2)}) collective-permute-start(bf16[16,5,128]{2,1,0:T(8,128)(2,1)S(1)} %bitcast.97), channel_id=1, source_target_pairs={{4,0},{8,4},{12,8},{5,1},{9,5},{13,9},{6,2},{10,6},{14,10},{7,3},{... | collective-permute-start | bytes 61448 | tf_op jit(solution)/shard_map/ppermute | solution.py:266
  9.4 0.6 slice.36
  10.1 4.6 %collective-permute-start = (bf16[16,6,128]{2,1,0:T(8,128)(2,1)}, bf16[16,6,128]{2,1,0:T(8,128)(2,1)S(1)}, u32[]{:S(2)}, u32[]{:S(2)}) collective-permute-start(bf16[16,6,128]{2,1,0:T(8,128)(2,1)} %slice.36), channel_id=1, source_target_pairs={{0,4},{4,8},{8,12},{1,5},{5,9},{9,13},{2,6},{6,10},{10,14},{3,7},{... | collective-permute-start | bytes 73736 | tf_op jit(solution)/shard_map/ppermute | solution.py:266
  14.7 1.3 %fusion.25 = (bf16[8,1,8,128]{3,2,1,0:T(8,128)(2,1)}, bf16[8,1,8,128]{3,2,1,0:T(8,128)(2,1)}) fusion(bf16[8,4,8,128]{3,2,1,0:T(8,128)(2,1)} %bitcast.99), kind=kLoop, calls=%fused_computation.73 | loop fusion | bytes 65536 | tf_op jit(solution)/shard_map/slice | solution.py:271
  16.1 1.3 %collective-permute-start.5 = (bf16[8,1,8,128]{3,2,1,0:T(8,128)(2,1)}, bf16[8,1,8,128]{3,2,1,0:T(8,128)(2,1)S(1)}, u32[]{:S(2)}, u32[]{:S(2)}) collective-permute-start(bf16[8,1,8,128]{3,2,1,0:T(8,128)(2,1)} %get-tuple-element.22), channel_id=1, source_target_pairs={{4,0},{8,4},{12,8},{5,1},{9,5},{13,9},{6,2},{10,6},{14,10},{7,3},{... | collective-permute-start | bytes 49160 | tf_op jit(solution)/shard_map/ppermute | solution.py:266
  17.4 5.1 %collective-permute-start.4 = (bf16[8,1,8,128]{3,2,1,0:T(8,128)(2,1)}, bf16[8,1,8,128]{3,2,1,0:T(8,128)(2,1)}, u32[]{:S(2)}, u32[]{:S(2)}) collective-permute-start(bf16[8,1,8,128]{3,2,1,0:T(8,128)(2,1)} %get-tuple-element.21), channel_id=1, source_target_pairs={{0,4},{4,8},{8,12},{1,5},{5,9},{9,13},{2,6},{6,10},{10,14},{3,7},{... | collective-permute-start | bytes 49160 | tf_op jit(solution)/shard_map/ppermute | solution.py:266
  22.5 0.7 copy.39
  23.2 0.9 broadcast_multiply_fusion
  24.1 2.1 %reshape.131 = bf16[64,9,192]{2,1,0:T(8,128)(2,1)} reshape(bf16[64,1728]{1,0:T(8,128)(2,1)} %param.12) | data formatting | bytes 442368 | tf_op jit(solution)/shard_map/reshape | solution.py:329
  26.2 2.3 %fusion.7 = bf16[256,9,384]{2,1,0:T(8,128)(2,1)S(1)} fusion(bf16[64,9,192]{2,1,0:T(8,128)(2,1)} %reshape.131), kind=kLoop, calls=%fused_computation.13 | loop fusion | flops 17694720 | bytes 1990656 | tf_op jit(solution)/shard_map/concatenate | solution.py:330
  28.5 0.1 broadcast_multiply_fusion.1
  28.6 0.7 pad_add_fusion.refs_0_
  29.2 0.7 mul.51.refs_2_
  29.9 0.7 copy.57
  30.7 1.8 %copy.41.refs_3_ = bf16[512,256]{1,0:T(8,128)(2,1)} copy(bf16[512,256]{0,1:T(8,128)(2,1)} %bitcast.93) | data formatting | bytes 524288 | tf_op jit(solution)/shard_map/jit(kron)/mul | solution.py:328
  32.5 3.1 %copy.40 = bf16[256,9,384]{0,2,1:T(8,128)(2,1)} copy(bf16[256,9,384]{2,1,0:T(8,128)(2,1)S(1)} %fusion.7) | data formatting | bytes 3538944 | tf_op jit(solution)/shard_map/concatenate | solution.py:330
  35.5 3.9 %copy.42.refs_4_ = bf16[256,3456]{1,0:T(8,128)(2,1)} copy(bf16[256,3456]{0,1:T(8,128)(2,1)} %bitcast.84) | data formatting | bytes 3538944 | tf_op jit(solution)/shard_map/reshape | solution.py:332
  39.5 1.1 copy.43.refs_5_
  40.6 0.8 pad_maximum_fusion.4
  41.4 1.3 %collective-permute-start.7 = (bf16[8,6,1,128]{3,2,1,0:T(2,128)(2,1)S(1)}, bf16[8,6,1,128]{3,2,1,0:T(2,128)(2,1)S(1)}, u32[]{:S(2)}, u32[]{:S(2)}) collective-permute-start(bf16[8,6,1,128]{3,2,1,0:T(2,128)(2,1)S(1)} %get-tuple-element.18), channel_id=1, source_target_pairs={{1,0},{2,1},{3,2},{5,4},{6,5},{7,6},{9,8},{10,9},{11,10},{13,12},{... | collective-permute-start | bytes 36872 | tf_op jit(solution)/shard_map/ppermute | solution.py:266
  42.7 3.0 %collective-permute-start.6 = (bf16[8,6,1,128]{3,2,1,0:T(2,128)(2,1)S(1)}, bf16[8,6,1,128]{3,2,1,0:T(2,128)(2,1)S(1)}, u32[]{:S(2)}, u32[]{:S(2)}) collective-permute-start(bf16[8,6,1,128]{3,2,1,0:T(2,128)(2,1)S(1)} %get-tuple-element.17), channel_id=1, source_target_pairs={{0,1},{1,2},{2,3},{4,5},{5,6},{6,7},{8,9},{9,10},{10,11},{12,13},{... | collective-permute-start | bytes 36872 | tf_op jit(solution)/shard_map/ppermute | solution.py:266
  45.9 0.1 fusion.24
  46.0 1.3 %collective-permute-start.3 = (bf16[16,19,48]{2,1,0:T(8,128)(2,1)S(1)}, bf16[16,19,48]{2,1,0:T(8,128)(2,1)S(1)}, u32[]{:S(2)}, u32[]{:S(2)}) collective-permute-start(bf16[16,19,48]{2,1,0:T(8,128)(2,1)S(1)} %get-tuple-element.20), channel_id=1, source_target_pairs={{1,0},{2,1},{3,2},{5,4},{6,5},{7,6},{9,8},{10,9},{11,10},{13,12},{... | collective-permute-start | bytes 87560 | tf_op jit(solution)/shard_map/ppermute | solution.py:266
  47.3 4.3 %collective-permute-start.2 = (bf16[16,19,48]{2,1,0:T(8,128)(2,1)S(1)}, bf16[16,19,48]{2,1,0:T(8,128)(2,1)S(1)}, u32[]{:S(2)}, u32[]{:S(2)}) collective-permute-start(bf16[16,19,48]{2,1,0:T(8,128)(2,1)S(1)} %get-tuple-element.19), channel_id=1, source_target_pairs={{0,1},{1,2},{2,3},{4,5},{5,6},{6,7},{8,9},{9,10},{10,11},{12,13},{... | collective-permute-start | bytes 87560 | tf_op jit(solution)/shard_map/ppermute | solution.py:266
  51.6 0.9 select_maximum_fusion
  52.5 0.8 reshape.135.refs_7_
  53.3 0.2 pad_maximum_fusion
  53.5 0.3 reshape.149
  53.8 1.0 pad.32.clone
  54.8 17.5 %forward.1 = (bf16[256,256]{1,0:T(8,128)(2,1)}, bf16[256,256]{1,0:T(8,128)(2,1)}, bf16[3456,128]{1,0:T(8,128)(2,1)}, f32[5,2,5,2,8,384]{5,4,3,2,1,0:T(8,128)}, f32[128,256]{1,0:T(8,128)}) custom-call(s32[3]{0:T(128)} %pad_add_fusion.refs_0_, bf16[2432,32]{1,0:T(8,128)(2,1)} %bitcast.87, bf16[32,256]{1,0:T(8,128)(2,1)} %mul.51.refs_2_, ...), custom_call_target="tpu_custom_call" | custom-call | tf_op jit(solution)/shard_map/forward/pallas_call | solution.py:341
  72.3 1.6 %constant_dynamic-slice_fusion.6 = (bf16[1,128,256]{2,1,0:T(8,128)(2,1)S(1)}, bf16[128,256]{1,0:T(8,128)(2,1)}) fusion(bf16[2,128,256]{2,1,0:T(8,128)(2,1)} %bitcast.105, s32[]{:T(128)S(6)} %select_n.101, s32[]{:T(128)S(6)} %select_n.100), kind=kLoop, calls=%fused_computation.68 | loop fusion | bytes 262152 | tf_op jit(solution)/shard_map/jit(dynamic_index_in_dim)/dynamic_slice | solution.py:374
  73.9 1.5 %collective-permute-start.8 = (bf16[1,128,256]{2,1,0:T(8,128)(2,1)S(1)}, bf16[1,128,256]{2,1,0:T(8,128)(2,1)S(1)}, u32[]{:S(2)}, u32[]{:S(2)}) collective-permute-start(bf16[1,128,256]{2,1,0:T(8,128)(2,1)S(1)} %get-tuple-element.15), channel_id=1, source_target_pairs={{0,16},{16,0},{1,17},{17,1},{2,18},{18,2},{3,19},{19,3},{4,20},{20... | collective-permute-start | bytes 196616 | tf_op jit(solution)/shard_map/ppermute | solution.py:375
  75.4 2.8 %collective-permute-done.8.refs_1_ = bf16[1,128,256]{2,1,0:T(8,128)(2,1)S(1)} collective-permute-done((bf16[1,128,256]{2,1,0:T(8,128)(2,1)S(1)}, bf16[1,128,256]{2,1,0:T(8,128)(2,1)S(1)}, u32[]{:S(2)}, u32[]{:S(2)}) %collective-permute-start.8) | collective-permute-done | bytes 65568 | tf_op jit(solution)/shard_map/ppermute | solution.py:375
  78.2 0.6 copy-done.4
  78.8 3.0 %down_gradient.1 = bf16[1728,128]{1,0:T(8,128)(2,1)} custom-call(bf16[128,256]{1,0:T(8,128)(2,1)} %get-tuple-element.16.refs_0_, bf16[1,128,256]{2,1,0:T(8,128)(2,1)} %copy-done.4, f32[128,256]{1,0:T(8,128)} %get-tuple-element.10.refs_2_, f32[5,2,5,2,8,384]{5,4,3,2,1,0:T(8,128)} %get-tuple-element.11.refs_3_), custom_call_target="tpu_custom_call" | custom-call | tf_op jit(solution)/shard_map/down_gradient/pallas_call | solution.py:382
  81.8 1.2 %copy.44 = bf16[1728,128]{0,1:T(8,128)(2,1)S(1)} copy(bf16[1728,128]{1,0:T(8,128)(2,1)} %down_gradient.1) | data formatting | bytes 884736 | tf_op jit(solution)/shard_map/down_gradient/pallas_call | solution.py:382
  83.0 1.6 %collective-permute-start.9 = (bf16[1,1728,64]{1,2,0:T(8,128)(2,1)S(1)}, bf16[1,1728,64]{1,2,0:T(8,128)(2,1)S(1)}, u32[]{:S(2)}, u32[]{:S(2)}) collective-permute-start(bf16[1,1728,64]{1,2,0:T(8,128)(2,1)S(1)} %dynamic-slice_bitcast_fusion.1), channel_id=1, source_target_pairs={{0,16},{16,0},{1,17},{17,1},{2,18},{18,2},{3,19},{19,3},{4,20},{20... | collective-permute-start | bytes 663560 | tf_op jit(solution)/shard_map/ppermute | solution.py:286
  84.8 0.4 collective-permute-start.14
  85.1 6.1 %collective-permute-done.9 = bf16[1,1728,64]{1,2,0:T(8,128)(2,1)S(1)} collective-permute-done((bf16[1,1728,64]{1,2,0:T(8,128)(2,1)S(1)}, bf16[1,1728,64]{1,2,0:T(8,128)(2,1)S(1)}, u32[]{:S(2)}, u32[]{:S(2)}) %collective-permute-start.9) | collective-permute-done | bytes 221216 | tf_op jit(solution)/shard_map/ppermute | solution.py:286
  91.2 0.5 reshape_squeeze.9
  91.8 0.5 constant_dynamic-slice_fusion.5
  92.4 0.1 collective-permute-start.10
  92.5 0.7 slice_bitcast_fusion
  93.1 0.7 collective-permute-done.10
  93.9 1.8 %collective-permute-start.11 = (bf16[1,4,108,64]{2,3,1,0:T(8,128)(2,1)S(1)}, bf16[1,4,108,64]{2,3,1,0:T(8,128)(2,1)S(1)}, u32[]{:S(2)}, u32[]{:S(2)}) collective-permute-start(bf16[1,4,108,64]{2,3,1,0:T(8,128)(2,1)S(1)} %constant_dynamic-slice_fusion.3), channel_id=1, source_target_pairs={{0,2},{1,3},{2,0},{3,1},{4,6},{5,7},{6,4},{7,5},{8,10},{9,11},{10,... | collective-permute-start | bytes 165896 | tf_op jit(solution)/shard_map/ppermute | solution.py:286
  95.7 0.1 fusion.9
  95.8 2.5 %collective-permute-done.11 = bf16[1,4,108,64]{2,3,1,0:T(8,128)(2,1)S(1)} collective-permute-done((bf16[1,4,108,64]{2,3,1,0:T(8,128)(2,1)S(1)}, bf16[1,4,108,64]{2,3,1,0:T(8,128)(2,1)S(1)}, u32[]{:S(2)}, u32[]{:S(2)}) %collective-permute-start.11) | collective-permute-done | bytes 55328 | tf_op jit(solution)/shard_map/ppermute | solution.py:286
  98.3 1.1 collective-permute-start.12
  99.4 1.8 %collective-permute-start.15 = (bf16[1,4,216,128]{3,2,1,0:T(8,128)(2,1)S(1)}, bf16[1,4,216,128]{3,2,1,0:T(8,128)(2,1)S(1)}, u32[]{:S(2)}, u32[]{:S(2)}) collective-permute-start(bf16[1,4,216,128]{3,2,1,0:T(8,128)(2,1)S(1)} %constant_dynamic-slice_fusion.1), channel_id=1, source_target_pairs={{0,2},{1,3},{2,0},{3,1},{4,6},{5,7},{6,4},{7,5},{8,10},{9,11},{10,... | collective-permute-start | bytes 663560 | tf_op jit(solution)/shard_map/ppermute | solution.py:286
  101.1 1.1 collective-permute-done.12
  102.3 3.2 %collective-permute-done.15 = bf16[1,4,216,128]{3,2,1,0:T(8,128)(2,1)S(1)} collective-permute-done((bf16[1,4,216,128]{3,2,1,0:T(8,128)(2,1)S(1)}, bf16[1,4,216,128]{3,2,1,0:T(8,128)(2,1)S(1)}, u32[]{:S(2)}, u32[]{:S(2)}) %collective-permute-start.15) | collective-permute-done | bytes 221216 | tf_op jit(solution)/shard_map/ppermute | solution.py:286
  105.6 1.1 collective-permute-start.16
  106.7 2.0 %collective-permute-start.13 = (bf16[1,108,64]{1,2,0:T(8,128)(2,1)S(1)}, bf16[1,108,64]{1,2,0:T(8,128)(2,1)S(1)}, u32[]{:S(2)}, u32[]{:S(2)}) collective-permute-start(bf16[1,108,64]{1,2,0:T(8,128)(2,1)S(1)} %constant_dynamic-slice_fusion.2), channel_id=1, source_target_pairs={{0,8},{4,12},{8,0},{12,4},{1,9},{5,13},{9,1},{13,5},{2,10},{6,14},... | collective-permute-start | bytes 41480 | tf_op jit(solution)/shard_map/ppermute | solution.py:286
  108.7 1.7 %collective-permute-done.16 = bf16[2,216,128]{2,1,0:T(8,128)(2,1)S(1)} collective-permute-done((bf16[2,216,128]{2,1,0:T(8,128)(2,1)S(1)}, bf16[2,216,128]{2,1,0:T(8,128)(2,1)S(1)}, u32[]{:S(2)}, u32[]{:S(2)}) %collective-permute-start.16) | collective-permute-done | bytes 110624 | tf_op jit(solution)/shard_map/ppermute | solution.py:286
  110.5 1.4 %collective-permute-start.17 = (bf16[1,216,128]{2,1,0:T(8,128)(2,1)S(1)}, bf16[1,216,128]{2,1,0:T(8,128)(2,1)S(1)}, u32[]{:S(2)}, u32[]{:S(2)}) collective-permute-start(bf16[1,216,128]{2,1,0:T(8,128)(2,1)S(1)} %constant_dynamic-slice_fusion), channel_id=1, source_target_pairs={{0,8},{4,12},{8,0},{12,4},{1,9},{5,13},{9,1},{13,5},{2,10},{6,14},... | collective-permute-start | bytes 165896 | tf_op jit(solution)/shard_map/ppermute | solution.py:286
  111.9 0.4 collective-permute-done.13
  112.3 0.6 convert_bitcast_fusion.1
  112.9 3.3 %collective-permute-done.17 = bf16[1,216,128]{2,1,0:T(8,128)(2,1)S(1)} collective-permute-done((bf16[1,216,128]{2,1,0:T(8,128)(2,1)S(1)}, bf16[1,216,128]{2,1,0:T(8,128)(2,1)S(1)}, u32[]{:S(2)}, u32[]{:S(2)}) %collective-permute-start.17) | collective-permute-done | bytes 55328 | tf_op jit(solution)/shard_map/ppermute | solution.py:286
  116.2 0.7 convert_bitcast_fusion
  (43 shorter events, 0.7 us)
Async XLA Ops:
  0.6 27.8 %copy-start.6 = (bf16[64,7]{0,1:T(8,128)(2,1)S(1)}, bf16[64,7]{0,1:T(8,128)(2,1)}, u32[]{:S(2)}) copy-start(bf16[64,7]{0,1:T(8,128)(2,1)} %param.11) | copy-start | bytes 2692
  8.1 37.6 %collective-permute-start.1 = (bf16[16,5,128]{2,1,0:T(8,128)(2,1)S(1)}, bf16[16,5,128]{2,1,0:T(8,128)(2,1)S(1)}, u32[]{:S(2)}, u32[]{:S(2)}) collective-permute-start(bf16[16,5,128]{2,1,0:T(8,128)(2,1)S(1)} %bitcast.97), channel_id=1, source_target_pairs={{4,0},{8,4},{12,8},{5,1},{9,5},{13,9},{6,2},{10,6},{14,10},{7,3},{... | collective-permute-start | bytes 61448 | tf_op jit(solution)/shard_map/ppermute | solution.py:266
  10.1 35.7 %collective-permute-start = (bf16[16,6,128]{2,1,0:T(8,128)(2,1)}, bf16[16,6,128]{2,1,0:T(8,128)(2,1)S(1)}, u32[]{:S(2)}, u32[]{:S(2)}) collective-permute-start(bf16[16,6,128]{2,1,0:T(8,128)(2,1)} %slice.36), channel_id=1, source_target_pairs={{0,4},{4,8},{8,12},{1,5},{5,9},{9,13},{2,6},{6,10},{10,14},{3,7},{... | collective-permute-start | bytes 73736 | tf_op jit(solution)/shard_map/ppermute | solution.py:266
  16.1 24.5 %collective-permute-start.5 = (bf16[8,1,8,128]{3,2,1,0:T(8,128)(2,1)}, bf16[8,1,8,128]{3,2,1,0:T(8,128)(2,1)S(1)}, u32[]{:S(2)}, u32[]{:S(2)}) collective-permute-start(bf16[8,1,8,128]{3,2,1,0:T(8,128)(2,1)} %get-tuple-element.22), channel_id=1, source_target_pairs={{4,0},{8,4},{12,8},{5,1},{9,5},{13,9},{6,2},{10,6},{14,10},{7,3},{... | collective-permute-start | bytes 49160 | tf_op jit(solution)/shard_map/ppermute | solution.py:266
  17.4 23.2 %collective-permute-start.4 = (bf16[8,1,8,128]{3,2,1,0:T(8,128)(2,1)}, bf16[8,1,8,128]{3,2,1,0:T(8,128)(2,1)}, u32[]{:S(2)}, u32[]{:S(2)}) collective-permute-start(bf16[8,1,8,128]{3,2,1,0:T(8,128)(2,1)} %get-tuple-element.21), channel_id=1, source_target_pairs={{0,4},{4,8},{8,12},{1,5},{5,9},{9,13},{2,6},{6,10},{10,14},{3,7},{... | collective-permute-start | bytes 49160 | tf_op jit(solution)/shard_map/ppermute | solution.py:266
  26.2 2.3 %copy-start.5 = (bf16[4,4]{1,0:T(4,128)(2,1)S(1)}, bf16[4,4]{1,0:T(4,128)(2,1)}, u32[]{:S(2)}) copy-start(bf16[4,4]{1,0:T(4,128)(2,1)} %copy.39) | copy-start | bytes 100
  35.5 3.9 %copy-start.1 = (bf16[128,1728]{0,1:T(8,128)(2,1)S(1)}, bf16[128,1728]{0,1:T(8,128)(2,1)}, u32[]{:S(2)}) copy-start(bf16[128,1728]{0,1:T(8,128)(2,1)} %param.13) | copy-start | bytes 1327108
  35.5 5.1 %copy-start.2 = (bf16[128,8,4,8]{0,3,2,1:T(8,128)(2,1)S(1)}, bf16[128,8,4,8]{0,3,2,1:T(8,128)(2,1)}, u32[]{:S(2)}) copy-start(bf16[128,8,4,8]{0,3,2,1:T(8,128)(2,1)} %param.15) | copy-start | bytes 196612
  41.4 10.1 %collective-permute-start.7 = (bf16[8,6,1,128]{3,2,1,0:T(2,128)(2,1)S(1)}, bf16[8,6,1,128]{3,2,1,0:T(2,128)(2,1)S(1)}, u32[]{:S(2)}, u32[]{:S(2)}) collective-permute-start(bf16[8,6,1,128]{3,2,1,0:T(2,128)(2,1)S(1)} %get-tuple-element.18), channel_id=1, source_target_pairs={{1,0},{2,1},{3,2},{5,4},{6,5},{7,6},{9,8},{10,9},{11,10},{13,12},{... | collective-permute-start | bytes 36872 | tf_op jit(solution)/shard_map/ppermute | solution.py:266
  42.7 8.8 %collective-permute-start.6 = (bf16[8,6,1,128]{3,2,1,0:T(2,128)(2,1)S(1)}, bf16[8,6,1,128]{3,2,1,0:T(2,128)(2,1)S(1)}, u32[]{:S(2)}, u32[]{:S(2)}) collective-permute-start(bf16[8,6,1,128]{3,2,1,0:T(2,128)(2,1)S(1)} %get-tuple-element.17), channel_id=1, source_target_pairs={{0,1},{1,2},{2,3},{4,5},{5,6},{6,7},{8,9},{9,10},{10,11},{12,13},{... | collective-permute-start | bytes 36872 | tf_op jit(solution)/shard_map/ppermute | solution.py:266
  46.0 7.3 %collective-permute-start.3 = (bf16[16,19,48]{2,1,0:T(8,128)(2,1)S(1)}, bf16[16,19,48]{2,1,0:T(8,128)(2,1)S(1)}, u32[]{:S(2)}, u32[]{:S(2)}) collective-permute-start(bf16[16,19,48]{2,1,0:T(8,128)(2,1)S(1)} %get-tuple-element.20), channel_id=1, source_target_pairs={{1,0},{2,1},{3,2},{5,4},{6,5},{7,6},{9,8},{10,9},{11,10},{13,12},{... | collective-permute-start | bytes 87560 | tf_op jit(solution)/shard_map/ppermute | solution.py:266
  47.3 6.0 %collective-permute-start.2 = (bf16[16,19,48]{2,1,0:T(8,128)(2,1)S(1)}, bf16[16,19,48]{2,1,0:T(8,128)(2,1)S(1)}, u32[]{:S(2)}, u32[]{:S(2)}) collective-permute-start(bf16[16,19,48]{2,1,0:T(8,128)(2,1)S(1)} %get-tuple-element.19), channel_id=1, source_target_pairs={{0,1},{1,2},{2,3},{4,5},{5,6},{6,7},{8,9},{9,10},{10,11},{12,13},{... | collective-permute-start | bytes 87560 | tf_op jit(solution)/shard_map/ppermute | solution.py:266
  72.3 12.3 %copy-start.3 = (bf16[256,256]{1,0:T(8,128)(2,1)S(1)}, bf16[256,256]{1,0:T(8,128)(2,1)}, u32[]{:S(2)}) copy-start(bf16[256,256]{1,0:T(8,128)(2,1)} %get-tuple-element.8) | copy-start | bytes 393220
  72.3 12.3 %copy-start = (bf16[3456,128]{1,0:T(8,128)(2,1)S(1)}, bf16[3456,128]{1,0:T(8,128)(2,1)}, u32[]{:S(2)}) copy-start(bf16[3456,128]{1,0:T(8,128)(2,1)} %get-tuple-element.12) | copy-start | bytes 2654212
  73.9 4.3 %collective-permute-start.8 = (bf16[1,128,256]{2,1,0:T(8,128)(2,1)S(1)}, bf16[1,128,256]{2,1,0:T(8,128)(2,1)S(1)}, u32[]{:S(2)}, u32[]{:S(2)}) collective-permute-start(bf16[1,128,256]{2,1,0:T(8,128)(2,1)S(1)} %get-tuple-element.15), channel_id=1, source_target_pairs={{0,16},{16,0},{1,17},{17,1},{2,18},{18,2},{3,19},{19,3},{4,20},{20... | collective-permute-start | bytes 196616 | tf_op jit(solution)/shard_map/ppermute | solution.py:375
  78.2 0.6 copy-start.4
  83.0 8.2 %collective-permute-start.9 = (bf16[1,1728,64]{1,2,0:T(8,128)(2,1)S(1)}, bf16[1,1728,64]{1,2,0:T(8,128)(2,1)S(1)}, u32[]{:S(2)}, u32[]{:S(2)}) collective-permute-start(bf16[1,1728,64]{1,2,0:T(8,128)(2,1)S(1)} %dynamic-slice_bitcast_fusion.1), channel_id=1, source_target_pairs={{0,16},{16,0},{1,17},{17,1},{2,18},{18,2},{3,19},{19,3},{4,20},{20... | collective-permute-start | bytes 663560 | tf_op jit(solution)/shard_map/ppermute | solution.py:286
  84.8 10.9 %collective-permute-start.14 = (bf16[2,4,216,128]{3,2,1,0:T(8,128)(2,1)S(1)}, bf16[2,4,216,128]{3,2,1,0:T(8,128)(2,1)S(1)}, u32[]{:S(2)}, u32[]{:S(2)}) collective-permute-start(bf16[2,4,216,128]{3,2,1,0:T(8,128)(2,1)S(1)} %dynamic-slice_bitcast_fusion), channel_id=1, source_target_pairs={{0,1},{1,0},{2,3},{3,2},{4,5},{5,4},{6,7},{7,6},{8,9},{9,8},{10,11... | collective-permute-start | bytes 1327112 | tf_op jit(solution)/shard_map/ppermute | solution.py:286
  92.4 1.4 %collective-permute-start.10 = (bf16[2,4,108,64]{2,3,1,0:T(8,128)(2,1)S(1)}, bf16[2,4,108,64]{2,3,1,0:T(8,128)(2,1)S(1)}, u32[]{:S(2)}, u32[]{:S(2)}) collective-permute-start(bf16[2,4,108,64]{2,3,1,0:T(8,128)(2,1)S(1)} %bitcast.104), channel_id=1, source_target_pairs={{0,1},{1,0},{2,3},{3,2},{4,5},{5,4},{6,7},{7,6},{8,9},{9,8},{10,11... | collective-permute-start | bytes 331784 | tf_op jit(solution)/shard_map/ppermute | solution.py:286
  93.9 4.3 %collective-permute-start.11 = (bf16[1,4,108,64]{2,3,1,0:T(8,128)(2,1)S(1)}, bf16[1,4,108,64]{2,3,1,0:T(8,128)(2,1)S(1)}, u32[]{:S(2)}, u32[]{:S(2)}) collective-permute-start(bf16[1,4,108,64]{2,3,1,0:T(8,128)(2,1)S(1)} %constant_dynamic-slice_fusion.3), channel_id=1, source_target_pairs={{0,2},{1,3},{2,0},{3,1},{4,6},{5,7},{6,4},{7,5},{8,10},{9,11},{10,... | collective-permute-start | bytes 165896 | tf_op jit(solution)/shard_map/ppermute | solution.py:286
  98.3 4.0 %collective-permute-start.12 = (bf16[2,108,64]{1,2,0:T(8,128)(2,1)S(1)}, bf16[2,108,64]{1,2,0:T(8,128)(2,1)S(1)}, u32[]{:S(2)}, u32[]{:S(2)}) collective-permute-start(bf16[2,108,64]{1,2,0:T(8,128)(2,1)S(1)} %dynamic-slice_bitcast_fusion.4), channel_id=1, source_target_pairs={{0,4},{4,0},{8,12},{12,8},{1,5},{5,1},{9,13},{13,9},{2,6},{6,2},{1... | collective-permute-start | bytes 82952 | tf_op jit(solution)/shard_map/ppermute | solution.py:286
  99.4 6.1 %collective-permute-start.15 = (bf16[1,4,216,128]{3,2,1,0:T(8,128)(2,1)S(1)}, bf16[1,4,216,128]{3,2,1,0:T(8,128)(2,1)S(1)}, u32[]{:S(2)}, u32[]{:S(2)}) collective-permute-start(bf16[1,4,216,128]{3,2,1,0:T(8,128)(2,1)S(1)} %constant_dynamic-slice_fusion.1), channel_id=1, source_target_pairs={{0,2},{1,3},{2,0},{3,1},{4,6},{5,7},{6,4},{7,5},{8,10},{9,11},{10,... | collective-permute-start | bytes 663560 | tf_op jit(solution)/shard_map/ppermute | solution.py:286
  105.6 4.8 %collective-permute-start.16 = (bf16[2,216,128]{2,1,0:T(8,128)(2,1)S(1)}, bf16[2,216,128]{2,1,0:T(8,128)(2,1)S(1)}, u32[]{:S(2)}, u32[]{:S(2)}) collective-permute-start(bf16[2,216,128]{2,1,0:T(8,128)(2,1)S(1)} %dynamic-slice_bitcast_fusion.2), channel_id=1, source_target_pairs={{0,4},{4,0},{8,12},{12,8},{1,5},{5,1},{9,13},{13,9},{2,6},{6,2},{1... | collective-permute-start | bytes 331784 | tf_op jit(solution)/shard_map/ppermute | solution.py:286
  106.7 5.6 %collective-permute-start.13 = (bf16[1,108,64]{1,2,0:T(8,128)(2,1)S(1)}, bf16[1,108,64]{1,2,0:T(8,128)(2,1)S(1)}, u32[]{:S(2)}, u32[]{:S(2)}) collective-permute-start(bf16[1,108,64]{1,2,0:T(8,128)(2,1)S(1)} %constant_dynamic-slice_fusion.2), channel_id=1, source_target_pairs={{0,8},{4,12},{8,0},{12,4},{1,9},{5,13},{9,1},{13,5},{2,10},{6,14},... | collective-permute-start | bytes 41480 | tf_op jit(solution)/shard_map/ppermute | solution.py:286
  110.5 5.7 %collective-permute-start.17 = (bf16[1,216,128]{2,1,0:T(8,128)(2,1)S(1)}, bf16[1,216,128]{2,1,0:T(8,128)(2,1)S(1)}, u32[]{:S(2)}, u32[]{:S(2)}) collective-permute-start(bf16[1,216,128]{2,1,0:T(8,128)(2,1)S(1)} %constant_dynamic-slice_fusion), channel_id=1, source_target_pairs={{0,8},{4,12},{8,0},{12,4},{1,9},{5,13},{9,1},{13,5},{2,10},{6,14},... | collective-permute-start | bytes 165896 | tf_op jit(solution)/shard_map/ppermute | solution.py:286

commit v2 on v1

--- a/solution.py
+++ b/solution.py
@@ -42,7 +42,7 @@
 
 def forward_kernel(
     place, feat, wide_weight, wide_table, band_fine, band_down, kernel_bottle, cotangent,
-    bottle_out, act_out, grad_out, fine_out, slope_out,
+    bottle_out, mine_out, others_out, grad_out, fine_out, slope_out,
     emb, fine, coarse, grads, pre, fine_mask, coarse_mask, *, dims,
 ):
     nx, by, bz, c1, c2, outs, grains, limits = dims
@@ -52,6 +52,7 @@
     nq = emb.shape[2]
     coarse_x = nx // 2
     own_x = slope_out.shape[0] // (ny_own * nq)
+    groups = coarse_x // own_x
     lanes = 4 * c1
     half = lanes // 2
 
@@ -89,7 +90,9 @@
             jnp.where(wide[:, quad * k + quad - 1 : quad * k + quad] == grain, 1.0, 0.0).astype(BF16)
             for k in range(4)
         ]
-        mixture = jnp.dot(values, wide_weight[...], preferred_element_type=F32) + jnp.dot(
+        mixture = lax.dot_general(
+            values, wide_weight[...], CONTRACT_LANES, preferred_element_type=F32
+        ) + jnp.dot(
             jnp.concatenate(picks, axis=1), wide_table[...], preferred_element_type=F32
         )
         out = silu(mixture).astype(BF16).astype(F32)
@@ -218,8 +221,20 @@
                 lax.dot_general(patches, stacked, CONTRACT_PLAIN, preferred_element_type=F32)
             )
         values = jnp.concatenate(parts, axis=1)
-        start = pl.multiple_of(x0 * own_rows, 16)
-        act_out[pl.ds(start, mid_step * own_rows), :] = values.astype(BF16)
+        values = values.astype(BF16)
+        owner = lax.rem(x0 // own_x - place[2] + groups, groups)
+        inner = lax.rem(x0, own_x)
+
+        @pl.when(owner == 0)
+        def _():
+            start = pl.multiple_of(inner * own_rows, 16)
+            mine_out[pl.ds(start, mid_step * own_rows), :] = values
+
+        @pl.when(owner > 0)
+        def _():
+            start = pl.multiple_of(inner * own_rows, 16)
+            others_out[owner - 1, pl.ds(start, mid_step * own_rows), :] = values
+
         return carry
 
     lax.fori_loop(0, coarse_x // mid_step, transpose_conv, 0)
@@ -242,7 +257,37 @@
     slope_out[...] = flat(slope)
 
 
-def down_kernel(mine, other, slope, fine, grad_out, *, dims):
+def prepare_kernel(
+    input_weight, table, kernel_fine, kernel_down, weight_out, table_out, fine_out, down_out
+):
+    c1, comps = input_weight.shape
+    grains = table.shape[0]
+    c2 = kernel_down.shape[0]
+    quad = comps + 1
+    weight_out[...] = jnp.zeros(weight_out.shape, BF16)
+    table_out[...] = jnp.zeros(table_out.shape, BF16)
+    weight = input_weight[...]
+    for k in range(4):
+        weight_out[k * c1 : (k + 1) * c1, k * quad : k * quad + comps] = weight
+        table_out[k * grains : (k + 1) * grains, k * c1 : (k + 1) * c1] = table[...]
+    width = 3 * c1
+    for tap in range(9):
+        piece = kernel_fine[:, tap * width : (tap + 1) * width].astype(F32)
+        for k in range(4):
+            parts = [piece]
+            if k:
+                parts.insert(0, jnp.zeros((c1, k * c1), F32))
+            if k < 3:
+                parts.append(jnp.zeros((c1, (3 - k) * c1), F32))
+            fine_out[k * c1 : (k + 1) * c1, tap * 2 * width : (tap + 1) * 2 * width] = (
+                jnp.concatenate(parts, axis=1).astype(BF16)
+            )
+        piece = kernel_down[:, tap * width : (tap + 1) * width].astype(F32)
+        piece = jnp.concatenate([piece, jnp.zeros((c2, c1), F32)], axis=1)
+        down_out[:, tap * 4 * c1 : (tap + 1) * 4 * c1] = piece.astype(BF16)
+
+
+def down_kernel(mine, other, slope, fine, grad_out, total_ref, *, dims):
     bz, c1, c2, nq, scale = dims
     own_x, ny_own = fine.shape[0] - 1, fine.shape[2] - 1
     grad = jnp.sum(other[...].astype(F32), axis=0) + mine[...].astype(F32)
@@ -256,35 +301,43 @@
         ).astype(BF16)
         product = jnp.dot(turned, rows, preferred_element_type=F32)
         total = product[:c2, : 4 * c1] + product[c2:, 2 * c1 : 6 * c1]
-        total = jnp.transpose(total * scale, (1, 0))[: 3 * c1].astype(BF16)
-        grad_out[number * 3 * c1 : (number + 1) * 3 * c1, :] = total
-
-
-def shifted(block, axis, step):
-    count = lax.axis_size(axis)
-    pairs = [(i, i + step) for i in range(count) if 0 <= i + step < count]
-    return lax.ppermute(block, axis, pairs)
-
-
-def with_halo(block, axis, dim, low, high):
-    size = block.shape[dim]
-    before = shifted(lax.slice_in_dim(block, size - low, size, axis=dim), axis, 1)
-    after = shifted(lax.slice_in_dim(block, 0, high, axis=dim), axis, -1)
-    return jnp.concatenate([before, block, after], axis=dim)
-
-
-def scatter_sum(block, axis, distance):
+        total = jnp.transpose(total * scale, (1, 0))[: 3 * c1]
+        total_ref[number * 3 * c1 : (number + 1) * 3 * c1, :] = total
+    if len(grad_out.shape) == 2:
+        grad_out[...] = total_ref[...].astype(BF16)
+        return
+    chunks, rows = grad_out.shape[1:3]
+    low = lax.broadcasted_iota(jnp.int32, (rows, c2), 1) < c2 // 2
+    for k in range(chunks):
+        first = total_ref[2 * k * rows : (2 * k + 1) * rows, :]
+        second = total_ref[(2 * k + 1) * rows : (2 * k + 2) * rows, :]
+        grad_out[0, k] = jnp.where(low, first, pltpu.roll(second, c2 // 2, 1)).astype(BF16)
+        grad_out[1, k] = jnp.where(low, pltpu.roll(first, c2 // 2, 1), second).astype(BF16)
+
+
+def ring_halo(forward, backward, axis):
     count = lax.axis_size(axis)
     index = lax.axis_index(axis)
-    rest = block.shape[1:]
-    bit = 1
-    while bit < count:
-        split = block.reshape((-1, 2) + rest)
-        mine = (index // bit) % 2
-        keep = lax.dynamic_index_in_dim(split, mine, 1, keepdims=False)
-        send = lax.dynamic_index_in_dim(split, 1 - mine, 1, keepdims=False)
-        got = lax.ppermute(send, axis, [(i, i ^ bit) for i in range(count)])
-        block = (keep.astype(F32) + got.astype(F32)).astype(BF16)
+    before = lax.ppermute(forward, axis, [(i, (i + 1) % count) for i in range(count)])
+    after = lax.ppermute(backward, axis, [(i, (i - 1) % count) for i in range(count)])
+    zero = jnp.zeros((), before.dtype)
+    return jnp.where(index > 0, before, zero), jnp.where(index < count - 1, after, zero)
+
+
+def halve(block, axes, bit):
+    count = math.prod(lax.axis_size(axis) for axis in axes)
+    index = lax.axis_index(axes)
+    split = block.reshape((-1, 2) + block.shape[1:])
+    mine = (index // bit) % 2
+    keep = lax.dynamic_index_in_dim(split, mine, 1, keepdims=False)
+    send = lax.dynamic_index_in_dim(split, 1 - mine, 1, keepdims=False)
+    got = lax.ppermute(send, axes, [(i, i ^ bit) for i in range(count)])
+    return keep.astype(F32) + got.astype(F32)
+
+
+def halve_all(block, axes, bit=1):
+    while block.shape[0] > 1:
+        block = halve(block.astype(BF16), axes, bit)
         bit *= 2
     return block[0]
 
@@ -307,50 +360,76 @@
         cotangent = jnp.pad(cotangent, ((0, outs - outs_true), (0, 0), (0, 0), (0, 0)))
 
     quad = comps + 1
+    half_y, half_z = by // 2, bz // 2
     feat = jnp.concatenate([fields, (grain_ids + 1).astype(BF16)[None]], axis=0)
     feat = jnp.transpose(feat, (1, 2, 3, 0)).reshape(bx, by, bz * quad)
     feat = lax.all_gather(feat, "gx", axis=0, tiled=True)
-    feat = with_halo(feat, "gy", 1, 6, 5)
-    feat = with_halo(feat, "gz", 2, 6 * quad, 6 * quad)
-    feat = feat.reshape(nx, by + 11, (bz + 12) // 4, 4 * quad)
-    feat = jnp.pad(feat, ((0, 0), (0, 0), (0, nq - feat.shape[2]), (0, 0)))
+    cot = jnp.transpose(cotangent, (1, 2, 3, 0))
+
+    def packed(first, second):
+        return jnp.concatenate([first.reshape(-1, 128), second.reshape(-1, 128)], axis=0)
+
+    def unpacked(both, first_shape, second_shape):
+        cut = math.prod(first_shape) // 128
+        return both[:cut].reshape(first_shape), both[cut:].reshape(second_shape)
+
+    before, after = ring_halo(
+        packed(feat[:, by - 6 :], cot[:, half_y - 1 :]), packed(feat[:, :5], cot[:, :1]), "gy"
+    )
+    edge = (coarse_x, 1, half_z, outs)
+    feat_before, cot_before = unpacked(before, (nx, 6, bz * quad), edge)
+    feat_after, cot_after = unpacked(after, (nx, 5, bz * quad), edge)
+    feat = jnp.concatenate([feat_before, feat, feat_after], axis=1)
+    cot = jnp.concatenate([cot_before, cot, cot_after], axis=1)
+    before, after = ring_halo(packed(feat, cot[:, :, half_z - 1 :]), packed(feat, cot[:, :, :1]), "gz")
+    edge = (coarse_x, half_y + 2, 1, outs)
+    feat_before, cot_before = unpacked(before, feat.shape, edge)
+    feat_after, cot_after = unpacked(after, feat.shape, edge)
+    feat = jnp.concatenate(
+        [feat_before[:, :, (bz - 6) * quad :], feat, feat_after[:, :, : 6 * quad]], axis=2
+    )
+    feat = jnp.pad(feat, ((0, 0), (0, 0), (0, 4 * nq * quad - feat.shape[2])))
     feat = feat.reshape(-1, 4 * quad)
-
-    cot = jnp.transpose(cotangent, (1, 2, 3, 0))
-    cot = with_halo(cot, "gy", 1, 1, 1)
-    cot = with_halo(cot, "gz", 2, 1, 1)
-    cot = jnp.pad(cot, ((0, 0), (0, 0), (1, 2 * nq - bz // 2 - 3), (0, 0)))
+    gap = (coarse_x, half_y + 2, 2 * nq - half_z - 3, outs)
+    cot = jnp.concatenate(
+        [jnp.zeros(edge, BF16), cot_before, cot, cot_after, jnp.zeros(gap, BF16)], axis=2
+    )
     cot = cot.reshape(-1, 2 * outs)
 
-    eye = jnp.eye(4, dtype=BF16)
-    tall = jnp.pad(input_weight.T, ((0, 1), (0, 0)))
-    wide_weight = jnp.kron(eye, tall)
-    wide_table = jnp.kron(eye, material_table)
-    split = kernel_fine.reshape(c1, 9, 3 * c1)
-    band_fine = jnp.concatenate(
-        [jnp.pad(split, ((0, 0), (0, 0), (k * c1, (3 - k) * c1))) for k in range(4)], axis=0
-    ).reshape(4 * c1, 9 * 6 * c1)
-    band_down = jnp.pad(kernel_down.reshape(c2, 9, 3 * c1), ((0, 0), (0, 0), (0, c1)))
-    band_down = band_down.reshape(c2, 9 * 4 * c1)
+    vmem = pl.BlockSpec(memory_space=pltpu.VMEM)
+    wide_weight, wide_table, band_fine, band_down = pl.pallas_call(
+        prepare_kernel,
+        out_shape=(
+            jax.ShapeDtypeStruct((4 * c1, 4 * quad), BF16),
+            jax.ShapeDtypeStruct((4 * grains, 4 * c1), BF16),
+            jax.ShapeDtypeStruct((4 * c1, 9 * 6 * c1), BF16),
+            jax.ShapeDtypeStruct((c2, 9 * 4 * c1), BF16),
+        ),
+        in_specs=[vmem] * 4,
+        out_specs=(vmem,) * 4,
+        cost_estimate=pl.CostEstimate(flops=10**9, transcendentals=0, bytes_accessed=4 * 10**6),
+        name="prepare",
+    )(input_weight, material_table, kernel_fine, kernel_down)
     place = jnp.stack([lax.axis_index("gy"), lax.axis_index("gz"), lax.axis_index("gx")])
 
     ny_own, ny_mid, ny_bot = by // 2, by // 2 + 4, by // 2 + 2
     own_x = bx // 2
     lanes = 6 * c1
-    vmem = pl.BlockSpec(memory_space=pltpu.VMEM)
-    bottle_rows, act, bottle_part, fine_own, slope = pl.pallas_call(
+    own_rows = own_x * ny_own * nq
+    bottle_rows, mine, others, bottle_part, fine_own, slope = pl.pallas_call(
         lambda *refs: forward_kernel(
             *refs, dims=(nx, by, bz, c1, c2, outs, grains, (total_y, total_z))
         ),
         out_shape=(
             jax.ShapeDtypeStruct((coarse_x * ny_own * nq, 2 * outs), BF16),
-            jax.ShapeDtypeStruct((coarse_x * ny_own * nq, 2 * c2), BF16),
+            jax.ShapeDtypeStruct((own_rows, 2 * c2), BF16),
+            jax.ShapeDtypeStruct((gx - 1, own_rows, 2 * c2), BF16),
             jax.ShapeDtypeStruct((27 * c2, outs), BF16),
             jax.ShapeDtypeStruct((own_x + 1, 2, ny_own + 1, 2, nq, lanes), F32),
             jax.ShapeDtypeStruct((own_x * ny_own * nq, 2 * c2), F32),
         ),
         in_specs=[pl.BlockSpec(memory_space=pltpu.SMEM)] + [vmem] * 7,
-        out_specs=(vmem,) * 5,
+        out_specs=(vmem,) * 6,
         scratch_shapes=[
             pltpu.VMEM((nx + 2, by + 11, nq, lanes), F32),
             pltpu.VMEM((coarse_x + 1, 2, (by + 10) // 2, 2, nq, lanes), F32),
@@ -361,43 +440,54 @@
             pltpu.VMEM((ny_mid * nq, 2 * c2), F32),
         ],
         compiler_params=pltpu.CompilerParams(vmem_limit_bytes=60 * 1024 * 1024),
+        cost_estimate=pl.CostEstimate(flops=10**10, transcendentals=0, bytes_accessed=10**7),
         name="forward",
     )(place, feat, wide_weight, wide_table, band_fine, band_down, kernel_bottle, cot)
 
     bottle = bottle_rows.reshape(coarse_x, ny_own, 2 * nq, outs)[:, :, 2 : 2 + bz // 2]
     bottle = jnp.transpose(bottle, (3, 0, 1, 2))[:outs_true]
 
-    act = act.reshape(gx, own_x * ny_own * nq, 2 * c2)
-    index = lax.axis_index("gx")
-    mine = lax.dynamic_index_in_dim(act, index, 0, keepdims=False)
-    if gx == 2:
-        other = lax.dynamic_index_in_dim(act, 1 - index, 0, keepdims=True)
-        other = lax.ppermute(other, "gx", [(0, 1), (1, 0)])
-    else:
-        spread = lax.all_to_all(act, "gx", 0, 0, tiled=True)
-        others = [(index + k) % gx for k in range(1, gx)]
-        other = jnp.concatenate([lax.dynamic_slice_in_dim(spread, k, 1, 0) for k in others], axis=0)
-
+    other = jnp.stack(
+        [
+            lax.ppermute(others[k - 1], "gx", [(i, (i + k) % gx) for i in range(gx)])
+            for k in range(1, gx)
+        ]
+    )
+
+    chunks = gy * gz
+    rows = 27 * c1 // chunks
+    side_by_side = gx == 2 and rows % 2 == 0
+    part_shape = (2, chunks, rows // 2, c2) if side_by_side else (27 * c1, c2)
     scale = 1.0 / math.sqrt(coarse_x * (total_y // 2) * (total_z // 2))
     down_part = pl.pallas_call(
         lambda *refs: down_kernel(*refs, dims=(bz, c1, c2, nq, scale)),
-        out_shape=jax.ShapeDtypeStruct((27 * c1, c2), BF16),
+        out_shape=jax.ShapeDtypeStruct(part_shape, BF16),
         in_specs=[vmem] * 4,
         out_specs=vmem,
+        scratch_shapes=[pltpu.VMEM((27 * c1, c2), F32)],
+        cost_estimate=pl.CostEstimate(flops=2 * 10**9, transcendentals=0, bytes_accessed=10**6),
         name="down_gradient",
     )(mine, other, slope, fine_own)
 
-    def reduce_chunks(part):
-        rows, width = part.shape
-        part = part.reshape(gy, gz, rows // (gy * gz), width)
-        part = jnp.transpose(part, (1, 0, 2, 3))
-        part = scatter_sum(part, "gz", 1)
-        return scatter_sum(part, "gy", 1)
-
-    grad_bottle = reduce_chunks(bottle_part)[:, :outs_true].astype(F32).T
-    down_part = down_part.reshape(27 * c1, gx, c2 // gx)
-    down_part = scatter_sum(jnp.transpose(down_part, (1, 0, 2)), "gx", 1)
-    grad_down = reduce_chunks(down_part).astype(F32).T
+    both = ("gy", "gz")
+    bottle_part = bottle_part.reshape(chunks, 27 * c2 // chunks, outs)
+    if side_by_side:
+        bottle_part = halve(bottle_part, both, 1).astype(BF16)
+        bottle_part = halve(bottle_part, both, 2).astype(BF16)
+        turned = jnp.moveaxis(down_part, 0, 1)
+        turned = halve(turned, both, 1).astype(BF16)
+        down_part = halve(jnp.moveaxis(turned, 1, 0), ("gx",), 1).astype(BF16)[0]
+        down_part = halve(down_part, both, 2).astype(BF16)
+        summed = halve_all(jnp.concatenate([bottle_part, down_part], axis=1), both, 4)
+        cut = bottle_part.shape[1]
+        grad_bottle = summed[:cut, :outs_true].T
+        halves = summed[cut:]
+        grad_down = jnp.concatenate([halves[:, : c2 // 2].T, halves[:, c2 // 2 :].T], axis=1)
+    else:
+        grad_bottle = halve_all(bottle_part, both)[:, :outs_true].T
+        down_part = jnp.transpose(down_part.reshape(27 * c1, gx, c2 // gx), (1, 0, 2))
+        down_part = halve_all(down_part, ("gx",)).reshape(chunks, rows, c2 // gx)
+        grad_down = halve_all(down_part, both).T
     return (bottle, grad_down, grad_bottle)
 
 

time: 118 us -> 83.4 us (0.71)
  starting transfers between devices: 34.9 us -> 14.4 us
  local copies, waits for them, and re-layouts: 24.2 us -> 11 us
  other arithmetic: 9.25 us -> 3.05 us
  Pallas kernels: 20.5 us -> 24.1 us
  waiting for transfers between devices: 21.7 us -> 24.2 us
    ppermute x18 -> x12, starting transfers between devices: 34.9 us -> 14.4 us  [the longest x7 6.69 us: halve(): got = lax.ppermute(send, axes, [(i, i ^ bit) for i in range(count)])]
    reshape x5 -> x15, local copies, waits for them, and re-layouts: 7.48 us -> 2.11 us  [the longest x1 1.13 us: per_device(): feat = feat.reshape(-1, 4 * quad)]
    concatenate x4 -> x8, other arithmetic: 3.45 us -> 0.34 us  [the longest x1 0.21 us: per_device(): jnp.concatenate([feat_before[:, :, (bz - 6) * quad:], feat, feat_after[:,...]
    pallas_call x0 -> x1, Pallas kernels: none -> 2.95 us  [per_device(): pl.pallas_call(prepare_kernel, out_shape=(jax.ShapeDtypeStruct((4 * c1, 4...]
    ppermute x18 -> x12, waiting for transfers between devices: 21.7 us -> 24.2 us  [the longest x7 19.3 us: halve(): got = lax.ppermute(send, axes, [(i, i ^ bit) for i in range(count)])]
    mul x2 -> x0, local copies, waits for them, and re-layouts: 2.5 us -> none  [the longest x1 1.79 us: per_device(): wide_table = jnp.kron(eye, material_table)]
    concatenate x1, local copies, waits for them, and re-layouts: 3.05 us -> 0.61 us  [per_device(): jnp.concatenate([jnp.zeros(edge, BF16), cot_before, cot, cot_after, jnp.z...]
    unnamed x15 -> x18, local copies, waits for them, and re-layouts: 1.39 us -> 3.77 us
  transfers between devices with their start and end apart: 18 -> 12, of which waited for: 9 -> 8; matrix products, arithmetic and copies ran while one was open for 22% -> 5% of each run, Pallas kernels for 0% -> 4%
where the time goes in v2:
time: 83.4 us; the launch traced here: 83.1 us
  waiting for transfers between devices  24.2 us (29%)
  Pallas kernels  24.1 us (29%)
  starting transfers between devices  14.4 us (17%)
  local copies, waits for them, and re-layouts  11 us (13%)
  blocking collectives  5.33 us (6%)
  other arithmetic  3.05 us (4%)
  between operations  1.05 us (1%)
    ppermute x7, waiting for transfers between devices, halve(): got = lax.ppermute(send, axes, [(i, i ^ bit) for i in range(count)])  19.3 us
    pallas_call x1, Pallas kernels, per_device(): pl.pallas_call(lambda *refs: forward_kernel(*refs, dims=(nx, by, bz, c1,...  17.6 us
    ppermute x7, starting transfers between devices, halve(): got = lax.ppermute(send, axes, [(i, i ^ bit) for i in range(count)])  6.69 us
    all_gather x1, blocking collectives, per_device(): feat = lax.all_gather(feat, 'gx', axis=0, tiled=True)  5.33 us
    ppermute x2, starting transfers between devices, ring_halo(): lax.ppermute(backward, axis, [(i, (i - 1) % count) for i in range(count)])  3.82 us
    unnamed x18, local copies, waits for them, and re-layouts  3.77 us
    pallas_call x1, Pallas kernels, per_device(): pl.pallas_call(lambda *refs: down_kernel(*refs, dims=(bz, c1, c2, nq, sca...  3.5 us
    pallas_call x1, Pallas kernels, per_device(): pl.pallas_call(prepare_kernel, out_shape=(jax.ShapeDtypeStruct((4 * c1, 4...  2.95 us
  transfers between devices with their start and end apart: 12, of which 8 were waited for; matrix products, arithmetic and copies ran while one was open for 5% of the time, Pallas kernels for 4%

profile of v2, /device:TPU:0, one launch (start us, length us, event | category | flops | bytes accessed | tf_op | source)
XLA Modules:
  0.0 83.1 jit_solution(18179263909375376769)
XLA Ops:
  0.6 0.0 copy-start.2
  0.6 0.0 copy-start.1
  0.7 0.0 copy-start.4
  0.7 0.0 copy-start.5
  0.7 0.8 fusion.15
  1.5 0.9 %maximum_bitcast_fusion = bf16[8,8,16,8]{2,1,0,3:T(8,128)(2,1)S(1)} fusion(bf16[1,8,8,16]{3,2,1,0:T(8,128)(2,1)S(1)} %fusion.15, bf16[7,8,8,16]{3,2,1,0:T(8,128)(2,1)} %param.8), kind=kLoop, calls=%fused_computation.27 | loop fusion | flops 8192 | bytes 32768 | tf_op jit(solution)/shard_map/transpose | solution.py:365
  2.4 0.2 copy.38
  2.6 0.2 reshape.112
  2.9 5.3 %all_gather.3 = bf16[16,8,128]{2,1,0:T(8,128)(2,1)S(1)} all-gather(bf16[8,8,128]{2,1,0:T(8,128)(2,1)S(1)} %reshape.112), channel_id=1, replica_groups=mesh['gx'=2,'gy'=4,'gz'=4] {'gx'}, dimensions={0}, use_global_device_ids=true | all-gather | bytes 49152 | tf_op jit(solution)/shard_map/all_gather | solution.py:366
  8.3 0.7 slice_bitcast_fusion.8
  9.0 2.2 %collective-permute-start = (bf16[160,128]{1,0:T(8,128)(2,1)S(1)}, bf16[160,128]{1,0:T(8,128)(2,1)S(1)}, u32[]{:S(2)}, u32[]{:S(2)}) collective-permute-start(bf16[160,128]{1,0:T(8,128)(2,1)S(1)} %pad_maximum_fusion.6), channel_id=1, source_target_pairs={{0,4},{4,8},{8,12},{12,0},{1,5},{5,9},{9,13},{13,1},{2,6},{6,10},{... | collective-permute-start | bytes 122888 | tf_op jit(solution)/shard_map/ppermute | solution.py:321
  11.2 2.1 %collective-permute-start.1 = (bf16[144,128]{1,0:T(8,128)(2,1)S(1)}, bf16[144,128]{1,0:T(8,128)(2,1)S(1)}, u32[]{:S(2)}, u32[]{:S(2)}) collective-permute-start(bf16[144,128]{1,0:T(8,128)(2,1)S(1)} %pad_maximum_fusion.7), channel_id=1, source_target_pairs={{0,12},{4,0},{8,4},{12,8},{1,13},{5,1},{9,5},{13,9},{2,14},{6,2},{... | collective-permute-start | bytes 110600 | tf_op jit(solution)/shard_map/ppermute | solution.py:322
  13.3 0.6 pad_add_fusion.refs_0_
  13.9 0.0 copy-done.1
  13.9 1.0 %copy.43.kernel_down = bf16[128,1728]{1,0:T(8,128)(2,1)} copy(bf16[128,1728]{0,1:T(8,128)(2,1)S(1)} %copy-done.1) | data formatting | bytes 884736 | tf_op args[5]
  14.9 0.0 copy-done.4
  14.9 0.7 copy.42.table
  15.6 0.0 copy-done.5
  15.6 0.7 copy.41.input_weight
  16.3 0.0 collective-permute-done.1
  16.4 0.0 collective-permute-done
  16.6 0.0 copy-done.2
  16.6 0.1 slice_reduce_fusion.1
  16.8 0.1 collective-permute-start.2
  16.9 2.9 %prepare.1 = (bf16[256,32]{1,0:T(8,128)(2,1)}, bf16[512,256]{1,0:T(8,128)(2,1)}, bf16[256,3456]{1,0:T(8,128)(2,1)}, bf16[128,2304]{1,0:T(8,128)(2,1)}) custom-call(bf16[64,7]{1,0:T(8,128)(2,1)} %copy.41.input_weight, bf16[128,64]{1,0:T(8,128)(2,1)} %copy.42.table, bf16[64,1728]{1,0:T(8,128)(2,1)} %kernel_fine.1, bf16[128,1728]{1,0:T(8,128)(2,1)} %copy.43.kernel_down), custom_call_target="tpu_custom_call" | custom-call | flops 1000000000 | bytes 4000000 | tf_op jit(solution)/shard_map/prepare/pallas_call | solution.py:400
  19.8 1.7 %collective-permute-start.3 = (bf16[352,128]{1,0:T(8,128)(2,1)S(1)}, bf16[352,128]{1,0:T(8,128)(2,1)S(1)}, u32[]{:S(2)}, u32[]{:S(2)}) collective-permute-start(bf16[352,128]{1,0:T(8,128)(2,1)S(1)} %get-tuple-element.42), channel_id=1, source_target_pairs={{0,3},{1,0},{2,1},{3,2},{4,7},{5,4},{6,5},{7,6},{8,11},{9,8},{10,9... | collective-permute-start | bytes 270344 | tf_op jit(solution)/shard_map/ppermute | solution.py:322
  21.5 0.0 collective-permute-done.2
  21.6 2.1 %collective-permute-done.3 = bf16[352,128]{1,0:T(8,128)(2,1)S(1)} collective-permute-done((bf16[352,128]{1,0:T(8,128)(2,1)S(1)}, bf16[352,128]{1,0:T(8,128)(2,1)S(1)}, u32[]{:S(2)}, u32[]{:S(2)}) %collective-permute-start.3) | collective-permute-done | bytes 90144 | tf_op jit(solution)/shard_map/ppermute | solution.py:322
  23.8 0.1 slice.102
  23.9 0.2 fusion.11
  24.1 1.1 %reshape.126.refs_1_ = bf16[2432,32]{1,0:T(8,128)(2,1)} reshape(bf16[16,19,256]{2,1,0:T(8,128)(2,1)S(1)} %fusion.11) | data formatting | bytes 311296 | tf_op jit(solution)/shard_map/reshape | solution.py:392
  25.3 0.6 concatenate.41
  25.9 0.8 reshape.129.refs_7_
  26.7 17.6 %forward.1 = (bf16[256,256]{1,0:T(8,128)(2,1)}, bf16[128,256]{1,0:T(8,128)(2,1)}, bf16[1,128,256]{2,1,0:T(8,128)(2,1)}, bf16[3456,128]{1,0:T(8,128)(2,1)}, f32[5...) custom-call(s32[3]{0:T(128)} %pad_add_fusion.refs_0_, bf16[2432,32]{1,0:T(8,128)(2,1)} %reshape.126.refs_1_, ...), custom_call_target="tpu_custom_call" | custom-call | flops 10000000000 | bytes 10000000 | tf_op jit(solution)/shard_map/forward/pallas_call | solution.py:419
  44.3 1.7 %collective-permute-start.6 = (bf16[128,256]{1,0:T(8,128)(2,1)}, bf16[128,256]{1,0:T(8,128)(2,1)S(1)}, u32[]{:S(2)}, u32[]{:S(2)}) collective-permute-start(bf16[128,256]{1,0:T(8,128)(2,1)} %bitcast.99), channel_id=1, source_target_pairs={{0,16},{16,0},{1,17},{17,1},{2,18},{18,2},{3,19},{19,3},{4,20},{20... | collective-permute-start | bytes 196616 | tf_op jit(solution)/shard_map/ppermute | solution.py:452
  46.0 2.8 %collective-permute-done.6 = bf16[128,256]{1,0:T(8,128)(2,1)S(1)} collective-permute-done((bf16[128,256]{1,0:T(8,128)(2,1)}, bf16[128,256]{1,0:T(8,128)(2,1)S(1)}, u32[]{:S(2)}, u32[]{:S(2)}) %collective-permute-start.6) | collective-permute-done | bytes 65568 | tf_op jit(solution)/shard_map/ppermute | solution.py:452
  48.8 0.0 copy-start.6
  48.8 0.6 copy-done.6
  49.4 3.5 %down_gradient.1 = bf16[2,16,54,128]{3,2,1,0:T(8,128)(2,1)} custom-call(bf16[128,256]{1,0:T(8,128)(2,1)} %get-tuple-element.19.refs_0_, bf16[1,128,256]{2,1,0:T(8,128)(2,1)} %bitcast.100, f32[128,256]{1,0:T(8,128)} %get-tuple-element.21.refs_2_, f32[5,2,5,2,8,384]{5,4,3,2,1,0:T(8,128)} %get-tuple-element.22.refs_3_), custom_call_target="tpu_custom_call" | custom-call | flops 2000000000 | bytes 1000000 | tf_op jit(solution)/shard_map/down_gradient/pallas_call | solution.py:462
  52.9 1.2 %constant_dynamic-slice_fusion.4 = (bf16[8,1,2,54,128]{4,3,1,0,2:T(8,128)(2,1)S(1)}, bf16[8,1,2,54,128]{4,3,1,0,2:T(8,128)(2,1)S(1)}) fusion(bf16[8,2,2,54,128]{4,3,1,0,2:T(8,128)(2,1)} %bitcast.93, s32[]{:T(128)S(6)} %select_n.121, s32[]{:T(128)S(6)} %select_n.122), kind=kLoop, calls=%fused_computation.61 | loop fusion | bytes 884744 | tf_op jit(solution)/shard_map/jit(dynamic_index_in_dim)/dynamic_slice | solution.py:332
  54.1 0.8 collective-permute-start.7
  54.9 1.1 %collective-permute-done.7 = bf16[8,2,54,128]{3,0,2,1:T(8,128)(2,1)S(1)} collective-permute-done((bf16[8,2,54,128]{3,0,2,1:T(8,128)(2,1)S(1)}, bf16[8,2,54,128]{3,0,2,1:T(8,128)(2,1)S(1)}, u32[]{:S(2)}, u32[]{:S(2)}) %collective-permute-start.7) | collective-permute-done | bytes 221216 | tf_op jit(solution)/shard_map/ppermute | solution.py:334
  56.1 1.5 %collective-permute-start.8 = (bf16[1,8,54,128]{3,1,2,0:T(8,128)(2,1)S(1)}, bf16[1,8,54,128]{3,1,2,0:T(8,128)(2,1)S(1)}, u32[]{:S(2)}, u32[]{:S(2)}) collective-permute-start(bf16[1,8,54,128]{3,1,2,0:T(8,128)(2,1)S(1)} %dynamic-slice_bitcast_fusion.3), channel_id=1, source_target_pairs={{0,16},{16,0},{1,17},{17,1},{2,18},{18,2},{3,19},{19,3},{4,20},{20... | collective-permute-start | bytes 331784 | tf_op jit(solution)/shard_map/ppermute | solution.py:334
  57.7 0.0 copy-done
  57.7 0.2 collective-permute-start.4
  57.9 3.7 %collective-permute-done.8 = bf16[1,8,54,128]{3,1,2,0:T(8,128)(2,1)S(1)} collective-permute-done((bf16[1,8,54,128]{3,1,2,0:T(8,128)(2,1)S(1)}, bf16[1,8,54,128]{3,1,2,0:T(8,128)(2,1)S(1)}, u32[]{:S(2)}, u32[]{:S(2)}) %collective-permute-start.8) | collective-permute-done | bytes 110624 | tf_op jit(solution)/shard_map/ppermute | solution.py:334
  61.6 0.2 constant_dynamic-slice_fusion.2
  61.8 0.0 copy-start.3
  61.8 1.4 %collective-permute-start.9 = (bf16[4,54,128]{2,1,0:T(8,128)(2,1)S(1)}, bf16[4,54,128]{2,1,0:T(8,128)(2,1)S(1)}, u32[]{:S(2)}, u32[]{:S(2)}) collective-permute-start(bf16[4,54,128]{2,1,0:T(8,128)(2,1)S(1)} %bitcast.98), channel_id=1, source_target_pairs={{0,2},{1,3},{2,0},{3,1},{4,6},{5,7},{6,4},{7,5},{8,10},{9,11},{10,... | collective-permute-start | bytes 165896 | tf_op jit(solution)/shard_map/ppermute | solution.py:334
  63.3 0.0 collective-permute-done.4
  63.3 0.1 fusion
  63.4 0.7 collective-permute-start.5
  64.2 2.5 %collective-permute-done.9 = bf16[4,54,128]{2,1,0:T(8,128)(2,1)S(1)} collective-permute-done((bf16[4,54,128]{2,1,0:T(8,128)(2,1)S(1)}, bf16[4,54,128]{2,1,0:T(8,128)(2,1)S(1)}, u32[]{:S(2)}, u32[]{:S(2)}) %collective-permute-start.9) | collective-permute-done | bytes 55328 | tf_op jit(solution)/shard_map/ppermute | solution.py:334
  66.7 3.7 %collective-permute-done.5 = bf16[4,216,128]{2,1,0:T(8,128)(2,1)S(1)} collective-permute-done((bf16[4,216,128]{2,1,0:T(8,128)(2,1)S(1)}, bf16[4,216,128]{2,1,0:T(8,128)(2,1)S(1)}, u32[]{:S(2)}, u32[]{:S(2)}) %collective-permute-start.5) | collective-permute-done | bytes 221216 | tf_op jit(solution)/shard_map/ppermute | solution.py:334
  70.4 0.1 fusion.2
  70.6 0.5 collective-permute-start.10
  71.1 0.0 copy-done.3
  71.1 4.5 %collective-permute-done.10 = bf16[2,270,128]{2,1,0:T(8,128)(2,1)S(1)} collective-permute-done((bf16[2,270,128]{2,1,0:T(8,128)(2,1)S(1)}, bf16[2,270,128]{2,1,0:T(8,128)(2,1)S(1)}, u32[]{:S(2)}, u32[]{:S(2)}) %collective-permute-start.10) | collective-permute-done | bytes 138272 | tf_op jit(solution)/shard_map/ppermute | solution.py:334
  75.7 1.5 %collective-permute-start.11 = (bf16[1,270,128]{2,1,0:T(8,128)(2,1)S(1)}, bf16[1,270,128]{2,1,0:T(8,128)(2,1)S(1)}, u32[]{:S(2)}, u32[]{:S(2)}) collective-permute-start(bf16[1,270,128]{2,1,0:T(8,128)(2,1)S(1)} %constant_dynamic-slice_fusion), channel_id=1, source_target_pairs={{0,8},{1,9},{2,10},{3,11},{4,12},{5,13},{6,14},{7,15},{8,0},{9,1},... | collective-permute-start | bytes 207368 | tf_op jit(solution)/shard_map/ppermute | solution.py:334
  77.2 0.7 slice_bitcast_fusion.1
  77.9 3.8 %collective-permute-done.11 = bf16[1,270,128]{2,1,0:T(8,128)(2,1)S(1)} collective-permute-done((bf16[1,270,128]{2,1,0:T(8,128)(2,1)S(1)}, bf16[1,270,128]{2,1,0:T(8,128)(2,1)S(1)}, u32[]{:S(2)}, u32[]{:S(2)}) %collective-permute-start.11) | collective-permute-done | bytes 69152 | tf_op jit(solution)/shard_map/ppermute | solution.py:334
  81.7 0.7 slice_bitcast_fusion
  82.4 0.1 slice_bitcast_fusion.3
  82.4 0.7 copy.51
  (48 shorter events, 0.8 us)
Async XLA Ops:
  0.6 15.9 %copy-start.2 = (bf16[128,8,4,8]{0,3,2,1:T(8,128)(2,1)S(1)}, bf16[128,8,4,8]{0,3,2,1:T(8,128)(2,1)}, u32[]{:S(2)}) copy-start(bf16[128,8,4,8]{0,3,2,1:T(8,128)(2,1)} %param.15) | copy-start | bytes 196612
  0.6 13.3 %copy-start.1 = (bf16[128,1728]{0,1:T(8,128)(2,1)S(1)}, bf16[128,1728]{0,1:T(8,128)(2,1)}, u32[]{:S(2)}) copy-start(bf16[128,1728]{0,1:T(8,128)(2,1)} %param.13) | copy-start | bytes 1327108
  0.7 14.2 %copy-start.4 = (bf16[128,64]{0,1:T(8,128)(2,1)S(1)}, bf16[128,64]{0,1:T(8,128)(2,1)}, u32[]{:S(2)}) copy-start(bf16[128,64]{0,1:T(8,128)(2,1)} %param.10) | copy-start | bytes 49156
  0.7 15.0 %copy-start.5 = (bf16[64,7]{0,1:T(8,128)(2,1)S(1)}, bf16[64,7]{0,1:T(8,128)(2,1)}, u32[]{:S(2)}) copy-start(bf16[64,7]{0,1:T(8,128)(2,1)} %param.11) | copy-start | bytes 2692
  9.0 7.4 %collective-permute-start = (bf16[160,128]{1,0:T(8,128)(2,1)S(1)}, bf16[160,128]{1,0:T(8,128)(2,1)S(1)}, u32[]{:S(2)}, u32[]{:S(2)}) collective-permute-start(bf16[160,128]{1,0:T(8,128)(2,1)S(1)} %pad_maximum_fusion.6), channel_id=1, source_target_pairs={{0,4},{4,8},{8,12},{12,0},{1,5},{5,9},{9,13},{13,1},{2,6},{6,10},{... | collective-permute-start | bytes 122888 | tf_op jit(solution)/shard_map/ppermute | solution.py:321
  11.2 5.1 %collective-permute-start.1 = (bf16[144,128]{1,0:T(8,128)(2,1)S(1)}, bf16[144,128]{1,0:T(8,128)(2,1)S(1)}, u32[]{:S(2)}, u32[]{:S(2)}) collective-permute-start(bf16[144,128]{1,0:T(8,128)(2,1)S(1)} %pad_maximum_fusion.7), channel_id=1, source_target_pairs={{0,12},{4,0},{8,4},{12,8},{1,13},{5,1},{9,5},{13,9},{2,14},{6,2},{... | collective-permute-start | bytes 110600 | tf_op jit(solution)/shard_map/ppermute | solution.py:322
  16.8 4.7 %collective-permute-start.2 = (bf16[352,128]{1,0:T(8,128)(2,1)S(1)}, bf16[352,128]{1,0:T(8,128)(2,1)S(1)}, u32[]{:S(2)}, u32[]{:S(2)}) collective-permute-start(bf16[352,128]{1,0:T(8,128)(2,1)S(1)} %get-tuple-element.41), channel_id=1, source_target_pairs={{0,1},{1,2},{2,3},{3,0},{4,5},{5,6},{6,7},{7,4},{8,9},{9,10},{10,1... | collective-permute-start | bytes 270344 | tf_op jit(solution)/shard_map/ppermute | solution.py:321
  19.8 3.9 %collective-permute-start.3 = (bf16[352,128]{1,0:T(8,128)(2,1)S(1)}, bf16[352,128]{1,0:T(8,128)(2,1)S(1)}, u32[]{:S(2)}, u32[]{:S(2)}) collective-permute-start(bf16[352,128]{1,0:T(8,128)(2,1)S(1)} %get-tuple-element.42), channel_id=1, source_target_pairs={{0,3},{1,0},{2,1},{3,2},{4,7},{5,4},{6,5},{7,6},{8,11},{9,8},{10,9... | collective-permute-start | bytes 270344 | tf_op jit(solution)/shard_map/ppermute | solution.py:322
  44.3 4.5 %collective-permute-start.6 = (bf16[128,256]{1,0:T(8,128)(2,1)}, bf16[128,256]{1,0:T(8,128)(2,1)S(1)}, u32[]{:S(2)}, u32[]{:S(2)}) collective-permute-start(bf16[128,256]{1,0:T(8,128)(2,1)} %bitcast.99), channel_id=1, source_target_pairs={{0,16},{16,0},{1,17},{17,1},{2,18},{18,2},{3,19},{19,3},{4,20},{20... | collective-permute-start | bytes 196616 | tf_op jit(solution)/shard_map/ppermute | solution.py:452
  48.8 0.6 copy-start.6
  52.9 4.7 %copy-start = (bf16[3456,128]{1,0:T(8,128)(2,1)S(1)}, bf16[3456,128]{1,0:T(8,128)(2,1)}, u32[]{:S(2)}) copy-start(bf16[3456,128]{1,0:T(8,128)(2,1)} %get-tuple-element.18) | copy-start | bytes 2654212
  54.1 1.9 %collective-permute-start.7 = (bf16[8,2,54,128]{3,0,2,1:T(8,128)(2,1)S(1)}, bf16[8,2,54,128]{3,0,2,1:T(8,128)(2,1)S(1)}, u32[]{:S(2)}, u32[]{:S(2)}) collective-permute-start(bf16[8,2,54,128]{3,0,2,1:T(8,128)(2,1)S(1)} %bitcast.95), channel_id=1, source_target_pairs={{0,1},{1,0},{2,3},{3,2},{4,5},{5,4},{6,7},{7,6},{8,9},{9,8},{10,11... | collective-permute-start | bytes 663560 | tf_op jit(solution)/shard_map/ppermute | solution.py:334
  56.1 5.4 %collective-permute-start.8 = (bf16[1,8,54,128]{3,1,2,0:T(8,128)(2,1)S(1)}, bf16[1,8,54,128]{3,1,2,0:T(8,128)(2,1)S(1)}, u32[]{:S(2)}, u32[]{:S(2)}) collective-permute-start(bf16[1,8,54,128]{3,1,2,0:T(8,128)(2,1)S(1)} %dynamic-slice_bitcast_fusion.3), channel_id=1, source_target_pairs={{0,16},{16,0},{1,17},{17,1},{2,18},{18,2},{3,19},{19,3},{4,20},{20... | collective-permute-start | bytes 331784 | tf_op jit(solution)/shard_map/ppermute | solution.py:334
  57.7 5.5 %collective-permute-start.4 = (bf16[8,216,128]{2,1,0:T(8,128)(2,1)S(1)}, bf16[8,216,128]{2,1,0:T(8,128)(2,1)S(1)}, u32[]{:S(2)}, u32[]{:S(2)}) collective-permute-start(bf16[8,216,128]{2,1,0:T(8,128)(2,1)S(1)} %dynamic-slice_bitcast_fusion), channel_id=1, source_target_pairs={{0,1},{1,0},{2,3},{3,2},{4,5},{5,4},{6,7},{7,6},{8,9},{9,8},{10,11... | collective-permute-start | bytes 1327112 | tf_op jit(solution)/shard_map/ppermute | solution.py:334
  61.8 9.3 %copy-start.3 = (bf16[256,256]{1,0:T(8,128)(2,1)S(1)}, bf16[256,256]{1,0:T(8,128)(2,1)}, u32[]{:S(2)}) copy-start(bf16[256,256]{1,0:T(8,128)(2,1)} %get-tuple-element.17) | copy-start | bytes 393220
  61.8 4.9 %collective-permute-start.9 = (bf16[4,54,128]{2,1,0:T(8,128)(2,1)S(1)}, bf16[4,54,128]{2,1,0:T(8,128)(2,1)S(1)}, u32[]{:S(2)}, u32[]{:S(2)}) collective-permute-start(bf16[4,54,128]{2,1,0:T(8,128)(2,1)S(1)} %bitcast.98), channel_id=1, source_target_pairs={{0,2},{1,3},{2,0},{3,1},{4,6},{5,7},{6,4},{7,5},{8,10},{9,11},{10,... | collective-permute-start | bytes 165896 | tf_op jit(solution)/shard_map/ppermute | solution.py:334
  63.4 7.0 %collective-permute-start.5 = (bf16[4,216,128]{2,1,0:T(8,128)(2,1)S(1)}, bf16[4,216,128]{2,1,0:T(8,128)(2,1)S(1)}, u32[]{:S(2)}, u32[]{:S(2)}) collective-permute-start(bf16[4,216,128]{2,1,0:T(8,128)(2,1)S(1)} %dynamic-slice_bitcast_fusion.1), channel_id=1, source_target_pairs={{0,2},{1,3},{2,0},{3,1},{4,6},{5,7},{6,4},{7,5},{8,10},{9,11},{10,... | collective-permute-start | bytes 663560 | tf_op jit(solution)/shard_map/ppermute | solution.py:334
  70.6 5.1 %collective-permute-start.10 = (bf16[2,270,128]{2,1,0:T(8,128)(2,1)S(1)}, bf16[2,270,128]{2,1,0:T(8,128)(2,1)S(1)}, u32[]{:S(2)}, u32[]{:S(2)}) collective-permute-start(bf16[2,270,128]{2,1,0:T(8,128)(2,1)S(1)} %dynamic-slice_bitcast_fusion.2), channel_id=1, source_target_pairs={{0,4},{1,5},{2,6},{3,7},{4,0},{5,1},{6,2},{7,3},{8,12},{9,13},{10,... | collective-permute-start | bytes 414728 | tf_op jit(solution)/shard_map/ppermute | solution.py:334
  75.7 5.9 %collective-permute-start.11 = (bf16[1,270,128]{2,1,0:T(8,128)(2,1)S(1)}, bf16[1,270,128]{2,1,0:T(8,128)(2,1)S(1)}, u32[]{:S(2)}, u32[]{:S(2)}) collective-permute-start(bf16[1,270,128]{2,1,0:T(8,128)(2,1)S(1)} %constant_dynamic-slice_fusion), channel_id=1, source_target_pairs={{0,8},{1,9},{2,10},{3,11},{4,12},{5,13},{6,14},{7,15},{8,0},{9,1},... | collective-permute-start | bytes 207368 | tf_op jit(solution)/shard_map/ppermute | solution.py:334

commit v3 on v2

v3 whole, which is shorter than its diff:
```python
import math

import jax
import jax.numpy as jnp
from jax import lax
from jax.experimental import pallas as pl
from jax.experimental.pallas import tpu as pltpu
from jax.sharding import PartitionSpec as P

F32 = jnp.float32
BF16 = jnp.bfloat16
CONTRACT_LANES = (((1,), (1,)), ((), ()))
CONTRACT_PLAIN = (((1,), (0,)), ((), ()))
LANES = 128
FINE_STEP = 8
MID_STEP = 4
TAPS_XY = [(kx, ky) for kx in range(3) for ky in range(3)]


def silu(values):
    half = 0.5 * values
    return half + half * jnp.tanh(half)


def silu_grad(values):
    sigmoid = 0.5 + 0.5 * jnp.tanh(0.5 * values)
    return sigmoid * (1.0 + values * (1.0 - sigmoid))


def flat(values):
    return values.reshape(-1, values.shape[-1])


def next_row(values):
    return pltpu.roll(values, values.shape[0] - 1, 0)


def previous_row(values):
    return pltpu.roll(values, 1, 0)


def pack_kernel(fields, grain_ids, out):
    comps, bx, by, bz = fields.shape
    quad = comps + 1
    column = lax.broadcasted_iota(jnp.int32, (bz, bz * quad), 1)
    row = lax.broadcasted_iota(jnp.int32, (bz, bz * quad), 0)
    total = jnp.zeros((bx * by, bz * quad), F32)
    for c in range(quad):
        plane = fields[c].astype(F32) if c < comps else (grain_ids[...] + 1).astype(F32)
        spread = jnp.where(column == row * quad + c, 1.0, 0.0).astype(BF16)
        total = total + jnp.dot(flat(plane).astype(BF16), spread, preferred_element_type=F32)
    out[...] = total.astype(BF16)


def widen_inputs(weight, table, weight_out, table_out):
    comps, c1 = weight.shape
    grains = table.shape[1]
    quad = comps + 1
    weight_out[...] = jnp.zeros(weight_out.shape, F32)
    table_out[...] = jnp.zeros(table_out.shape, BF16)
    entries = jnp.transpose(table[...].astype(F32), (1, 0)).astype(BF16)
    for k in range(4):
        weight_out[k * quad : k * quad + comps, k * c1 : (k + 1) * c1] = weight[...].astype(F32)
        table_out[k * grains : (k + 1) * grains, k * c1 : (k + 1) * c1] = entries


def widen_kernels(kernel_fine, kernel_down, fine_out, down_out):
    c1 = kernel_fine.shape[0]
    width = 3 * c1
    turned = jnp.transpose(kernel_fine[...].astype(F32), (1, 0))
    fine_out[...] = jnp.zeros(fine_out.shape, BF16)
    for tap in range(9):
        piece = turned[tap * width : (tap + 1) * width].astype(BF16)
        for k in range(4):
            start = tap * 2 * width + k * c1
            fine_out[start : start + width, k * c1 : (k + 1) * c1] = piece
        start = tap * 4 * c1
        down_out[start : start + width, :] = kernel_down[tap * width : (tap + 1) * width, :]
        down_out[start + width : start + 4 * c1, :] = jnp.zeros((c1, down_out.shape[1]), BF16)


def forward_kernel(
    place, feat, near, far, cot, weight, table, kernel_fine, kernel_down, kernel_bottle,
    bottle_out, mine_out, others_out, grad_out, slope_out, kept_out,
    emb, fine, coarse, grads, pre, fine_mask, coarse_mask, wide_feat, cot_rows, cotangent,
    wide_weight, wide_table, band_fine, band_down, *, dims,
):
    nx, by, bz, c1, c2, outs, grains, limits = dims
    total_y, total_z = limits
    ny_emb, ny_fine, ny_mid, ny_bot, ny_own = by + 11, by + 9, by // 2 + 4, by // 2 + 2, by // 2
    quad = weight.shape[0] + 1
    nq = fine.shape[4]
    coarse_x = nx // 2
    own_x = slope_out.shape[0] // (ny_own * nq)
    groups = coarse_x // own_x
    lanes = 4 * c1
    half = lanes // 2
    half_z = bz // 2

    widen_inputs(weight, table, wide_weight, wide_table)

    emb_rows = nx * ny_emb
    has_before = place[1] > 0
    has_after = place[1] < total_z // bz - 1
    odd = place[1] % 2 == 1
    near_all, far_all = near[...].astype(F32), far[...].astype(F32)
    before = jnp.where(has_before, jnp.where(odd, near_all, far_all), 0.0)
    after = jnp.where(has_after, jnp.where(odd, far_all, near_all), 0.0)
    low, high = before[:emb_rows], after[:emb_rows]
    spare = jnp.zeros((emb_rows, 4 * nq * quad - (bz + 12) * quad), F32)
    wide_feat[...] = jnp.concatenate(
        [low[:, (bz - 6) * quad :], feat[...].astype(F32), high[:, : 6 * quad], spare], axis=1
    )
    columns = coarse_x * ny_bot
    cotangent[...] = jnp.zeros(cotangent.shape, F32)
    edge_low = before[emb_rows:].reshape(-1, outs)
    edge_high = after[emb_rows:].reshape(-1, outs)
    slabs = outs // LANES
    cot_wide = cot[...].astype(F32)
    for k in range(slabs):
        cot_rows[k] = cot_wide[:, k * LANES : (k + 1) * LANES]
        for z in range(half_z):
            target = (z % 2 * slabs + k, pl.ds(z // 2 + 1, columns, stride=nq))
            cotangent[target] = cot_rows[k, pl.ds(z, columns, stride=half_z)]
        cotangent[slabs + k, pl.ds(0, columns, stride=nq)] = edge_low[:, k * LANES : (k + 1) * LANES]
        cotangent[k, pl.ds(half_z // 2 + 1, columns, stride=nq)] = edge_high[:, k * LANES : (k + 1) * LANES]

    shape = (ny_fine * nq, lanes)
    row = lax.broadcasted_iota(jnp.int32, shape, 0)
    lane = lax.broadcasted_iota(jnp.int32, shape, 1)
    y = place[0] * by - 5 + row // nq
    z = place[1] * bz - 5 + 4 * (row % nq) + lane // c1
    inside = (y >= 0) & (y < total_y) & (z >= 0) & (z < total_z)
    fine_mask[...] = jnp.where(inside, 1.0, 0.0)
    shape = (ny_mid * nq, 2 * c2)
    row = lax.broadcasted_iota(jnp.int32, shape, 0)
    lane = lax.broadcasted_iota(jnp.int32, shape, 1)
    y = place[0] * (by // 2) - 2 + row // nq
    z = place[1] * (bz // 2) - 2 + 2 * (row % nq) + lane // c2
    inside = (y >= 0) & (y < total_y // 2) & (z >= 0) & (z < total_z // 2)
    coarse_mask[...] = jnp.where(inside, 1.0, 0.0)

    layer_rows = ny_emb * nq
    blank = jnp.zeros((emb.shape[0], layer_rows, LANES), F32)
    emb[:, :layer_rows] = blank
    emb[:, (nx + 1) * layer_rows :] = blank
    fine[0, 0] = jnp.zeros(fine.shape[2:], F32)
    coarse[0] = jnp.zeros(coarse.shape[1:], F32)
    coarse[coarse_x + 1] = jnp.zeros(coarse.shape[1:], F32)
    grads[0] = jnp.zeros(grads.shape[1:], F32)
    grads[coarse_x + 1] = jnp.zeros(grads.shape[1:], F32)

    emb_step = 8
    chunk = emb_step * ny_emb

    def embed(step, carry):
        start = pl.multiple_of(step * chunk, 8)
        values = wide_feat[pl.ds(start, chunk), :]
        grain = lax.broadcasted_iota(jnp.int32, (1, grains), 1).astype(F32) + 1.0
        base = start * nq + layer_rows
        for q in range(nq):
            part = values[:, 4 * quad * q : 4 * quad * (q + 1)]
            picks = [
                jnp.where(part[:, quad * k + quad - 1 : quad * k + quad] == grain, 1.0, 0.0)
                for k in range(4)
            ]
            picks = jnp.concatenate([pick.astype(BF16) for pick in picks], axis=1)
            mixture = jnp.dot(
                part.astype(BF16), wide_weight[...].astype(BF16), preferred_element_type=F32
            ) + jnp.dot(picks, wide_table[...], preferred_element_type=F32)
            out = silu(mixture).astype(BF16).astype(F32)
            following = out[:, :half] if q else jnp.zeros((chunk, half), F32)
            for k in range(lanes // LANES):
                target = (k, pl.ds(base + q, chunk, stride=nq))
                emb[target] = out[:, k * LANES : (k + 1) * LANES]
            for k in range(half // LANES):
                target = (lanes // LANES + k, pl.ds(base + (q - 1) % nq, chunk, stride=nq))
                emb[target] = following[:, k * LANES : (k + 1) * LANES]
        return carry

    lax.fori_loop(0, nx // emb_step, embed, 0)

    widen_kernels(kernel_fine, kernel_down, band_fine, band_down)

    fine_step = FINE_STEP

    def fine_conv(step, carry):
        x0 = step * fine_step

        def layers(kx, ky):
            pieces = []
            for i in range(fine_step):
                start = pl.multiple_of((x0 + i + kx) * layer_rows + ky * nq, 8)
                pieces.append(
                    jnp.concatenate(
                        [emb[k, pl.ds(start, ny_fine * nq)] for k in range(emb.shape[0])], axis=1
                    )
                )
            return jnp.concatenate(pieces, axis=0).astype(BF16)

        patches = jnp.concatenate([layers(kx, ky) for kx, ky in TAPS_XY], axis=1)
        values = lax.dot_general(
            patches, band_fine[...], CONTRACT_PLAIN, preferred_element_type=F32
        )
        rows = ny_fine * nq
        for i in range(fine_step):
            layer = silu(values[i * rows : (i + 1) * rows]) * fine_mask[...]
            layer = layer.astype(BF16).astype(F32)
            following = next_row(layer[:, :half])
            for j in range(ny_fine):
                target = (x0 // 2 + (1 + i) // 2, (1 + i) % 2, j // 2, j % 2)
                fine[target + (slice(None), slice(0, lanes))] = layer[j * nq : (j + 1) * nq]
                fine[target + (slice(None), slice(lanes, None))] = following[j * nq : (j + 1) * nq]
        return carry

    lax.fori_loop(0, nx // fine_step, fine_conv, 0)

    first = place[2] * own_x
    kept_out[...] = flat(fine[pl.ds(first, own_x + 1), :, 2 : 3 + ny_own]).astype(BF16)

    mid_step = MID_STEP if coarse_x % MID_STEP == 0 else own_x

    def down_conv(step, carry):
        x0 = step * mid_step
        taps = [
            flat(
                fine[pl.ds(x0 + kx // 2, mid_step), kx % 2, ky // 2 : ky // 2 + ny_mid, ky % 2]
            ).astype(BF16)
            for kx, ky in TAPS_XY
        ]
        patches = jnp.concatenate(
            [
                jnp.concatenate([tap[:, 2 * k * c1 : 2 * k * c1 + lanes] for tap in taps], axis=1)
                for k in range(2)
            ],
            axis=0,
        )
        values = side_by_side(
            lax.dot_general(patches, band_down[...], CONTRACT_PLAIN, preferred_element_type=F32)
        )
        pre[pl.ds(x0, mid_step)] = values.reshape(mid_step, ny_mid, nq, 2 * c2)
        inside = coarse_mask[...]
        inside = jnp.concatenate([inside] * mid_step, axis=0)
        act = (silu(values) * inside).astype(BF16).astype(F32)
        where = pl.ds(1 + x0, mid_step)
        whole = (mid_step, ny_mid, nq)
        coarse[where, :, :, :c2] = previous_row(act[:, c2:]).reshape(whole + (c2,))
        coarse[where, :, :, c2 : 3 * c2] = act.reshape(whole + (2 * c2,))
        coarse[where, :, :, 3 * c2 :] = next_row(act[:, :c2]).reshape(whole + (c2,))
        return carry

    lax.fori_loop(0, coarse_x // mid_step, down_conv, 0)

    bot_rows = ny_bot * nq

    def bottle_conv(step, carry):
        x0 = step * mid_step
        taps = [
            flat(coarse[pl.ds(x0 + kx, mid_step), ky : ky + ny_bot]).astype(BF16)
            for kx, ky in TAPS_XY
        ]
        patches = jnp.concatenate(
            [
                jnp.concatenate([tap[:, k * c2 : (k + 3) * c2] for tap in taps], axis=1)
                for k in range(2)
            ],
            axis=0,
        )
        values = side_by_side(
            lax.dot_general(
                patches, kernel_bottle[...], CONTRACT_LANES, preferred_element_type=F32
            )
        )
        start = pl.multiple_of(x0 * bot_rows, 8)
        spread = [
            cotangent[k, pl.ds(start, mid_step * bot_rows)] for k in range(cotangent.shape[0])
        ]
        grad = jnp.concatenate(spread, axis=1) * silu_grad(values)
        grad = grad.astype(BF16).astype(F32)
        where = pl.ds(1 + x0, mid_step)
        whole = (mid_step, ny_bot, nq)
        grads[where, :, :, :outs] = previous_row(grad[:, outs:]).reshape(whole + (outs,))
        grads[where, :, :, outs : 3 * outs] = grad.reshape(whole + (2 * outs,))
        grads[where, :, :, 3 * outs :] = next_row(grad[:, :outs]).reshape(whole + (outs,))
        act = silu(values).reshape(whole + (2 * outs,))[:, 1 : 1 + ny_own]
        start = pl.multiple_of(x0 * ny_own * nq, 16)
        bottle_out[pl.ds(start, mid_step * ny_own * nq), :] = flat(act).astype(BF16)
        return carry

    lax.fori_loop(0, coarse_x // mid_step, bottle_conv, 0)

    stacked = jnp.concatenate(
        [kernel_bottle[:, t * c2 : (t + 1) * c2] for t in range(27)], axis=0
    )
    own_rows = ny_own * nq

    def transpose_conv(step, carry):
        x0 = step * mid_step
        taps = [
            flat(grads[pl.ds(x0 + 2 - kx, mid_step), 2 - ky : 2 - ky + ny_own]).astype(BF16)
            for kx, ky in TAPS_XY
        ]
        patches = jnp.concatenate(
            [
                jnp.concatenate(
                    [
                        tap[:, (k + 2 - kz) * outs : (k + 3 - kz) * outs]
                        for tap in taps
                        for kz in range(3)
                    ],
                    axis=1,
                )
                for k in range(2)
            ],
            axis=0,
        )
        values = side_by_side(
            lax.dot_general(patches, stacked, CONTRACT_PLAIN, preferred_element_type=F32)
        )
        values = values.astype(BF16)
        for k in range(mid_step // own_x):
            piece = values[k * own_x * own_rows : (k + 1) * own_x * own_rows]
            owner = lax.rem(x0 // own_x + k - place[2] + groups, groups)

            @pl.when(owner == 0)
            def _(piece=piece):
                mine_out[...] = piece

            @pl.when(owner > 0)
            def _(piece=piece, owner=owner):
                others_out[owner - 1] = piece

        return carry

    lax.fori_loop(0, coarse_x // mid_step, transpose_conv, 0)

    scale = 1.0 / math.sqrt(coarse_x * (total_y // 2) * (total_z // 2))
    own = flat(grads[1 : 1 + coarse_x, 1 : 1 + ny_own, :, outs : 3 * outs])
    place_row = lax.broadcasted_iota(jnp.int32, own.shape, 0) % nq
    own = jnp.where((place_row >= 1) & (place_row <= bz // 4), own, 0.0)
    turned = jnp.transpose(own, (1, 0)).astype(BF16)
    for number, (kx, ky) in enumerate(TAPS_XY):
        rows = flat(coarse[kx : kx + coarse_x, ky + 1 : ky + 1 + ny_own]).astype(BF16)
        product = jnp.dot(turned, rows, preferred_element_type=F32)
        total = product[:outs, : 3 * c2] + product[outs:, c2:]
        total = jnp.transpose(total * scale, (1, 0)).astype(BF16)
        grad_out[number * 3 * c2 : (number + 1) * 3 * c2, :] = total

    slope = silu_grad(pre[pl.ds(first, own_x), 2 : 2 + ny_own])
    slope_out[...] = flat(slope)


def down_kernel(mine, other, slope, kept, grad_out, total_ref, fine, *, dims):
    bz, c1, c2, nq, scale = dims
    own_x, ny_own = fine.shape[0] - 1, fine.shape[2] - 1
    grad = jnp.sum(other[...].astype(F32), axis=0) + mine[...].astype(F32)
    grad = (grad * slope[...]).astype(BF16).astype(F32)
    place_row = lax.broadcasted_iota(jnp.int32, grad.shape, 0) % nq
    grad = jnp.where((place_row >= 1) & (place_row <= bz // 4), grad, 0.0)
    turned = jnp.transpose(grad, (1, 0)).astype(BF16)
    fine[...] = kept[...].astype(F32).reshape(fine.shape)
    for number, (kx, ky) in enumerate(TAPS_XY):
        rows = flat(
            fine[kx // 2 : kx // 2 + own_x, kx % 2, ky // 2 : ky // 2 + ny_own, ky % 2]
        ).astype(BF16)
        product = jnp.dot(turned, rows, preferred_element_type=F32)
        total = product[:c2, : 4 * c1] + product[c2:, 2 * c1 : 6 * c1]
        total = jnp.transpose(total * scale, (1, 0))[: 3 * c1]
        total_ref[number * 3 * c1 : (number + 1) * 3 * c1, :] = total
    if len(grad_out.shape) == 2:
        grad_out[...] = total_ref[...].astype(BF16)
        return
    chunks, rows = grad_out.shape[0], grad_out.shape[2]
    low = lax.broadcasted_iota(jnp.int32, (rows, c2), 1) < c2 // 2
    for k in range(chunks):
        first = total_ref[2 * k * rows : (2 * k + 1) * rows, :]
        second = total_ref[(2 * k + 1) * rows : (2 * k + 2) * rows, :]
        grad_out[k, 0] = jnp.where(low, first, pltpu.roll(second, c2 // 2, 1)).astype(BF16)
        grad_out[k, 1] = jnp.where(low, pltpu.roll(first, c2 // 2, 1), second).astype(BF16)


def halo(forward, backward, axis):
    count = lax.axis_size(axis)
    before = lax.ppermute(forward, axis, [(i, (i + 1) % count) for i in range(count)])
    after = lax.ppermute(backward, axis, [(i, (i - 1) % count) for i in range(count)])
    return before, after


def swap_halo(forward, backward, axis):
    count = lax.axis_size(axis)
    odd = lax.axis_index(axis) % 2 == 1
    if count % 2:
        before, after = halo(forward, backward, axis)
        return jnp.where(odd, before, after), jnp.where(odd, after, before)
    near = lax.ppermute(
        jnp.where(odd, backward, forward), axis, [(i, i ^ 1) for i in range(count)]
    )
    far = lax.ppermute(
        jnp.where(odd, forward, backward),
        axis,
        [(i, (i + (1 if i % 2 else -1)) % count) for i in range(count)],
    )
    return near, far


def open_halo(forward, backward, axis):
    count = lax.axis_size(axis)
    index = lax.axis_index(axis)
    before, after = halo(forward, backward, axis)
    zero = jnp.zeros((), before.dtype)
    return jnp.where(index > 0, before, zero), jnp.where(index < count - 1, after, zero)


def side_by_side(values):
    rows = values.shape[0] // 2
    return jnp.concatenate([values[:rows], values[rows:]], axis=1)


def halve(block, axes, bit, dim=0):
    count = math.prod(lax.axis_size(axis) for axis in axes)
    index = lax.axis_index(axes)
    pairs = block.shape[:dim] + ((-1, 2) if block.shape[dim] > 2 else (2,))
    split = block.reshape(pairs + block.shape[dim + 1 :])
    dim = len(pairs) - 1
    mine = (index // bit) % 2
    keep = lax.dynamic_index_in_dim(split, mine, dim, keepdims=False)
    send = lax.dynamic_index_in_dim(split, 1 - mine, dim, keepdims=False)
    got = lax.ppermute(send, axes, [(i, i ^ bit) for i in range(count)])
    return keep.astype(F32) + got.astype(F32)


def halve_all(block, axes, bit=1):
    count = block.shape[0]
    while count > 1:
        block = halve(block.astype(BF16), axes, bit)
        bit, count = 2 * bit, count // 2
    return block


def window(
    fields, grain_ids, material_table, input_weight, kernel_fine, kernel_down, kernel_bottle,
    cotangent,
):
    comps, bx, by, bz = fields.shape
    grains, c1 = material_table.shape
    c2 = kernel_down.shape[0]
    outs_true = kernel_bottle.shape[0]
    gx, gy, gz = lax.axis_size("gx"), lax.axis_size("gy"), lax.axis_size("gz")
    nx, total_y, total_z = bx * gx, by * gy, bz * gz
    coarse_x = nx // 2
    nq = -(-(bz + 12) // 32) * 8
    outs = -(-outs_true // 128) * 128
    if outs != outs_true:
        kernel_bottle = jnp.pad(kernel_bottle, ((0, outs - outs_true), (0, 0)))
        cotangent = jnp.pad(cotangent, ((0, outs - outs_true), (0, 0), (0, 0), (0, 0)))

    quad = comps + 1
    half_y, half_z = by // 2, bz // 2
    vmem = pl.BlockSpec(memory_space=pltpu.VMEM)
    feat = pl.pallas_call(
        pack_kernel,
        out_shape=jax.ShapeDtypeStruct((bx * by, bz * quad), BF16),
        in_specs=[vmem] * 2,
        out_specs=vmem,
        compiler_params=pltpu.CompilerParams(vmem_limit_bytes=4 << 20),
        name="pack",
    )(fields, grain_ids)
    feat = lax.all_gather(feat.reshape(bx, by, bz * quad), "gx", axis=0, tiled=True)
    cot = jnp.transpose(cotangent, (1, 2, 3, 0))

    def packed(first, second):
        return jnp.concatenate([first.reshape(-1, 128), second.reshape(-1, 128)], axis=0)

    def unpacked(both, first_shape, second_shape):
        cut = math.prod(first_shape) // 128
        return both[:cut].reshape(first_shape), both[cut:].reshape(second_shape)

    before, after = open_halo(
        packed(feat[:, by - 6 :], cot[:, half_y - 1 :]), packed(feat[:, :5], cot[:, :1]), "gy"
    )
    edge = (coarse_x, 1, half_z, outs)
    feat_before, cot_before = unpacked(before, (nx, 6, bz * quad), edge)
    feat_after, cot_after = unpacked(after, (nx, 5, bz * quad), edge)
    feat = jnp.concatenate([feat_before, feat, feat_after], axis=1)
    cot = jnp.concatenate([cot_before, cot, cot_after], axis=1)
    near, far = swap_halo(
        packed(feat, cot[:, :, half_z - 1 :]), packed(feat, cot[:, :, :1]), "gz"
    )
    place = jnp.stack([lax.axis_index("gy"), lax.axis_index("gz"), lax.axis_index("gx")])

    ny_own, ny_mid, ny_bot = by // 2, by // 2 + 4, by // 2 + 2
    own_x = bx // 2
    lanes = 6 * c1
    own_rows = own_x * ny_own * nq
    kept = (own_x + 1, 2, ny_own + 1, 2, nq, lanes)
    limit = min(60 << 20, (14 << 20) + nx * (5 << 17))
    bottle_rows, mine, others, bottle_part, slope, fine_own = pl.pallas_call(
        lambda *refs: forward_kernel(
            *refs, dims=(nx, by, bz, c1, c2, outs, grains, (total_y, total_z))
        ),
        out_shape=(
            jax.ShapeDtypeStruct((coarse_x * ny_own * nq, 2 * outs), BF16),
            jax.ShapeDtypeStruct((own_rows, 2 * c2), BF16),
            jax.ShapeDtypeStruct((gx - 1, own_rows, 2 * c2), BF16),
            jax.ShapeDtypeStruct((27 * c2, outs), BF16),
            jax.ShapeDtypeStruct((own_x * ny_own * nq, 2 * c2), F32),
            jax.ShapeDtypeStruct((math.prod(kept[:-1]), lanes), BF16),
        ),
        in_specs=[pl.BlockSpec(memory_space=pltpu.SMEM)] + [vmem] * 9,
        out_specs=(vmem,) * 6,
        scratch_shapes=[
            pltpu.VMEM((lanes // LANES, (nx + 2) * (by + 11) * nq, LANES), F32),
            pltpu.VMEM((coarse_x + 1, 2, (by + 10) // 2, 2, nq, lanes), F32),
            pltpu.VMEM((coarse_x + 2, ny_mid, nq, 4 * c2), F32),
            pltpu.VMEM((coarse_x + 2, ny_bot, nq, 4 * outs), F32),
            pltpu.VMEM((coarse_x, ny_mid, nq, 2 * c2), F32),
            pltpu.VMEM(((by + 9) * nq, 4 * c1), F32),
            pltpu.VMEM((ny_mid * nq, 2 * c2), F32),
            pltpu.VMEM((nx * (by + 11), 4 * nq * quad), F32),
            pltpu.VMEM((outs // LANES, coarse_x * ny_bot * bz // 2, LANES), F32),
            pltpu.VMEM((2 * outs // LANES, coarse_x * ny_bot * nq, LANES), F32),
            pltpu.VMEM((4 * quad, 4 * c1), F32),
            pltpu.VMEM((4 * grains, 4 * c1), BF16),
            pltpu.VMEM((9 * lanes, 4 * c1), BF16),
            pltpu.VMEM((9 * 4 * c1, c2), BF16),
        ],
        compiler_params=pltpu.CompilerParams(vmem_limit_bytes=limit),
        cost_estimate=pl.CostEstimate(flops=10**10, transcendentals=0, bytes_accessed=10**7),
        name="forward",
    )(
        place, feat.reshape(-1, bz * quad), near, far, cot.reshape(-1, outs),
        input_weight.T, material_table.T, kernel_fine, kernel_down.T, kernel_bottle,
    )

    bottle = bottle_rows.reshape(coarse_x, ny_own, 2 * nq, outs)[:, :, 2 : 2 + bz // 2]
    bottle = jnp.transpose(bottle, (3, 0, 1, 2))[:outs_true]

    other = jnp.stack(
        [
            lax.ppermute(others[k - 1], "gx", [(i, (i + k) % gx) for i in range(gx)])
            for k in range(1, gx)
        ]
    )

    chunks = gy * gz
    rows = 27 * c1 // chunks
    paired = gx == 2 and rows % 2 == 0
    part_shape = (chunks, 2, rows // 2, c2) if paired else (27 * c1, c2)
    scale = 1.0 / math.sqrt(coarse_x * (total_y // 2) * (total_z // 2))
    down_part = pl.pallas_call(
        lambda *refs: down_kernel(*refs, dims=(bz, c1, c2, nq, scale)),
        out_shape=jax.ShapeDtypeStruct(part_shape, BF16),
        in_specs=[vmem] * 4,
        out_specs=vmem,
        scratch_shapes=[
            pltpu.VMEM((27 * c1, c2), F32),
            pltpu.VMEM(kept, F32),
        ],
        compiler_params=pltpu.CompilerParams(vmem_limit_bytes=10 << 20),
        cost_estimate=pl.CostEstimate(flops=2 * 10**9, transcendentals=0, bytes_accessed=10**6),
        name="down_gradient",
    )(mine, other, slope, fine_own)

    both = ("gy", "gz")
    bottle_part = bottle_part.reshape(chunks, 27 * c2 // chunks, outs)
    if paired:
        bottle_part = halve(bottle_part, both, 1).astype(BF16)
        bottle_part = halve(bottle_part, both, 2).astype(BF16)
        down_part = halve(down_part, both, 1).astype(BF16)
        down_part = halve(down_part, ("gx",), 1, 1).astype(BF16)
        down_part = halve(down_part, both, 2).astype(BF16)
        summed = halve_all(jnp.concatenate([bottle_part, down_part], axis=1), both, 4)
        cut = bottle_part.shape[1]
        grad_bottle = summed[:cut, :outs_true].T
        halves = summed[cut:]
        grad_down = jnp.concatenate([halves[:, : c2 // 2].T, halves[:, c2 // 2 :].T], axis=1)
    else:
        grad_bottle = halve_all(bottle_part, both)[:, :outs_true].T
        down_part = jnp.transpose(down_part.reshape(27 * c1, gx, c2 // gx), (1, 0, 2))
        down_part = halve_all(down_part, ("gx",)).reshape(chunks, rows, c2 // gx)
        grad_down = halve_all(down_part, both).T
    return (bottle, grad_down, grad_bottle)


def solution(mesh):
    placed = (
        P(None, "gx", "gy", "gz"),
        P("gx", "gy", "gz"),
        P(),
        P(),
        P(),
        P(),
        P("gx", None),
        P("gx", None, "gy", "gz"),
    )
    return jax.shard_map(
        window,
        mesh=mesh,
        in_specs=placed,
        out_specs=(P("gx", None, "gy", "gz"), P("gx", ("gy", "gz")), P("gx", ("gy", "gz"))),
        check_vma=False,
    )
```

time: 83.4 us -> 74.5 us (0.89)
  Pallas kernels: 24.1 us -> 15.8 us
  waiting for transfers between devices: 24.2 us -> 32.3 us
  local copies, waits for them, and re-layouts: 11 us -> 7.6 us
  starting transfers between devices: 14.4 us -> 11.4 us
  other arithmetic: 3.05 us -> 0.57 us
    pallas_call x3, Pallas kernels: 24.1 us -> 15.8 us  [the longest x1 14.4 us: window(): pl.pallas_call(lambda *refs: forward_kernel(*refs, dims=(nx, by, bz, c1,...]
    ppermute x5, waiting for transfers between devices: 4.92 us -> 11.3 us  [the longest x1 4.21 us: halo(): lax.ppermute(forward, axis, [(i, (i + 1) % count) for i in range(count)])]
    ppermute x7, starting transfers between devices: 6.69 us -> 3.99 us  [halve(): got = lax.ppermute(send, axes, [(i, i ^ bit) for i in range(count)])]
    reshape x4 -> x2, local copies, waits for them, and re-layouts: 2.18 us -> 0.09 us  [the longest x1 0.05 us: window(): bottle_rows.reshape(coarse_x, ny_own, 2 * nq, outs)[:, :, 2:2 + bz // 2]]
    ppermute x7, waiting for transfers between devices: 19.3 us -> 21 us  [halve(): got = lax.ppermute(send, axes, [(i, i ^ bit) for i in range(count)])]
    dynamic_slice x4, local copies, waits for them, and re-layouts: 1.45 us -> 0.36 us  [the longest x2 0.28 us: halve(): keep = lax.dynamic_index_in_dim(split, mine, dim, keepdims=False)]
    transpose x1 -> x0, other arithmetic: 0.93 us -> none  [per_device(): feat = jnp.transpose(feat, (1, 2, 3, 0)).reshape(bx, by, bz * quad)]
    unnamed x18 -> x23, local copies, waits for them, and re-layouts: 3.77 us -> 4.65 us
  transfers between devices with their start and end apart: 12 -> 12, of which waited for: 8 -> 10; matrix products, arithmetic and copies ran while one was open for 5% -> 2% of each run, Pallas kernels for 4% -> 0%
where the time goes in v3:
time: 74.5 us; the launch traced here: 74.3 us
  waiting for transfers between devices  32.3 us (43%)
  Pallas kernels  15.8 us (21%)
  starting transfers between devices  11.4 us (15%)
  local copies, waits for them, and re-layouts  7.6 us (10%)
  blocking collectives  5.33 us (7%)
  between operations  1.2 us (2%)
    ppermute x7, waiting for transfers between devices, halve(): got = lax.ppermute(send, axes, [(i, i ^ bit) for i in range(count)])  21 us
    pallas_call x1, Pallas kernels, window(): pl.pallas_call(lambda *refs: forward_kernel(*refs, dims=(nx, by, bz, c1,...  14.4 us
    all_gather x1, blocking collectives, window(): lax.all_gather(feat.reshape(bx, by, bz * quad), 'gx', axis=0, tiled=True)  5.33 us
    unnamed x23, local copies, waits for them, and re-layouts  4.65 us
    ppermute x1, waiting for transfers between devices, halo(): lax.ppermute(forward, axis, [(i, (i + 1) % count) for i in range(count)])  4.21 us
    ppermute x1, starting transfers between devices, halo(): lax.ppermute(backward, axis, [(i, (i - 1) % count) for i in range(count)])  4.2 us
    ppermute x7, starting transfers between devices, halve(): got = lax.ppermute(send, axes, [(i, i ^ bit) for i in range(count)])  3.99 us
    ppermute x1, waiting for transfers between devices, window(): lax.ppermute(others[k - 1], 'gx', [(i, (i + k) % gx) for i in range(gx)])  2.95 us
  transfers between devices with their start and end apart: 12, of which 10 were waited for; matrix products, arithmetic and copies ran while one was open for 2% of the time, Pallas kernels for 0%

profile of v3, /device:TPU:0, one launch (start us, length us, event | category | flops | bytes accessed | tf_op | source)
XLA Modules:
  0.0 74.3 jit_solution(12903347568248384170)
XLA Ops:
  0.6 0.0 copy-start.1
  0.6 0.7 %slice_bitcast_fusion.7 = (bf16[64,128]{1,0:T(8,128)(2,1)S(1)}, bf16[64,128]{1,0:T(8,128)(2,1)S(1)}) fusion(bf16[8,4,8,128]{3,2,1,0:T(8,128)(2,1)} %bitcast.97), kind=kLoop, calls=%fused_computation.41 | loop fusion | bytes 65536 | tf_op jit(solution)/shard_map/reshape | solution.py:472
  1.4 0.0 copy-done.1
  1.4 0.0 copy-start
  1.4 0.9 %copy-done = bf16[7,8,8,16]{3,2,1,0:T(8,128)(2,1)S(1)} copy-done((bf16[7,8,8,16]{3,2,1,0:T(8,128)(2,1)S(1)}, bf16[7,8,8,16]{3,2,1,0:T(8,128)(2,1)}, u32[]{:S(2)}) %copy-start) | copy-done | bytes 14360
  2.3 0.1 pack.1
  2.5 5.3 %all_gather.3 = bf16[16,8,128]{2,1,0:T(8,128)(2,1)S(1)} all-gather(bf16[8,8,128]{2,1,0:T(8,128)(2,1)S(1)} %bitcast.84), channel_id=1, replica_groups=mesh['gx'=2,'gy'=4,'gz'=4] {'gx'}, dimensions={0}, use_global_device_ids=true | all-gather | bytes 49152 | tf_op jit(solution)/shard_map/all_gather | solution.py:468
  7.8 4.2 %collective-permute-start.1 = (bf16[144,128]{1,0:T(8,128)(2,1)S(1)}, bf16[144,128]{1,0:T(8,128)(2,1)S(1)}, u32[]{:S(2)}, u32[]{:S(2)}) collective-permute-start(bf16[144,128]{1,0:T(8,128)(2,1)S(1)} %pad_maximum_fusion.5), channel_id=1, source_target_pairs={{0,12},{4,0},{8,4},{12,8},{1,13},{5,1},{9,5},{13,9},{2,14},{6,2},{... | collective-permute-start | bytes 110600 | tf_op jit(solution)/shard_map/ppermute | solution.py:385
  12.1 0.1 collective-permute-start
  12.2 1.5 %collective-permute-done.1 = bf16[144,128]{1,0:T(8,128)(2,1)S(1)} collective-permute-done((bf16[144,128]{1,0:T(8,128)(2,1)S(1)}, bf16[144,128]{1,0:T(8,128)(2,1)S(1)}, u32[]{:S(2)}, u32[]{:S(2)}) %collective-permute-start.1) | collective-permute-done | bytes 36896 | tf_op jit(solution)/shard_map/ppermute | solution.py:385
  13.7 0.0 copy-start.2
  13.7 4.2 %collective-permute-done = bf16[160,128]{1,0:T(8,128)(2,1)S(1)} collective-permute-done((bf16[160,128]{1,0:T(8,128)(2,1)S(1)}, bf16[160,128]{1,0:T(8,128)(2,1)S(1)}, u32[]{:S(2)}, u32[]{:S(2)}) %collective-permute-start) | collective-permute-done | bytes 40992 | tf_op jit(solution)/shard_map/ppermute | solution.py:384
  18.1 0.0 copy-start.9
  18.1 0.0 copy-start.3
  18.1 0.8 %copy-done.9 = bf16[128,8,4,8]{0,3,2,1:T(8,128)(2,1)S(1)} copy-done((bf16[128,8,4,8]{0,3,2,1:T(8,128)(2,1)S(1)}, bf16[128,8,4,8]{0,3,2,1:T(8,128)(2,1)}, u32[]{:S(2)}) %copy-start.9) | copy-done | bytes 65560
  18.9 0.1 slice_reduce_fusion
  19.1 0.0 copy-start.4
  19.2 0.0 copy-start.5
  19.2 0.1 collective-permute-start.2
  19.3 1.6 %collective-permute-start.3 = (bf16[352,128]{1,0:T(8,128)(2,1)S(1)}, bf16[352,128]{1,0:T(8,128)(2,1)S(1)}, u32[]{:S(2)}, u32[]{:S(2)}) collective-permute-start(bf16[352,128]{1,0:T(8,128)(2,1)S(1)} %get-tuple-element.31), channel_id=1, source_target_pairs={{0,3},{1,2},{2,1},{3,0},{4,7},{5,6},{6,5},{7,4},{8,11},{9,10},{10,... | collective-permute-start | bytes 270344 | tf_op jit(solution)/shard_map/ppermute | solution.py:398
  20.9 0.1 pad_add_fusion.refs_0_
  21.0 0.0 collective-permute-done.2.refs_2_
  21.0 2.7 %collective-permute-done.3.refs_3_ = bf16[352,128]{1,0:T(8,128)(2,1)S(1)} collective-permute-done((bf16[352,128]{1,0:T(8,128)(2,1)S(1)}, bf16[352,128]{1,0:T(8,128)(2,1)S(1)}, u32[]{:S(2)}, u32[]{:S(2)}) %collective-permute-start.3) | collective-permute-done | bytes 90144 | tf_op jit(solution)/shard_map/ppermute | solution.py:398
  23.6 0.0 copy-start.6
  23.7 0.0 copy-done.2
  23.7 0.0 copy-done.3
  23.7 0.0 copy-done.4
  23.7 0.0 copy-done.5
  23.7 0.7 copy-done.6
  24.3 14.4 %forward.1 = (bf16[256,256]{1,0:T(8,128)(2,1)S(1)}, bf16[128,256]{1,0:T(8,128)(2,1)S(1)}, bf16[1,128,256]{2,1,0:T(8,128)(2,1)S(1)}, bf16[3456,128]{1,0:T(8,128)(...) custom-call(s32[3]{0:T(128)S(1)} %pad_add_fusion.refs_0_, bf16[304,128]{1,0:T(8,128)(2,1)S(1)} %reshape.83.refs_1_, ...), custom_call_target="tpu_custom_call" | custom-call | flops 10000000000 | bytes 10000000 | tf_op jit(solution)/shard_map/forward/pallas_call | solution.py:497
  38.7 0.0 copy-start.7
  38.8 0.6 copy-done.7
  39.4 1.5 %collective-permute-start.6 = (bf16[128,256]{1,0:T(8,128)(2,1)S(1)}, bf16[128,256]{1,0:T(8,128)(2,1)S(1)}, u32[]{:S(2)}, u32[]{:S(2)}) collective-permute-start(bf16[128,256]{1,0:T(8,128)(2,1)S(1)} %bitcast.86), channel_id=1, source_target_pairs={{0,16},{16,0},{1,17},{17,1},{2,18},{18,2},{3,19},{19,3},{4,20},{20... | collective-permute-start | bytes 196616 | tf_op jit(solution)/shard_map/ppermute | solution.py:540
  40.9 3.0 %collective-permute-done.6 = bf16[128,256]{1,0:T(8,128)(2,1)S(1)} collective-permute-done((bf16[128,256]{1,0:T(8,128)(2,1)S(1)}, bf16[128,256]{1,0:T(8,128)(2,1)S(1)}, u32[]{:S(2)}, u32[]{:S(2)}) %collective-permute-start.6) | collective-permute-done | bytes 65568 | tf_op jit(solution)/shard_map/ppermute | solution.py:540
  43.8 0.0 copy-start.8
  43.8 0.9 %copy-done.8 = f32[128,256]{1,0:T(8,128)S(1)} copy-done((f32[128,256]{1,0:T(8,128)S(1)}, f32[128,256]{1,0:T(8,128)}, u32[]{:S(2)}) %copy-start.8) | copy-done | bytes 131096
  44.7 1.3 %down_gradient.1 = bf16[16,2,54,128]{3,2,1,0:T(8,128)(2,1)S(1)} custom-call(bf16[128,256]{1,0:T(8,128)(2,1)S(1)} %get-tuple-element.11.refs_0_, bf16[1,128,256]{2,1,0:T(8,128)(2,1)S(1)} %bitcast.87, f32[128,256]{1,0:T(8,128)S(1)} %copy-done.8, bf16[800,384]{1,0:T(8,128)(2,1)S(1)} %get-tuple-element.14.refs_3_), custom_call_target="tpu_custom_call" | custom-call | flops 2000000000 | bytes 1000000 | tf_op jit(solution)/shard_map/down_gradient/pallas_call | solution.py:550
  46.1 0.1 copy.44
  46.2 0.1 collective-permute-start.7
  46.3 1.4 %collective-permute-done.7 = bf16[8,2,54,128]{3,0,2,1:T(8,128)(2,1)S(1)} collective-permute-done((bf16[8,2,54,128]{3,0,2,1:T(8,128)(2,1)S(1)}, bf16[8,2,54,128]{3,0,2,1:T(8,128)(2,1)S(1)}, u32[]{:S(2)}, u32[]{:S(2)}) %collective-permute-start.7) | collective-permute-done | bytes 221216 | tf_op jit(solution)/shard_map/ppermute | solution.py:428
  47.7 0.1 fusion.1
  47.8 1.6 %collective-permute-start.8 = (bf16[8,54,128]{2,0,1:T(8,128)(2,1)S(1)}, bf16[8,54,128]{2,0,1:T(8,128)(2,1)S(1)}, u32[]{:S(2)}, u32[]{:S(2)}) collective-permute-start(bf16[8,54,128]{2,0,1:T(8,128)(2,1)S(1)} %dynamic-slice_bitcast_fusion.3), channel_id=1, source_target_pairs={{0,16},{16,0},{1,17},{17,1},{2,18},{18,2},{3,19},{19,3},{4,20},{20... | collective-permute-start | bytes 331784 | tf_op jit(solution)/shard_map/ppermute | solution.py:428
  49.4 0.1 collective-permute-start.4
  49.5 3.4 %collective-permute-done.8 = bf16[8,54,128]{2,0,1:T(8,128)(2,1)S(1)} collective-permute-done((bf16[8,54,128]{2,0,1:T(8,128)(2,1)S(1)}, bf16[8,54,128]{2,0,1:T(8,128)(2,1)S(1)}, u32[]{:S(2)}, u32[]{:S(2)}) %collective-permute-start.8) | collective-permute-done | bytes 110624 | tf_op jit(solution)/shard_map/ppermute | solution.py:428
  53.0 0.2 constant_dynamic-slice_fusion.1
  53.3 1.6 %collective-permute-start.9 = (bf16[4,54,128]{2,1,0:T(8,128)(2,1)S(1)}, bf16[4,54,128]{2,1,0:T(8,128)(2,1)S(1)}, u32[]{:S(2)}, u32[]{:S(2)}) collective-permute-start(bf16[4,54,128]{2,1,0:T(8,128)(2,1)S(1)} %bitcast.99), channel_id=1, source_target_pairs={{0,2},{1,3},{2,0},{3,1},{4,6},{5,7},{6,4},{7,5},{8,10},{9,11},{10,... | collective-permute-start | bytes 165896 | tf_op jit(solution)/shard_map/ppermute | solution.py:428
  54.9 0.0 collective-permute-done.4
  54.9 0.1 fusion
  55.0 0.6 collective-permute-start.5
  55.6 2.5 %collective-permute-done.9 = bf16[4,54,128]{2,1,0:T(8,128)(2,1)S(1)} collective-permute-done((bf16[4,54,128]{2,1,0:T(8,128)(2,1)S(1)}, bf16[4,54,128]{2,1,0:T(8,128)(2,1)S(1)}, u32[]{:S(2)}, u32[]{:S(2)}) %collective-permute-start.9) | collective-permute-done | bytes 55328 | tf_op jit(solution)/shard_map/ppermute | solution.py:428
  58.1 3.9 %collective-permute-done.5 = bf16[4,216,128]{2,1,0:T(8,128)(2,1)S(1)} collective-permute-done((bf16[4,216,128]{2,1,0:T(8,128)(2,1)S(1)}, bf16[4,216,128]{2,1,0:T(8,128)(2,1)S(1)}, u32[]{:S(2)}, u32[]{:S(2)}) %collective-permute-start.5) | collective-permute-done | bytes 221216 | tf_op jit(solution)/shard_map/ppermute | solution.py:428
  62.0 0.1 fusion.2
  62.2 0.1 collective-permute-start.10
  62.3 4.9 %collective-permute-done.10 = bf16[2,270,128]{2,1,0:T(8,128)(2,1)S(1)} collective-permute-done((bf16[2,270,128]{2,1,0:T(8,128)(2,1)S(1)}, bf16[2,270,128]{2,1,0:T(8,128)(2,1)S(1)}, u32[]{:S(2)}, u32[]{:S(2)}) %collective-permute-start.10) | collective-permute-done | bytes 138272 | tf_op jit(solution)/shard_map/ppermute | solution.py:428
  67.3 0.1 collective-permute-start.11
  67.4 0.7 slice_bitcast_fusion.1
  68.1 4.7 %collective-permute-done.11 = bf16[270,128]{1,0:T(8,128)(2,1)S(1)} collective-permute-done((bf16[270,128]{1,0:T(8,128)(2,1)S(1)}, bf16[270,128]{1,0:T(8,128)(2,1)S(1)}, u32[]{:S(2)}, u32[]{:S(2)}) %collective-permute-start.11) | collective-permute-done | bytes 69152 | tf_op jit(solution)/shard_map/ppermute | solution.py:428
  72.8 0.1 slice_bitcast_fusion.3
  72.9 0.7 slice_bitcast_fusion
  73.6 0.7 copy.30
  (37 shorter events, 0.7 us)
Async XLA Ops:
  0.6 0.8 %copy-start.1 = (s32[8,8,16]{2,1,0:T(8,128)S(1)}, s32[8,8,16]{2,1,0:T(8,128)}, u32[]{:S(2)}) copy-start(s32[8,8,16]{2,1,0:T(8,128)} %grain_ids.1) | copy-start | bytes 12292
  1.4 0.9 %copy-start = (bf16[7,8,8,16]{3,2,1,0:T(8,128)(2,1)S(1)}, bf16[7,8,8,16]{3,2,1,0:T(8,128)(2,1)}, u32[]{:S(2)}) copy-start(bf16[7,8,8,16]{3,2,1,0:T(8,128)(2,1)} %fields.1) | copy-start | bytes 43012
  7.8 5.8 %collective-permute-start.1 = (bf16[144,128]{1,0:T(8,128)(2,1)S(1)}, bf16[144,128]{1,0:T(8,128)(2,1)S(1)}, u32[]{:S(2)}, u32[]{:S(2)}) collective-permute-start(bf16[144,128]{1,0:T(8,128)(2,1)S(1)} %pad_maximum_fusion.5), channel_id=1, source_target_pairs={{0,12},{4,0},{8,4},{12,8},{1,13},{5,1},{9,5},{13,9},{2,14},{6,2},{... | collective-permute-start | bytes 110600 | tf_op jit(solution)/shard_map/ppermute | solution.py:385
  12.1 5.9 %collective-permute-start = (bf16[160,128]{1,0:T(8,128)(2,1)S(1)}, bf16[160,128]{1,0:T(8,128)(2,1)S(1)}, u32[]{:S(2)}, u32[]{:S(2)}) collective-permute-start(bf16[160,128]{1,0:T(8,128)(2,1)S(1)} %pad_maximum_fusion.4), channel_id=1, source_target_pairs={{0,4},{4,8},{8,12},{12,0},{1,5},{5,9},{9,13},{13,1},{2,6},{6,10},{... | collective-permute-start | bytes 122888 | tf_op jit(solution)/shard_map/ppermute | solution.py:384
  13.7 10.0 %copy-start.2 = (bf16[128,3456]{1,0:T(8,128)(2,1)S(1)}, bf16[128,3456]{1,0:T(8,128)(2,1)}, u32[]{:S(2)}) copy-start(bf16[128,3456]{1,0:T(8,128)(2,1)} %refs_9_.1) | copy-start | bytes 2654212
  18.1 0.8 %copy-start.9 = (bf16[128,8,4,8]{0,3,2,1:T(8,128)(2,1)S(1)}, bf16[128,8,4,8]{0,3,2,1:T(8,128)(2,1)}, u32[]{:S(2)}) copy-start(bf16[128,8,4,8]{0,3,2,1:T(8,128)(2,1)} %param.15) | copy-start | bytes 196612
  18.1 5.5 %copy-start.3 = (bf16[128,1728]{0,1:T(8,128)(2,1)S(1)}, bf16[128,1728]{0,1:T(8,128)(2,1)}, u32[]{:S(2)}) copy-start(bf16[128,1728]{0,1:T(8,128)(2,1)} %param.13) | copy-start | bytes 1327108
  19.1 4.6 %copy-start.4 = (bf16[64,1728]{1,0:T(8,128)(2,1)S(1)}, bf16[64,1728]{1,0:T(8,128)(2,1)}, u32[]{:S(2)}) copy-start(bf16[64,1728]{1,0:T(8,128)(2,1)} %refs_7_.1) | copy-start | bytes 663556
  19.2 4.5 %copy-start.5 = (bf16[128,64]{0,1:T(8,128)(2,1)S(1)}, bf16[128,64]{0,1:T(8,128)(2,1)}, u32[]{:S(2)}) copy-start(bf16[128,64]{0,1:T(8,128)(2,1)} %param.10) | copy-start | bytes 49156
  19.2 1.8 %collective-permute-start.2 = (bf16[352,128]{1,0:T(8,128)(2,1)S(1)}, bf16[352,128]{1,0:T(8,128)(2,1)S(1)}, u32[]{:S(2)}, u32[]{:S(2)}) collective-permute-start(bf16[352,128]{1,0:T(8,128)(2,1)S(1)} %get-tuple-element.32), channel_id=1, source_target_pairs={{0,1},{1,0},{2,3},{3,2},{4,5},{5,4},{6,7},{7,6},{8,9},{9,8},{10,11... | collective-permute-start | bytes 270344 | tf_op jit(solution)/shard_map/ppermute | solution.py:395
  19.3 4.4 %collective-permute-start.3 = (bf16[352,128]{1,0:T(8,128)(2,1)S(1)}, bf16[352,128]{1,0:T(8,128)(2,1)S(1)}, u32[]{:S(2)}, u32[]{:S(2)}) collective-permute-start(bf16[352,128]{1,0:T(8,128)(2,1)S(1)} %get-tuple-element.31), channel_id=1, source_target_pairs={{0,3},{1,2},{2,1},{3,0},{4,7},{5,6},{6,5},{7,4},{8,11},{9,10},{10,... | collective-permute-start | bytes 270344 | tf_op jit(solution)/shard_map/ppermute | solution.py:398
  23.6 0.7 copy-start.6
  38.7 0.7 copy-start.7
  39.4 4.4 %collective-permute-start.6 = (bf16[128,256]{1,0:T(8,128)(2,1)S(1)}, bf16[128,256]{1,0:T(8,128)(2,1)S(1)}, u32[]{:S(2)}, u32[]{:S(2)}) collective-permute-start(bf16[128,256]{1,0:T(8,128)(2,1)S(1)} %bitcast.86), channel_id=1, source_target_pairs={{0,16},{16,0},{1,17},{17,1},{2,18},{18,2},{3,19},{19,3},{4,20},{20... | collective-permute-start | bytes 196616 | tf_op jit(solution)/shard_map/ppermute | solution.py:540
  43.8 0.9 %copy-start.8 = (f32[128,256]{1,0:T(8,128)S(1)}, f32[128,256]{1,0:T(8,128)}, u32[]{:S(2)}) copy-start(f32[128,256]{1,0:T(8,128)} %copy-done.7) | copy-start | bytes 393220
  46.2 1.5 %collective-permute-start.7 = (bf16[8,2,54,128]{3,0,2,1:T(8,128)(2,1)S(1)}, bf16[8,2,54,128]{3,0,2,1:T(8,128)(2,1)S(1)}, u32[]{:S(2)}, u32[]{:S(2)}) collective-permute-start(bf16[8,2,54,128]{3,0,2,1:T(8,128)(2,1)S(1)} %bitcast.96), channel_id=1, source_target_pairs={{0,1},{1,0},{2,3},{3,2},{4,5},{5,4},{6,7},{7,6},{8,9},{9,8},{10,11... | collective-permute-start | bytes 663560 | tf_op jit(solution)/shard_map/ppermute | solution.py:428
  47.8 5.2 %collective-permute-start.8 = (bf16[8,54,128]{2,0,1:T(8,128)(2,1)S(1)}, bf16[8,54,128]{2,0,1:T(8,128)(2,1)S(1)}, u32[]{:S(2)}, u32[]{:S(2)}) collective-permute-start(bf16[8,54,128]{2,0,1:T(8,128)(2,1)S(1)} %dynamic-slice_bitcast_fusion.3), channel_id=1, source_target_pairs={{0,16},{16,0},{1,17},{17,1},{2,18},{18,2},{3,19},{19,3},{4,20},{20... | collective-permute-start | bytes 331784 | tf_op jit(solution)/shard_map/ppermute | solution.py:428
  49.4 5.5 %collective-permute-start.4 = (bf16[8,216,128]{2,1,0:T(8,128)(2,1)S(1)}, bf16[8,216,128]{2,1,0:T(8,128)(2,1)S(1)}, u32[]{:S(2)}, u32[]{:S(2)}) collective-permute-start(bf16[8,216,128]{2,1,0:T(8,128)(2,1)S(1)} %dynamic-slice_bitcast_fusion), channel_id=1, source_target_pairs={{0,1},{1,0},{2,3},{3,2},{4,5},{5,4},{6,7},{7,6},{8,9},{9,8},{10,11... | collective-permute-start | bytes 1327112 | tf_op jit(solution)/shard_map/ppermute | solution.py:428
  53.3 4.9 %collective-permute-start.9 = (bf16[4,54,128]{2,1,0:T(8,128)(2,1)S(1)}, bf16[4,54,128]{2,1,0:T(8,128)(2,1)S(1)}, u32[]{:S(2)}, u32[]{:S(2)}) collective-permute-start(bf16[4,54,128]{2,1,0:T(8,128)(2,1)S(1)} %bitcast.99), channel_id=1, source_target_pairs={{0,2},{1,3},{2,0},{3,1},{4,6},{5,7},{6,4},{7,5},{8,10},{9,11},{10,... | collective-permute-start | bytes 165896 | tf_op jit(solution)/shard_map/ppermute | solution.py:428
  55.0 7.0 %collective-permute-start.5 = (bf16[4,216,128]{2,1,0:T(8,128)(2,1)S(1)}, bf16[4,216,128]{2,1,0:T(8,128)(2,1)S(1)}, u32[]{:S(2)}, u32[]{:S(2)}) collective-permute-start(bf16[4,216,128]{2,1,0:T(8,128)(2,1)S(1)} %dynamic-slice_bitcast_fusion.1), channel_id=1, source_target_pairs={{0,2},{1,3},{2,0},{3,1},{4,6},{5,7},{6,4},{7,5},{8,10},{9,11},{10,... | collective-permute-start | bytes 663560 | tf_op jit(solution)/shard_map/ppermute | solution.py:428
  62.2 5.1 %collective-permute-start.10 = (bf16[2,270,128]{2,1,0:T(8,128)(2,1)S(1)}, bf16[2,270,128]{2,1,0:T(8,128)(2,1)S(1)}, u32[]{:S(2)}, u32[]{:S(2)}) collective-permute-start(bf16[2,270,128]{2,1,0:T(8,128)(2,1)S(1)} %dynamic-slice_bitcast_fusion.2), channel_id=1, source_target_pairs={{0,4},{1,5},{2,6},{3,7},{4,0},{5,1},{6,2},{7,3},{8,12},{9,13},{10,... | collective-permute-start | bytes 414728 | tf_op jit(solution)/shard_map/ppermute | solution.py:428
  67.3 5.5 %collective-permute-start.11 = (bf16[270,128]{1,0:T(8,128)(2,1)S(1)}, bf16[270,128]{1,0:T(8,128)(2,1)S(1)}, u32[]{:S(2)}, u32[]{:S(2)}) collective-permute-start(bf16[270,128]{1,0:T(8,128)(2,1)S(1)} %dynamic-slice_bitcast_fusion.4), channel_id=1, source_target_pairs={{0,8},{1,9},{2,10},{3,11},{4,12},{5,13},{6,14},{7,15},{8,0},{9,1},... | collective-permute-start | bytes 207368 | tf_op jit(solution)/shard_map/ppermute | solution.py:428

commit v4 on v3

--- a/solution.py
+++ b/solution.py
@@ -39,7 +39,7 @@
     return pltpu.roll(values, 1, 0)
 
 
-def pack_kernel(fields, grain_ids, out):
+def pack_kernel(fields, grain_ids, cotangent, out, cot_out):
     comps, bx, by, bz = fields.shape
     quad = comps + 1
     column = lax.broadcasted_iota(jnp.int32, (bz, bz * quad), 1)
@@ -50,6 +50,7 @@
         spread = jnp.where(column == row * quad + c, 1.0, 0.0).astype(BF16)
         total = total + jnp.dot(flat(plane).astype(BF16), spread, preferred_element_type=F32)
     out[...] = total.astype(BF16)
+    cot_out[...] = cotangent[...]
 
 
 def widen_inputs(weight, table, weight_out, table_out):
@@ -80,15 +81,15 @@
 
 
 def forward_kernel(
-    place, feat, near, far, cot, weight, table, kernel_fine, kernel_down, kernel_bottle,
+    place, feat, near, far, cot, wide_weight, wide_table, kernel_fine, kernel_down, kernel_bottle,
     bottle_out, mine_out, others_out, grad_out, slope_out, kept_out,
     emb, fine, coarse, grads, pre, fine_mask, coarse_mask, wide_feat, cot_rows, cotangent,
-    wide_weight, wide_table, band_fine, band_down, *, dims,
+    band_fine, band_down, *, dims,
 ):
     nx, by, bz, c1, c2, outs, grains, limits = dims
     total_y, total_z = limits
     ny_emb, ny_fine, ny_mid, ny_bot, ny_own = by + 11, by + 9, by // 2 + 4, by // 2 + 2, by // 2
-    quad = weight.shape[0] + 1
+    quad = wide_weight.shape[0] // 4
     nq = fine.shape[4]
     coarse_x = nx // 2
     own_x = slope_out.shape[0] // (ny_own * nq)
@@ -97,7 +98,6 @@
     half = lanes // 2
     half_z = bz // 2
 
-    widen_inputs(weight, table, wide_weight, wide_table)
 
     emb_rows = nx * ny_emb
     has_before = place[1] > 0
@@ -379,6 +379,15 @@
         grad_out[k, 1] = jnp.where(low, pltpu.roll(first, c2 // 2, 1), second).astype(BF16)
 
 
+def finish_kernel(index, joined, got, bottle_out, down_out):
+    cut = bottle_out.shape[0]
+    width = down_out.shape[0]
+    total = joined[index[0]].astype(F32) + got[...].astype(F32)
+    bottle_out[...] = total[:cut]
+    turned = jnp.transpose(total[cut:], (1, 0))
+    down_out[...] = jnp.concatenate([turned[:width], turned[width:]], axis=1)
+
+
 def halo(forward, backward, axis):
     count = lax.axis_size(axis)
     before = lax.ppermute(forward, axis, [(i, (i + 1) % count) for i in range(count)])
@@ -392,9 +401,7 @@
     if count % 2:
         before, after = halo(forward, backward, axis)
         return jnp.where(odd, before, after), jnp.where(odd, after, before)
-    near = lax.ppermute(
-        jnp.where(odd, backward, forward), axis, [(i, i ^ 1) for i in range(count)]
-    )
+    near = lax.ppermute(jnp.where(odd, backward, forward), axis, [(i, i ^ 1) for i in range(count)])
     far = lax.ppermute(
         jnp.where(odd, forward, backward),
         axis,
@@ -457,16 +464,20 @@
     quad = comps + 1
     half_y, half_z = by // 2, bz // 2
     vmem = pl.BlockSpec(memory_space=pltpu.VMEM)
-    feat = pl.pallas_call(
+    cot = jnp.transpose(cotangent, (1, 2, 3, 0))
+    feat, cot = pl.pallas_call(
         pack_kernel,
-        out_shape=jax.ShapeDtypeStruct((bx * by, bz * quad), BF16),
-        in_specs=[vmem] * 2,
-        out_specs=vmem,
+        out_shape=(
+            jax.ShapeDtypeStruct((bx * by, bz * quad), BF16),
+            jax.ShapeDtypeStruct((math.prod(cot.shape[:3]), outs), BF16),
+        ),
+        in_specs=[vmem] * 3,
+        out_specs=(vmem,) * 2,
         compiler_params=pltpu.CompilerParams(vmem_limit_bytes=4 << 20),
         name="pack",
-    )(fields, grain_ids)
+    )(fields, grain_ids, cot.reshape(-1, outs))
+    cot = cot.reshape(coarse_x, half_y, half_z, outs)
     feat = lax.all_gather(feat.reshape(bx, by, bz * quad), "gx", axis=0, tiled=True)
-    cot = jnp.transpose(cotangent, (1, 2, 3, 0))
 
     def packed(first, second):
         return jnp.concatenate([first.reshape(-1, 128), second.reshape(-1, 128)], axis=0)
@@ -486,6 +497,17 @@
     near, far = swap_halo(
         packed(feat, cot[:, :, half_z - 1 :]), packed(feat, cot[:, :, :1]), "gz"
     )
+    wide_weight, wide_table = pl.pallas_call(
+        widen_inputs,
+        out_shape=(
+            jax.ShapeDtypeStruct((4 * quad, 4 * c1), F32),
+            jax.ShapeDtypeStruct((4 * grains, 4 * c1), BF16),
+        ),
+        in_specs=[vmem] * 2,
+        out_specs=(vmem,) * 2,
+        compiler_params=pltpu.CompilerParams(vmem_limit_bytes=4 << 20),
+        name="widen",
+    )(input_weight.T, material_table.T)
     place = jnp.stack([lax.axis_index("gy"), lax.axis_index("gz"), lax.axis_index("gx")])
 
     ny_own, ny_mid, ny_bot = by // 2, by // 2 + 4, by // 2 + 2
@@ -519,8 +541,6 @@
             pltpu.VMEM((nx * (by + 11), 4 * nq * quad), F32),
             pltpu.VMEM((outs // LANES, coarse_x * ny_bot * bz // 2, LANES), F32),
             pltpu.VMEM((2 * outs // LANES, coarse_x * ny_bot * nq, LANES), F32),
-            pltpu.VMEM((4 * quad, 4 * c1), F32),
-            pltpu.VMEM((4 * grains, 4 * c1), BF16),
             pltpu.VMEM((9 * lanes, 4 * c1), BF16),
             pltpu.VMEM((9 * 4 * c1, c2), BF16),
         ],
@@ -529,7 +549,7 @@
         name="forward",
     )(
         place, feat.reshape(-1, bz * quad), near, far, cot.reshape(-1, outs),
-        input_weight.T, material_table.T, kernel_fine, kernel_down.T, kernel_bottle,
+        wide_weight, wide_table, kernel_fine, kernel_down.T, kernel_bottle,
     )
 
     bottle = bottle_rows.reshape(coarse_x, ny_own, 2 * nq, outs)[:, :, 2 : 2 + bz // 2]
@@ -544,7 +564,7 @@
 
     chunks = gy * gz
     rows = 27 * c1 // chunks
-    paired = gx == 2 and rows % 2 == 0
+    paired = gx == 2 and rows % 2 == 0 and chunks % 8 == 0
     part_shape = (chunks, 2, rows // 2, c2) if paired else (27 * c1, c2)
     scale = 1.0 / math.sqrt(coarse_x * (total_y // 2) * (total_z // 2))
     down_part = pl.pallas_call(
@@ -569,11 +589,27 @@
         down_part = halve(down_part, both, 1).astype(BF16)
         down_part = halve(down_part, ("gx",), 1, 1).astype(BF16)
         down_part = halve(down_part, both, 2).astype(BF16)
-        summed = halve_all(jnp.concatenate([bottle_part, down_part], axis=1), both, 4)
+        joined = jnp.concatenate([bottle_part, down_part], axis=1)
         cut = bottle_part.shape[1]
-        grad_bottle = summed[:cut, :outs_true].T
-        halves = summed[cut:]
-        grad_down = jnp.concatenate([halves[:, : c2 // 2].T, halves[:, c2 // 2 :].T], axis=1)
+        bit = 4
+        while joined.shape[0] > 2:
+            joined = halve(joined, both, bit).astype(BF16)
+            bit *= 2
+        mine = (lax.axis_index(both) // bit) % 2
+        send = lax.dynamic_index_in_dim(joined, 1 - mine, 0, keepdims=False)
+        got = lax.ppermute(send, both, [(i, i ^ bit) for i in range(chunks)])
+        grad_bottle, grad_down = pl.pallas_call(
+            finish_kernel,
+            out_shape=(
+                jax.ShapeDtypeStruct((cut, outs), F32),
+                jax.ShapeDtypeStruct((c2 // 2, rows), F32),
+            ),
+            in_specs=[pl.BlockSpec(memory_space=pltpu.SMEM)] + [vmem] * 2,
+            out_specs=(vmem,) * 2,
+            compiler_params=pltpu.CompilerParams(vmem_limit_bytes=4 << 20),
+            name="finish",
+        )(mine.reshape(1), joined, got)
+        grad_bottle = grad_bottle[:, :outs_true].T
     else:
         grad_bottle = halve_all(bottle_part, both)[:, :outs_true].T
         down_part = jnp.transpose(down_part.reshape(27 * c1, gx, c2 // gx), (1, 0, 2))

time: 74.5 us -> 73.1 us (0.981)
  local copies, waits for them, and re-layouts: 7.6 us -> 6.18 us
  waiting for transfers between devices: 32.3 us -> 31.3 us
  Pallas kernels: 15.8 us -> 16.6 us
    ppermute x0 -> x1, waiting for transfers between devices: none -> 4.73 us  [window(): got = lax.ppermute(send, both, [(i, i ^ bit) for i in range(chunks)])]
    ppermute x7 -> x6, waiting for transfers between devices: 21 us -> 16.2 us  [halve(): got = lax.ppermute(send, axes, [(i, i ^ bit) for i in range(count)])]
    pallas_call x1 -> x3, Pallas kernels: 0.14 us -> 1.11 us  [the longest x1 0.8 us: window(): pl.pallas_call(finish_kernel, out_shape=(jax.ShapeDtypeStruct((cut, outs)...]
    ppermute x1, waiting for transfers between devices: 1.5 us -> 0.58 us  [halo(): lax.ppermute(backward, axis, [(i, (i - 1) % count) for i in range(count)])]
    ppermute x7 -> x6, starting transfers between devices: 3.99 us -> 3.92 us  [halve(): got = lax.ppermute(send, axes, [(i, i ^ bit) for i in range(count)])]
    unnamed x23 -> x22, local copies, waits for them, and re-layouts: 4.65 us -> 4.68 us
where the time goes in v4:
time: 73.1 us; the launch traced here: 72.7 us
  waiting for transfers between devices  31.3 us (43%)
  Pallas kernels  16.6 us (23%)
  starting transfers between devices  11.4 us (16%)
  local copies, waits for them, and re-layouts  6.18 us (8%)
  blocking collectives  5.33 us (7%)
  between operations  1.23 us (2%)
    ppermute x6, waiting for transfers between devices, halve(): got = lax.ppermute(send, axes, [(i, i ^ bit) for i in range(count)])  16.2 us
    pallas_call x1, Pallas kernels, window(): pl.pallas_call(lambda *refs: forward_kernel(*refs, dims=(nx, by, bz, c1,...  14.2 us
    all_gather x1, blocking collectives, window(): lax.all_gather(feat.reshape(bx, by, bz * quad), 'gx', axis=0, tiled=True)  5.33 us
    ppermute x1, waiting for transfers between devices, window(): got = lax.ppermute(send, both, [(i, i ^ bit) for i in range(chunks)])  4.73 us
    unnamed x22, local copies, waits for them, and re-layouts  4.68 us
    ppermute x1, starting transfers between devices, halo(): lax.ppermute(backward, axis, [(i, (i - 1) % count) for i in range(count)])  4.2 us
    ppermute x1, waiting for transfers between devices, halo(): lax.ppermute(forward, axis, [(i, (i + 1) % count) for i in range(count)])  4.18 us
    ppermute x6, starting transfers between devices, halve(): got = lax.ppermute(send, axes, [(i, i ^ bit) for i in range(count)])  3.92 us
  transfers between devices with their start and end apart: 12, of which 10 were waited for; matrix products, arithmetic and copies ran while one was open for 2% of the time, Pallas kernels for 0%

profile of v4, /device:TPU:0, one launch (start us, length us, event | category | flops | bytes accessed | tf_op | source)
XLA Modules:
  0.0 72.7 jit_solution(6655568938489055625)
XLA Ops:
  0.6 0.0 copy-start
  0.6 0.9 %copy-done = bf16[7,8,8,16]{3,2,1,0:T(8,128)(2,1)S(1)} copy-done((bf16[7,8,8,16]{3,2,1,0:T(8,128)(2,1)S(1)}, bf16[7,8,8,16]{3,2,1,0:T(8,128)(2,1)}, u32[]{:S(2)}) %copy-start) | copy-done | bytes 14360
  1.5 0.0 copy-start.1
  1.5 0.8 %copy-done.1 = bf16[128,8,4,8]{0,3,2,1:T(8,128)(2,1)S(1)} copy-done((bf16[128,8,4,8]{0,3,2,1:T(8,128)(2,1)S(1)}, bf16[128,8,4,8]{0,3,2,1:T(8,128)(2,1)}, u32[]{:S(2)}) %copy-start.1) | copy-done | bytes 65560
  2.4 0.0 copy-start.2
  2.4 0.8 %copy-done.2 = s32[8,8,16]{2,1,0:T(8,128)S(1)} copy-done((s32[8,8,16]{2,1,0:T(8,128)S(1)}, s32[8,8,16]{2,1,0:T(8,128)}, u32[]{:S(2)}) %copy-start.2) | copy-done | bytes 4120
  3.1 0.1 pack.1
  3.3 5.3 %all_gather.3 = bf16[16,8,128]{2,1,0:T(8,128)(2,1)S(1)} all-gather(bf16[8,8,128]{2,1,0:T(8,128)(2,1)S(1)} %bitcast.85), channel_id=1, replica_groups=mesh['gx'=2,'gy'=4,'gz'=4] {'gx'}, dimensions={0}, use_global_device_ids=true | all-gather | bytes 49152 | tf_op jit(solution)/shard_map/all_gather | solution.py:480
  8.7 4.2 %collective-permute-start.1 = (bf16[144,128]{1,0:T(8,128)(2,1)S(1)}, bf16[144,128]{1,0:T(8,128)(2,1)S(1)}, u32[]{:S(2)}, u32[]{:S(2)}) collective-permute-start(bf16[144,128]{1,0:T(8,128)(2,1)S(1)} %pad_maximum_fusion.4), channel_id=1, source_target_pairs={{0,12},{4,0},{8,4},{12,8},{1,13},{5,1},{9,5},{13,9},{2,14},{6,2},{... | collective-permute-start | bytes 110600 | tf_op jit(solution)/shard_map/ppermute | solution.py:394
  12.9 0.1 collective-permute-start
  13.0 0.0 copy-start.3
  13.1 0.0 copy-start.4
  13.1 0.7 copy-done.3
  13.8 0.0 copy-done.4
  13.8 0.2 widen.1
  13.9 0.6 collective-permute-done.1
  14.6 4.2 %collective-permute-done = bf16[160,128]{1,0:T(8,128)(2,1)S(1)} collective-permute-done((bf16[160,128]{1,0:T(8,128)(2,1)S(1)}, bf16[160,128]{1,0:T(8,128)(2,1)S(1)}, u32[]{:S(2)}, u32[]{:S(2)}) %collective-permute-start) | collective-permute-done | bytes 40992 | tf_op jit(solution)/shard_map/ppermute | solution.py:393
  18.8 0.0 copy-start.5
  19.0 0.1 pad_maximum_fusion.1
  19.1 0.0 copy-start.6
  19.2 0.0 copy-start.7
  19.3 0.1 collective-permute-start.2
  19.3 1.6 %collective-permute-start.3 = (bf16[352,128]{1,0:T(8,128)(2,1)S(1)}, bf16[352,128]{1,0:T(8,128)(2,1)S(1)}, u32[]{:S(2)}, u32[]{:S(2)}) collective-permute-start(bf16[352,128]{1,0:T(8,128)(2,1)S(1)} %get-tuple-element.29), channel_id=1, source_target_pairs={{0,3},{1,2},{2,1},{3,0},{4,7},{5,6},{6,5},{7,4},{8,11},{9,10},{10,... | collective-permute-start | bytes 270344 | tf_op jit(solution)/shard_map/ppermute | solution.py:405
  21.0 0.1 pad_add_fusion.refs_0_
  21.0 0.1 copy.29
  21.1 0.0 collective-permute-done.2.refs_2_
  21.1 2.6 %collective-permute-done.3.refs_3_ = bf16[352,128]{1,0:T(8,128)(2,1)S(1)} collective-permute-done((bf16[352,128]{1,0:T(8,128)(2,1)S(1)}, bf16[352,128]{1,0:T(8,128)(2,1)S(1)}, u32[]{:S(2)}, u32[]{:S(2)}) %collective-permute-start.3) | collective-permute-done | bytes 90144 | tf_op jit(solution)/shard_map/ppermute | solution.py:405
  23.7 0.0 copy-done.5
  23.7 0.0 copy-done.6
  23.7 0.0 copy-done.7
  23.7 14.2 %forward.1 = (bf16[256,256]{1,0:T(8,128)(2,1)S(1)}, bf16[128,256]{1,0:T(8,128)(2,1)S(1)}, bf16[1,128,256]{2,1,0:T(8,128)(2,1)S(1)}, bf16[3456,128]{1,0:T(8,128)(...) custom-call(s32[3]{0:T(128)S(1)} %pad_add_fusion.refs_0_, bf16[304,128]{1,0:T(8,128)(2,1)S(1)} %reshape.92.refs_1_, ...), custom_call_target="tpu_custom_call" | custom-call | flops 10000000000 | bytes 10000000 | tf_op jit(solution)/shard_map/forward/pallas_call | solution.py:519
  38.0 0.0 copy-start.8
  38.0 0.6 copy-done.8
  38.6 1.5 %collective-permute-start.6 = (bf16[128,256]{1,0:T(8,128)(2,1)S(1)}, bf16[128,256]{1,0:T(8,128)(2,1)S(1)}, u32[]{:S(2)}, u32[]{:S(2)}) collective-permute-start(bf16[128,256]{1,0:T(8,128)(2,1)S(1)} %bitcast.89), channel_id=1, source_target_pairs={{0,16},{16,0},{1,17},{17,1},{2,18},{18,2},{3,19},{19,3},{4,20},{20... | collective-permute-start | bytes 196616 | tf_op jit(solution)/shard_map/ppermute | solution.py:560
  40.1 2.9 %collective-permute-done.6 = bf16[128,256]{1,0:T(8,128)(2,1)S(1)} collective-permute-done((bf16[128,256]{1,0:T(8,128)(2,1)S(1)}, bf16[128,256]{1,0:T(8,128)(2,1)S(1)}, u32[]{:S(2)}, u32[]{:S(2)}) %collective-permute-start.6) | collective-permute-done | bytes 65568 | tf_op jit(solution)/shard_map/ppermute | solution.py:560
  43.0 0.0 copy-start.9
  43.0 0.8 %copy-done.9 = bf16[128,256]{1,0:T(8,128)(2,1)S(1)} copy-done((bf16[128,256]{1,0:T(8,128)(2,1)S(1)}, bf16[128,256]{1,0:T(8,128)(2,1)}, u32[]{:S(2)}) %copy-start.9) | copy-done | bytes 65560
  43.9 1.3 %down_gradient.1 = bf16[16,2,54,128]{3,2,1,0:T(8,128)(2,1)S(1)} custom-call(bf16[128,256]{1,0:T(8,128)(2,1)S(1)} %copy-done.9, bf16[1,128,256]{2,1,0:T(8,128)(2,1)S(1)} %bitcast.90, f32[128,256]{1,0:T(8,128)S(1)} %get-tuple-element.23.refs_2_, bf16[800,384]{1,0:T(8,128)(2,1)S(1)} %get-tuple-element.24.refs_3_), custom_call_target="tpu_custom_call" | custom-call | flops 2000000000 | bytes 1000000 | tf_op jit(solution)/shard_map/down_gradient/pallas_call | solution.py:570
  45.2 0.1 copy.48
  45.3 0.1 collective-permute-start.7
  45.4 1.4 %collective-permute-done.7 = bf16[8,2,54,128]{3,0,2,1:T(8,128)(2,1)S(1)} collective-permute-done((bf16[8,2,54,128]{3,0,2,1:T(8,128)(2,1)S(1)}, bf16[8,2,54,128]{3,0,2,1:T(8,128)(2,1)S(1)}, u32[]{:S(2)}, u32[]{:S(2)}) %collective-permute-start.7) | collective-permute-done | bytes 221216 | tf_op jit(solution)/shard_map/ppermute | solution.py:435
  46.8 0.1 fusion.1
  46.9 1.6 %collective-permute-start.8 = (bf16[8,54,128]{2,0,1:T(8,128)(2,1)S(1)}, bf16[8,54,128]{2,0,1:T(8,128)(2,1)S(1)}, u32[]{:S(2)}, u32[]{:S(2)}) collective-permute-start(bf16[8,54,128]{2,0,1:T(8,128)(2,1)S(1)} %dynamic-slice_bitcast_fusion.3), channel_id=1, source_target_pairs={{0,16},{16,0},{1,17},{17,1},{2,18},{18,2},{3,19},{19,3},{4,20},{20... | collective-permute-start | bytes 331784 | tf_op jit(solution)/shard_map/ppermute | solution.py:435
  48.5 0.1 collective-permute-start.4
  48.7 3.4 %collective-permute-done.8 = bf16[8,54,128]{2,0,1:T(8,128)(2,1)S(1)} collective-permute-done((bf16[8,54,128]{2,0,1:T(8,128)(2,1)S(1)}, bf16[8,54,128]{2,0,1:T(8,128)(2,1)S(1)}, u32[]{:S(2)}, u32[]{:S(2)}) %collective-permute-start.8) | collective-permute-done | bytes 110624 | tf_op jit(solution)/shard_map/ppermute | solution.py:435
  52.1 0.2 constant_dynamic-slice_fusion.1
  52.4 1.6 %collective-permute-start.9 = (bf16[4,54,128]{2,1,0:T(8,128)(2,1)S(1)}, bf16[4,54,128]{2,1,0:T(8,128)(2,1)S(1)}, u32[]{:S(2)}, u32[]{:S(2)}) collective-permute-start(bf16[4,54,128]{2,1,0:T(8,128)(2,1)S(1)} %bitcast.98), channel_id=1, source_target_pairs={{0,2},{1,3},{2,0},{3,1},{4,6},{5,7},{6,4},{7,5},{8,10},{9,11},{10,... | collective-permute-start | bytes 165896 | tf_op jit(solution)/shard_map/ppermute | solution.py:435
  54.0 0.0 collective-permute-done.4
  54.0 0.1 fusion
  54.1 0.6 collective-permute-start.5
  54.7 2.5 %collective-permute-done.9 = bf16[4,54,128]{2,1,0:T(8,128)(2,1)S(1)} collective-permute-done((bf16[4,54,128]{2,1,0:T(8,128)(2,1)S(1)}, bf16[4,54,128]{2,1,0:T(8,128)(2,1)S(1)}, u32[]{:S(2)}, u32[]{:S(2)}) %collective-permute-start.9) | collective-permute-done | bytes 55328 | tf_op jit(solution)/shard_map/ppermute | solution.py:435
  57.3 3.9 %collective-permute-done.5 = bf16[4,216,128]{2,1,0:T(8,128)(2,1)S(1)} collective-permute-done((bf16[4,216,128]{2,1,0:T(8,128)(2,1)S(1)}, bf16[4,216,128]{2,1,0:T(8,128)(2,1)S(1)}, u32[]{:S(2)}, u32[]{:S(2)}) %collective-permute-start.5) | collective-permute-done | bytes 221216 | tf_op jit(solution)/shard_map/ppermute | solution.py:435
  61.2 0.1 fusion.2
  61.3 0.1 collective-permute-start.10
  61.5 4.9 %collective-permute-done.10 = bf16[2,270,128]{2,1,0:T(8,128)(2,1)S(1)} collective-permute-done((bf16[2,270,128]{2,1,0:T(8,128)(2,1)S(1)}, bf16[2,270,128]{2,1,0:T(8,128)(2,1)S(1)}, u32[]{:S(2)}, u32[]{:S(2)}) %collective-permute-start.10) | collective-permute-done | bytes 138272 | tf_op jit(solution)/shard_map/ppermute | solution.py:435
  66.5 0.1 collective-permute-start.11
  66.5 0.7 slice_bitcast_fusion
  67.2 4.7 %collective-permute-done.11.got = bf16[270,128]{1,0:T(8,128)(2,1)S(1)} collective-permute-done((bf16[270,128]{1,0:T(8,128)(2,1)S(1)}, bf16[270,128]{1,0:T(8,128)(2,1)S(1)}, u32[]{:S(2)}, u32[]{:S(2)}) %collective-permute-start.11) | collective-permute-done | bytes 69152 | tf_op jit(solution)/shard_map/ppermute | solution.py:600
  71.9 0.8 %finish.1 = (f32[216,128]{1,0:T(8,128)}, f32[64,108]{1,0:T(8,128)}) custom-call(s32[1]{0:T(128)} %bitcast.16.index, bf16[2,270,128]{2,1,0:T(8,128)(2,1)S(1)} %fusion.3.joined, bf16[270,128]{1,0:T(8,128)(2,1)S(1)} %collective-permute-done.11.got), custom_call_target="tpu_custom_call" | custom-call | tf_op jit(solution)/shard_map/finish/pallas_call | solution.py:601
  (39 shorter events, 0.7 us)
Async XLA Ops:
  0.6 0.9 %copy-start = (bf16[7,8,8,16]{3,2,1,0:T(8,128)(2,1)S(1)}, bf16[7,8,8,16]{3,2,1,0:T(8,128)(2,1)}, u32[]{:S(2)}) copy-start(bf16[7,8,8,16]{3,2,1,0:T(8,128)(2,1)} %fields.1) | copy-start | bytes 43012
  1.5 0.8 %copy-start.1 = (bf16[128,8,4,8]{0,3,2,1:T(8,128)(2,1)S(1)}, bf16[128,8,4,8]{0,3,2,1:T(8,128)(2,1)}, u32[]{:S(2)}) copy-start(bf16[128,8,4,8]{0,3,2,1:T(8,128)(2,1)} %param.15) | copy-start | bytes 196612
  2.4 0.8 %copy-start.2 = (s32[8,8,16]{2,1,0:T(8,128)S(1)}, s32[8,8,16]{2,1,0:T(8,128)}, u32[]{:S(2)}) copy-start(s32[8,8,16]{2,1,0:T(8,128)} %grain_ids.1) | copy-start | bytes 12292
  8.7 5.8 %collective-permute-start.1 = (bf16[144,128]{1,0:T(8,128)(2,1)S(1)}, bf16[144,128]{1,0:T(8,128)(2,1)S(1)}, u32[]{:S(2)}, u32[]{:S(2)}) collective-permute-start(bf16[144,128]{1,0:T(8,128)(2,1)S(1)} %pad_maximum_fusion.4), channel_id=1, source_target_pairs={{0,12},{4,0},{8,4},{12,8},{1,13},{5,1},{9,5},{13,9},{2,14},{6,2},{... | collective-permute-start | bytes 110600 | tf_op jit(solution)/shard_map/ppermute | solution.py:394
  12.9 5.9 %collective-permute-start = (bf16[160,128]{1,0:T(8,128)(2,1)S(1)}, bf16[160,128]{1,0:T(8,128)(2,1)S(1)}, u32[]{:S(2)}, u32[]{:S(2)}) collective-permute-start(bf16[160,128]{1,0:T(8,128)(2,1)S(1)} %pad_maximum_fusion.3), channel_id=1, source_target_pairs={{0,4},{4,8},{8,12},{12,0},{1,5},{5,9},{9,13},{13,1},{2,6},{6,10},{... | collective-permute-start | bytes 122888 | tf_op jit(solution)/shard_map/ppermute | solution.py:393
  13.0 0.7 copy-start.3
  13.1 0.7 copy-start.4
  18.8 4.9 %copy-start.5 = (bf16[128,3456]{1,0:T(8,128)(2,1)S(1)}, bf16[128,3456]{1,0:T(8,128)(2,1)}, u32[]{:S(2)}) copy-start(bf16[128,3456]{1,0:T(8,128)(2,1)} %refs_9_.1) | copy-start | bytes 2654212
  19.1 4.6 %copy-start.6 = (bf16[128,1728]{0,1:T(8,128)(2,1)S(1)}, bf16[128,1728]{0,1:T(8,128)(2,1)}, u32[]{:S(2)}) copy-start(bf16[128,1728]{0,1:T(8,128)(2,1)} %param.13) | copy-start | bytes 1327108
  19.2 4.5 %copy-start.7 = (bf16[64,1728]{1,0:T(8,128)(2,1)S(1)}, bf16[64,1728]{1,0:T(8,128)(2,1)}, u32[]{:S(2)}) copy-start(bf16[64,1728]{1,0:T(8,128)(2,1)} %refs_7_.1) | copy-start | bytes 663556
  19.3 1.9 %collective-permute-start.2 = (bf16[352,128]{1,0:T(8,128)(2,1)S(1)}, bf16[352,128]{1,0:T(8,128)(2,1)S(1)}, u32[]{:S(2)}, u32[]{:S(2)}) collective-permute-start(bf16[352,128]{1,0:T(8,128)(2,1)S(1)} %get-tuple-element.30), channel_id=1, source_target_pairs={{0,1},{1,0},{2,3},{3,2},{4,5},{5,4},{6,7},{7,6},{8,9},{9,8},{10,11... | collective-permute-start | bytes 270344 | tf_op jit(solution)/shard_map/ppermute | solution.py:404
  19.3 4.4 %collective-permute-start.3 = (bf16[352,128]{1,0:T(8,128)(2,1)S(1)}, bf16[352,128]{1,0:T(8,128)(2,1)S(1)}, u32[]{:S(2)}, u32[]{:S(2)}) collective-permute-start(bf16[352,128]{1,0:T(8,128)(2,1)S(1)} %get-tuple-element.29), channel_id=1, source_target_pairs={{0,3},{1,2},{2,1},{3,0},{4,7},{5,6},{6,5},{7,4},{8,11},{9,10},{10,... | collective-permute-start | bytes 270344 | tf_op jit(solution)/shard_map/ppermute | solution.py:405
  38.0 0.6 copy-start.8
  38.6 4.4 %collective-permute-start.6 = (bf16[128,256]{1,0:T(8,128)(2,1)S(1)}, bf16[128,256]{1,0:T(8,128)(2,1)S(1)}, u32[]{:S(2)}, u32[]{:S(2)}) collective-permute-start(bf16[128,256]{1,0:T(8,128)(2,1)S(1)} %bitcast.89), channel_id=1, source_target_pairs={{0,16},{16,0},{1,17},{17,1},{2,18},{18,2},{3,19},{19,3},{4,20},{20... | collective-permute-start | bytes 196616 | tf_op jit(solution)/shard_map/ppermute | solution.py:560
  43.0 0.8 %copy-start.9 = (bf16[128,256]{1,0:T(8,128)(2,1)S(1)}, bf16[128,256]{1,0:T(8,128)(2,1)}, u32[]{:S(2)}) copy-start(bf16[128,256]{1,0:T(8,128)(2,1)} %copy-done.8) | copy-start | bytes 196612
  45.3 1.5 %collective-permute-start.7 = (bf16[8,2,54,128]{3,0,2,1:T(8,128)(2,1)S(1)}, bf16[8,2,54,128]{3,0,2,1:T(8,128)(2,1)S(1)}, u32[]{:S(2)}, u32[]{:S(2)}) collective-permute-start(bf16[8,2,54,128]{3,0,2,1:T(8,128)(2,1)S(1)} %bitcast.97), channel_id=1, source_target_pairs={{0,1},{1,0},{2,3},{3,2},{4,5},{5,4},{6,7},{7,6},{8,9},{9,8},{10,11... | collective-permute-start | bytes 663560 | tf_op jit(solution)/shard_map/ppermute | solution.py:435
  46.9 5.2 %collective-permute-start.8 = (bf16[8,54,128]{2,0,1:T(8,128)(2,1)S(1)}, bf16[8,54,128]{2,0,1:T(8,128)(2,1)S(1)}, u32[]{:S(2)}, u32[]{:S(2)}) collective-permute-start(bf16[8,54,128]{2,0,1:T(8,128)(2,1)S(1)} %dynamic-slice_bitcast_fusion.3), channel_id=1, source_target_pairs={{0,16},{16,0},{1,17},{17,1},{2,18},{18,2},{3,19},{19,3},{4,20},{20... | collective-permute-start | bytes 331784 | tf_op jit(solution)/shard_map/ppermute | solution.py:435
  48.5 5.5 %collective-permute-start.4 = (bf16[8,216,128]{2,1,0:T(8,128)(2,1)S(1)}, bf16[8,216,128]{2,1,0:T(8,128)(2,1)S(1)}, u32[]{:S(2)}, u32[]{:S(2)}) collective-permute-start(bf16[8,216,128]{2,1,0:T(8,128)(2,1)S(1)} %dynamic-slice_bitcast_fusion), channel_id=1, source_target_pairs={{0,1},{1,0},{2,3},{3,2},{4,5},{5,4},{6,7},{7,6},{8,9},{9,8},{10,11... | collective-permute-start | bytes 1327112 | tf_op jit(solution)/shard_map/ppermute | solution.py:435
  52.4 4.9 %collective-permute-start.9 = (bf16[4,54,128]{2,1,0:T(8,128)(2,1)S(1)}, bf16[4,54,128]{2,1,0:T(8,128)(2,1)S(1)}, u32[]{:S(2)}, u32[]{:S(2)}) collective-permute-start(bf16[4,54,128]{2,1,0:T(8,128)(2,1)S(1)} %bitcast.98), channel_id=1, source_target_pairs={{0,2},{1,3},{2,0},{3,1},{4,6},{5,7},{6,4},{7,5},{8,10},{9,11},{10,... | collective-permute-start | bytes 165896 | tf_op jit(solution)/shard_map/ppermute | solution.py:435
  54.1 7.0 %collective-permute-start.5 = (bf16[4,216,128]{2,1,0:T(8,128)(2,1)S(1)}, bf16[4,216,128]{2,1,0:T(8,128)(2,1)S(1)}, u32[]{:S(2)}, u32[]{:S(2)}) collective-permute-start(bf16[4,216,128]{2,1,0:T(8,128)(2,1)S(1)} %dynamic-slice_bitcast_fusion.1), channel_id=1, source_target_pairs={{0,2},{1,3},{2,0},{3,1},{4,6},{5,7},{6,4},{7,5},{8,10},{9,11},{10,... | collective-permute-start | bytes 663560 | tf_op jit(solution)/shard_map/ppermute | solution.py:435
  61.3 5.1 %collective-permute-start.10 = (bf16[2,270,128]{2,1,0:T(8,128)(2,1)S(1)}, bf16[2,270,128]{2,1,0:T(8,128)(2,1)S(1)}, u32[]{:S(2)}, u32[]{:S(2)}) collective-permute-start(bf16[2,270,128]{2,1,0:T(8,128)(2,1)S(1)} %dynamic-slice_bitcast_fusion.2), channel_id=1, source_target_pairs={{0,4},{1,5},{2,6},{3,7},{4,0},{5,1},{6,2},{7,3},{8,12},{9,13},{10,... | collective-permute-start | bytes 414728 | tf_op jit(solution)/shard_map/ppermute | solution.py:435
  66.5 5.5 %collective-permute-start.11 = (bf16[270,128]{1,0:T(8,128)(2,1)S(1)}, bf16[270,128]{1,0:T(8,128)(2,1)S(1)}, u32[]{:S(2)}, u32[]{:S(2)}) collective-permute-start(bf16[270,128]{1,0:T(8,128)(2,1)S(1)} %dynamic-slice_bitcast_fusion.4), channel_id=1, source_target_pairs={{0,8},{1,9},{2,10},{3,11},{4,12},{5,13},{6,14},{7,15},{8,0},{9,1},... | collective-permute-start | bytes 207368 | tf_op jit(solution)/shard_map/ppermute | solution.py:600

commit v5 on v4

--- a/solution.py
+++ b/solution.py
@@ -475,7 +475,12 @@
         out_specs=(vmem,) * 2,
         compiler_params=pltpu.CompilerParams(vmem_limit_bytes=4 << 20),
         name="pack",
-    )(fields, grain_ids, cot.reshape(-1, outs))
+    )(
+        *(
+            pltpu.with_memory_space_constraint(x, pltpu.HBM)
+            for x in (fields, grain_ids, cot.reshape(-1, outs))
+        )
+    )
     cot = cot.reshape(coarse_x, half_y, half_z, outs)
     feat = lax.all_gather(feat.reshape(bx, by, bz * quad), "gx", axis=0, tiled=True)
 

time: 73.1 us -> 71.4 us (0.977)
  local copies, waits for them, and re-layouts: 6.18 us -> 3.69 us
  Pallas kernels: 16.6 us -> 17.6 us
    unnamed x22 -> x16, local copies, waits for them, and re-layouts: 4.68 us -> 2.19 us
    pallas_call x1, Pallas kernels: 0.14 us -> 1.09 us  [window(): pl.pallas_call(pack_kernel, out_shape=(jax.ShapeDtypeStruct((bx * by, bz...]
where the time goes in v5:
time: 71.4 us; the launch traced here: 71.2 us
  waiting for transfers between devices  31.3 us (44%)
  Pallas kernels  17.6 us (25%)
  starting transfers between devices  11.4 us (16%)
  blocking collectives  5.33 us (7%)
  local copies, waits for them, and re-layouts  3.69 us (5%)
  between operations  1.2 us (2%)
    ppermute x6, waiting for transfers between devices, halve(): got = lax.ppermute(send, axes, [(i, i ^ bit) for i in range(count)])  16.2 us
    pallas_call x1, Pallas kernels, window(): pl.pallas_call(lambda *refs: forward_kernel(*refs, dims=(nx, by, bz, c1,...  14.2 us
    all_gather x1, blocking collectives, window(): lax.all_gather(feat.reshape(bx, by, bz * quad), 'gx', axis=0, tiled=True)  5.33 us
    ppermute x1, waiting for transfers between devices, window(): got = lax.ppermute(send, both, [(i, i ^ bit) for i in range(chunks)])  4.73 us
    ppermute x1, starting transfers between devices, halo(): lax.ppermute(backward, axis, [(i, (i - 1) % count) for i in range(count)])  4.2 us
    ppermute x1, waiting for transfers between devices, halo(): lax.ppermute(forward, axis, [(i, (i + 1) % count) for i in range(count)])  4.18 us
    ppermute x6, starting transfers between devices, halve(): got = lax.ppermute(send, axes, [(i, i ^ bit) for i in range(count)])  3.92 us
    ppermute x1, waiting for transfers between devices, window(): lax.ppermute(others[k - 1], 'gx', [(i, (i + k) % gx) for i in range(gx)])  2.95 us
  transfers between devices with their start and end apart: 12, of which 10 were waited for; matrix products, arithmetic and copies ran while one was open for 2% of the time, Pallas kernels for 0%

profile of v5, /device:TPU:0, one launch (start us, length us, event | category | flops | bytes accessed | tf_op | source)
XLA Modules:
  0.0 71.2 jit_solution(2423112974955998002)
XLA Ops:
  0.6 1.1 %pack.1 = (bf16[64,128]{1,0:T(8,128)(2,1)S(1)}, bf16[256,128]{1,0:T(8,128)(2,1)S(1)}) custom-call(bf16[7,8,8,16]{3,2,1,0:T(8,128)(2,1)} %fields.1, s32[8,8,16]{2,1,0:T(8,128)} %grain_ids.1, bf16[256,128]{1,0:T(8,128)(2,1)} %bitcast.97), custom_call_target="tpu_custom_call" | custom-call | tf_op jit(solution)/shard_map/pack/pallas_call | solution.py:468
  1.7 5.3 %all_gather.3 = bf16[16,8,128]{2,1,0:T(8,128)(2,1)S(1)} all-gather(bf16[8,8,128]{2,1,0:T(8,128)(2,1)S(1)} %bitcast.84), channel_id=1, replica_groups=mesh['gx'=2,'gy'=4,'gz'=4] {'gx'}, dimensions={0}, use_global_device_ids=true | all-gather | bytes 49152 | tf_op jit(solution)/shard_map/all_gather | solution.py:485
  7.1 4.2 %collective-permute-start.1 = (bf16[144,128]{1,0:T(8,128)(2,1)S(1)}, bf16[144,128]{1,0:T(8,128)(2,1)S(1)}, u32[]{:S(2)}, u32[]{:S(2)}) collective-permute-start(bf16[144,128]{1,0:T(8,128)(2,1)S(1)} %pad_maximum_fusion.4), channel_id=1, source_target_pairs={{0,12},{4,0},{8,4},{12,8},{1,13},{5,1},{9,5},{13,9},{2,14},{6,2},{... | collective-permute-start | bytes 110600 | tf_op jit(solution)/shard_map/ppermute | solution.py:394
  11.4 0.1 collective-permute-start
  11.5 0.0 copy-start
  11.5 0.0 copy-start.1
  11.5 0.7 copy-done
  12.2 0.0 copy-done.1
  12.2 0.2 widen.1
  12.4 0.6 collective-permute-done.1
  13.0 4.2 %collective-permute-done = bf16[160,128]{1,0:T(8,128)(2,1)S(1)} collective-permute-done((bf16[160,128]{1,0:T(8,128)(2,1)S(1)}, bf16[160,128]{1,0:T(8,128)(2,1)S(1)}, u32[]{:S(2)}, u32[]{:S(2)}) %collective-permute-start) | collective-permute-done | bytes 40992 | tf_op jit(solution)/shard_map/ppermute | solution.py:393
  17.3 0.0 copy-start.2
  17.4 0.1 pad_maximum_fusion.1
  17.6 0.0 copy-start.3
  17.7 0.0 copy-start.4
  17.7 0.1 collective-permute-start.2
  17.8 1.6 %collective-permute-start.3 = (bf16[352,128]{1,0:T(8,128)(2,1)S(1)}, bf16[352,128]{1,0:T(8,128)(2,1)S(1)}, u32[]{:S(2)}, u32[]{:S(2)}) collective-permute-start(bf16[352,128]{1,0:T(8,128)(2,1)S(1)} %get-tuple-element.29), channel_id=1, source_target_pairs={{0,3},{1,2},{2,1},{3,0},{4,7},{5,6},{6,5},{7,4},{8,11},{9,10},{10,... | collective-permute-start | bytes 270344 | tf_op jit(solution)/shard_map/ppermute | solution.py:405
  19.4 0.1 pad_add_fusion.refs_0_
  19.5 0.1 copy.29
  19.5 0.0 collective-permute-done.2.refs_2_
  19.6 2.6 %collective-permute-done.3.refs_3_ = bf16[352,128]{1,0:T(8,128)(2,1)S(1)} collective-permute-done((bf16[352,128]{1,0:T(8,128)(2,1)S(1)}, bf16[352,128]{1,0:T(8,128)(2,1)S(1)}, u32[]{:S(2)}, u32[]{:S(2)}) %collective-permute-start.3) | collective-permute-done | bytes 90144 | tf_op jit(solution)/shard_map/ppermute | solution.py:405
  22.1 0.0 copy-done.2
  22.1 0.0 copy-done.3
  22.1 0.0 copy-done.4
  22.2 14.2 %forward.1 = (bf16[256,256]{1,0:T(8,128)(2,1)S(1)}, bf16[128,256]{1,0:T(8,128)(2,1)S(1)}, bf16[1,128,256]{2,1,0:T(8,128)(2,1)S(1)}, bf16[3456,128]{1,0:T(8,128)(...) custom-call(s32[3]{0:T(128)S(1)} %pad_add_fusion.refs_0_, bf16[304,128]{1,0:T(8,128)(2,1)S(1)} %reshape.92.refs_1_, ...), custom_call_target="tpu_custom_call" | custom-call | flops 10000000000 | bytes 10000000 | tf_op jit(solution)/shard_map/forward/pallas_call | solution.py:524
  36.4 0.0 copy-start.5
  36.4 0.6 copy-done.5
  37.0 1.5 %collective-permute-start.6 = (bf16[128,256]{1,0:T(8,128)(2,1)S(1)}, bf16[128,256]{1,0:T(8,128)(2,1)S(1)}, u32[]{:S(2)}, u32[]{:S(2)}) collective-permute-start(bf16[128,256]{1,0:T(8,128)(2,1)S(1)} %bitcast.88), channel_id=1, source_target_pairs={{0,16},{16,0},{1,17},{17,1},{2,18},{18,2},{3,19},{19,3},{4,20},{20... | collective-permute-start | bytes 196616 | tf_op jit(solution)/shard_map/ppermute | solution.py:565
  38.5 2.9 %collective-permute-done.6 = bf16[128,256]{1,0:T(8,128)(2,1)S(1)} collective-permute-done((bf16[128,256]{1,0:T(8,128)(2,1)S(1)}, bf16[128,256]{1,0:T(8,128)(2,1)S(1)}, u32[]{:S(2)}, u32[]{:S(2)}) %collective-permute-start.6) | collective-permute-done | bytes 65568 | tf_op jit(solution)/shard_map/ppermute | solution.py:565
  41.5 0.0 copy-start.6
  41.5 0.8 %copy-done.6 = bf16[128,256]{1,0:T(8,128)(2,1)S(1)} copy-done((bf16[128,256]{1,0:T(8,128)(2,1)S(1)}, bf16[128,256]{1,0:T(8,128)(2,1)}, u32[]{:S(2)}) %copy-start.6) | copy-done | bytes 65560
  42.3 1.3 %down_gradient.1 = bf16[16,2,54,128]{3,2,1,0:T(8,128)(2,1)S(1)} custom-call(bf16[128,256]{1,0:T(8,128)(2,1)S(1)} %copy-done.6, bf16[1,128,256]{2,1,0:T(8,128)(2,1)S(1)} %bitcast.89, f32[128,256]{1,0:T(8,128)S(1)} %get-tuple-element.23.refs_2_, bf16[800,384]{1,0:T(8,128)(2,1)S(1)} %get-tuple-element.24.refs_3_), custom_call_target="tpu_custom_call" | custom-call | flops 2000000000 | bytes 1000000 | tf_op jit(solution)/shard_map/down_gradient/pallas_call | solution.py:575
  43.7 0.1 copy.48
  43.7 0.1 collective-permute-start.7
  43.8 1.4 %collective-permute-done.7 = bf16[8,2,54,128]{3,0,2,1:T(8,128)(2,1)S(1)} collective-permute-done((bf16[8,2,54,128]{3,0,2,1:T(8,128)(2,1)S(1)}, bf16[8,2,54,128]{3,0,2,1:T(8,128)(2,1)S(1)}, u32[]{:S(2)}, u32[]{:S(2)}) %collective-permute-start.7) | collective-permute-done | bytes 221216 | tf_op jit(solution)/shard_map/ppermute | solution.py:435
  45.3 0.1 fusion.1
  45.4 1.6 %collective-permute-start.8 = (bf16[8,54,128]{2,0,1:T(8,128)(2,1)S(1)}, bf16[8,54,128]{2,0,1:T(8,128)(2,1)S(1)}, u32[]{:S(2)}, u32[]{:S(2)}) collective-permute-start(bf16[8,54,128]{2,0,1:T(8,128)(2,1)S(1)} %dynamic-slice_bitcast_fusion.3), channel_id=1, source_target_pairs={{0,16},{16,0},{1,17},{17,1},{2,18},{18,2},{3,19},{19,3},{4,20},{20... | collective-permute-start | bytes 331784 | tf_op jit(solution)/shard_map/ppermute | solution.py:435
  46.9 0.1 collective-permute-start.4
  47.1 3.4 %collective-permute-done.8 = bf16[8,54,128]{2,0,1:T(8,128)(2,1)S(1)} collective-permute-done((bf16[8,54,128]{2,0,1:T(8,128)(2,1)S(1)}, bf16[8,54,128]{2,0,1:T(8,128)(2,1)S(1)}, u32[]{:S(2)}, u32[]{:S(2)}) %collective-permute-start.8) | collective-permute-done | bytes 110624 | tf_op jit(solution)/shard_map/ppermute | solution.py:435
  50.6 0.2 constant_dynamic-slice_fusion.1
  50.8 1.6 %collective-permute-start.9 = (bf16[4,54,128]{2,1,0:T(8,128)(2,1)S(1)}, bf16[4,54,128]{2,1,0:T(8,128)(2,1)S(1)}, u32[]{:S(2)}, u32[]{:S(2)}) collective-permute-start(bf16[4,54,128]{2,1,0:T(8,128)(2,1)S(1)} %bitcast.98), channel_id=1, source_target_pairs={{0,2},{1,3},{2,0},{3,1},{4,6},{5,7},{6,4},{7,5},{8,10},{9,11},{10,... | collective-permute-start | bytes 165896 | tf_op jit(solution)/shard_map/ppermute | solution.py:435
  52.4 0.0 collective-permute-done.4
  52.4 0.1 fusion
  52.6 0.6 collective-permute-start.5
  53.1 2.5 %collective-permute-done.9 = bf16[4,54,128]{2,1,0:T(8,128)(2,1)S(1)} collective-permute-done((bf16[4,54,128]{2,1,0:T(8,128)(2,1)S(1)}, bf16[4,54,128]{2,1,0:T(8,128)(2,1)S(1)}, u32[]{:S(2)}, u32[]{:S(2)}) %collective-permute-start.9) | collective-permute-done | bytes 55328 | tf_op jit(solution)/shard_map/ppermute | solution.py:435
  55.7 3.9 %collective-permute-done.5 = bf16[4,216,128]{2,1,0:T(8,128)(2,1)S(1)} collective-permute-done((bf16[4,216,128]{2,1,0:T(8,128)(2,1)S(1)}, bf16[4,216,128]{2,1,0:T(8,128)(2,1)S(1)}, u32[]{:S(2)}, u32[]{:S(2)}) %collective-permute-start.5) | collective-permute-done | bytes 221216 | tf_op jit(solution)/shard_map/ppermute | solution.py:435
  59.6 0.1 fusion.2
  59.7 0.1 collective-permute-start.10
  59.9 4.9 %collective-permute-done.10 = bf16[2,270,128]{2,1,0:T(8,128)(2,1)S(1)} collective-permute-done((bf16[2,270,128]{2,1,0:T(8,128)(2,1)S(1)}, bf16[2,270,128]{2,1,0:T(8,128)(2,1)S(1)}, u32[]{:S(2)}, u32[]{:S(2)}) %collective-permute-start.10) | collective-permute-done | bytes 138272 | tf_op jit(solution)/shard_map/ppermute | solution.py:435
  64.9 0.1 collective-permute-start.11
  65.0 0.7 slice_bitcast_fusion
  65.6 4.7 %collective-permute-done.11.got = bf16[270,128]{1,0:T(8,128)(2,1)S(1)} collective-permute-done((bf16[270,128]{1,0:T(8,128)(2,1)S(1)}, bf16[270,128]{1,0:T(8,128)(2,1)S(1)}, u32[]{:S(2)}, u32[]{:S(2)}) %collective-permute-start.11) | collective-permute-done | bytes 69152 | tf_op jit(solution)/shard_map/ppermute | solution.py:605
  70.4 0.8 %finish.1 = (f32[216,128]{1,0:T(8,128)}, f32[64,108]{1,0:T(8,128)}) custom-call(s32[1]{0:T(128)} %bitcast.16.index, bf16[2,270,128]{2,1,0:T(8,128)(2,1)S(1)} %fusion.3.joined, bf16[270,128]{1,0:T(8,128)(2,1)S(1)} %collective-permute-done.11.got), custom_call_target="tpu_custom_call" | custom-call | tf_op jit(solution)/shard_map/finish/pallas_call | solution.py:606
  (39 shorter events, 0.7 us)
Async XLA Ops:
  7.1 5.8 %collective-permute-start.1 = (bf16[144,128]{1,0:T(8,128)(2,1)S(1)}, bf16[144,128]{1,0:T(8,128)(2,1)S(1)}, u32[]{:S(2)}, u32[]{:S(2)}) collective-permute-start(bf16[144,128]{1,0:T(8,128)(2,1)S(1)} %pad_maximum_fusion.4), channel_id=1, source_target_pairs={{0,12},{4,0},{8,4},{12,8},{1,13},{5,1},{9,5},{13,9},{2,14},{6,2},{... | collective-permute-start | bytes 110600 | tf_op jit(solution)/shard_map/ppermute | solution.py:394
  11.4 5.9 %collective-permute-start = (bf16[160,128]{1,0:T(8,128)(2,1)S(1)}, bf16[160,128]{1,0:T(8,128)(2,1)S(1)}, u32[]{:S(2)}, u32[]{:S(2)}) collective-permute-start(bf16[160,128]{1,0:T(8,128)(2,1)S(1)} %pad_maximum_fusion.3), channel_id=1, source_target_pairs={{0,4},{4,8},{8,12},{12,0},{1,5},{5,9},{9,13},{13,1},{2,6},{6,10},{... | collective-permute-start | bytes 122888 | tf_op jit(solution)/shard_map/ppermute | solution.py:393
  11.5 0.7 %copy-start = (bf16[128,64]{0,1:T(8,128)(2,1)S(1)}, bf16[128,64]{0,1:T(8,128)(2,1)}, u32[]{:S(2)}) copy-start(bf16[128,64]{0,1:T(8,128)(2,1)} %param.10) | copy-start | bytes 49156
  11.5 0.7 copy-start.1
  17.3 4.9 %copy-start.2 = (bf16[128,3456]{1,0:T(8,128)(2,1)S(1)}, bf16[128,3456]{1,0:T(8,128)(2,1)}, u32[]{:S(2)}) copy-start(bf16[128,3456]{1,0:T(8,128)(2,1)} %refs_9_.1) | copy-start | bytes 2654212
  17.6 4.6 %copy-start.3 = (bf16[128,1728]{0,1:T(8,128)(2,1)S(1)}, bf16[128,1728]{0,1:T(8,128)(2,1)}, u32[]{:S(2)}) copy-start(bf16[128,1728]{0,1:T(8,128)(2,1)} %param.13) | copy-start | bytes 1327108
  17.7 4.5 %copy-start.4 = (bf16[64,1728]{1,0:T(8,128)(2,1)S(1)}, bf16[64,1728]{1,0:T(8,128)(2,1)}, u32[]{:S(2)}) copy-start(bf16[64,1728]{1,0:T(8,128)(2,1)} %refs_7_.1) | copy-start | bytes 663556
  17.7 1.9 %collective-permute-start.2 = (bf16[352,128]{1,0:T(8,128)(2,1)S(1)}, bf16[352,128]{1,0:T(8,128)(2,1)S(1)}, u32[]{:S(2)}, u32[]{:S(2)}) collective-permute-start(bf16[352,128]{1,0:T(8,128)(2,1)S(1)} %get-tuple-element.30), channel_id=1, source_target_pairs={{0,1},{1,0},{2,3},{3,2},{4,5},{5,4},{6,7},{7,6},{8,9},{9,8},{10,11... | collective-permute-start | bytes 270344 | tf_op jit(solution)/shard_map/ppermute | solution.py:404
  17.8 4.4 %collective-permute-start.3 = (bf16[352,128]{1,0:T(8,128)(2,1)S(1)}, bf16[352,128]{1,0:T(8,128)(2,1)S(1)}, u32[]{:S(2)}, u32[]{:S(2)}) collective-permute-start(bf16[352,128]{1,0:T(8,128)(2,1)S(1)} %get-tuple-element.29), channel_id=1, source_target_pairs={{0,3},{1,2},{2,1},{3,0},{4,7},{5,6},{6,5},{7,4},{8,11},{9,10},{10,... | collective-permute-start | bytes 270344 | tf_op jit(solution)/shard_map/ppermute | solution.py:405
  36.4 0.6 copy-start.5
  37.0 4.4 %collective-permute-start.6 = (bf16[128,256]{1,0:T(8,128)(2,1)S(1)}, bf16[128,256]{1,0:T(8,128)(2,1)S(1)}, u32[]{:S(2)}, u32[]{:S(2)}) collective-permute-start(bf16[128,256]{1,0:T(8,128)(2,1)S(1)} %bitcast.88), channel_id=1, source_target_pairs={{0,16},{16,0},{1,17},{17,1},{2,18},{18,2},{3,19},{19,3},{4,20},{20... | collective-permute-start | bytes 196616 | tf_op jit(solution)/shard_map/ppermute | solution.py:565
  41.5 0.8 %copy-start.6 = (bf16[128,256]{1,0:T(8,128)(2,1)S(1)}, bf16[128,256]{1,0:T(8,128)(2,1)}, u32[]{:S(2)}) copy-start(bf16[128,256]{1,0:T(8,128)(2,1)} %copy-done.5) | copy-start | bytes 196612
  43.7 1.5 %collective-permute-start.7 = (bf16[8,2,54,128]{3,0,2,1:T(8,128)(2,1)S(1)}, bf16[8,2,54,128]{3,0,2,1:T(8,128)(2,1)S(1)}, u32[]{:S(2)}, u32[]{:S(2)}) collective-permute-start(bf16[8,2,54,128]{3,0,2,1:T(8,128)(2,1)S(1)} %bitcast.96), channel_id=1, source_target_pairs={{0,1},{1,0},{2,3},{3,2},{4,5},{5,4},{6,7},{7,6},{8,9},{9,8},{10,11... | collective-permute-start | bytes 663560 | tf_op jit(solution)/shard_map/ppermute | solution.py:435
  45.4 5.2 %collective-permute-start.8 = (bf16[8,54,128]{2,0,1:T(8,128)(2,1)S(1)}, bf16[8,54,128]{2,0,1:T(8,128)(2,1)S(1)}, u32[]{:S(2)}, u32[]{:S(2)}) collective-permute-start(bf16[8,54,128]{2,0,1:T(8,128)(2,1)S(1)} %dynamic-slice_bitcast_fusion.3), channel_id=1, source_target_pairs={{0,16},{16,0},{1,17},{17,1},{2,18},{18,2},{3,19},{19,3},{4,20},{20... | collective-permute-start | bytes 331784 | tf_op jit(solution)/shard_map/ppermute | solution.py:435
  46.9 5.5 %collective-permute-start.4 = (bf16[8,216,128]{2,1,0:T(8,128)(2,1)S(1)}, bf16[8,216,128]{2,1,0:T(8,128)(2,1)S(1)}, u32[]{:S(2)}, u32[]{:S(2)}) collective-permute-start(bf16[8,216,128]{2,1,0:T(8,128)(2,1)S(1)} %dynamic-slice_bitcast_fusion), channel_id=1, source_target_pairs={{0,1},{1,0},{2,3},{3,2},{4,5},{5,4},{6,7},{7,6},{8,9},{9,8},{10,11... | collective-permute-start | bytes 1327112 | tf_op jit(solution)/shard_map/ppermute | solution.py:435
  50.8 4.9 %collective-permute-start.9 = (bf16[4,54,128]{2,1,0:T(8,128)(2,1)S(1)}, bf16[4,54,128]{2,1,0:T(8,128)(2,1)S(1)}, u32[]{:S(2)}, u32[]{:S(2)}) collective-permute-start(bf16[4,54,128]{2,1,0:T(8,128)(2,1)S(1)} %bitcast.98), channel_id=1, source_target_pairs={{0,2},{1,3},{2,0},{3,1},{4,6},{5,7},{6,4},{7,5},{8,10},{9,11},{10,... | collective-permute-start | bytes 165896 | tf_op jit(solution)/shard_map/ppermute | solution.py:435
  52.6 7.0 %collective-permute-start.5 = (bf16[4,216,128]{2,1,0:T(8,128)(2,1)S(1)}, bf16[4,216,128]{2,1,0:T(8,128)(2,1)S(1)}, u32[]{:S(2)}, u32[]{:S(2)}) collective-permute-start(bf16[4,216,128]{2,1,0:T(8,128)(2,1)S(1)} %dynamic-slice_bitcast_fusion.1), channel_id=1, source_target_pairs={{0,2},{1,3},{2,0},{3,1},{4,6},{5,7},{6,4},{7,5},{8,10},{9,11},{10,... | collective-permute-start | bytes 663560 | tf_op jit(solution)/shard_map/ppermute | solution.py:435
  59.7 5.1 %collective-permute-start.10 = (bf16[2,270,128]{2,1,0:T(8,128)(2,1)S(1)}, bf16[2,270,128]{2,1,0:T(8,128)(2,1)S(1)}, u32[]{:S(2)}, u32[]{:S(2)}) collective-permute-start(bf16[2,270,128]{2,1,0:T(8,128)(2,1)S(1)} %dynamic-slice_bitcast_fusion.2), channel_id=1, source_target_pairs={{0,4},{1,5},{2,6},{3,7},{4,0},{5,1},{6,2},{7,3},{8,12},{9,13},{10,... | collective-permute-start | bytes 414728 | tf_op jit(solution)/shard_map/ppermute | solution.py:435
  64.9 5.5 %collective-permute-start.11 = (bf16[270,128]{1,0:T(8,128)(2,1)S(1)}, bf16[270,128]{1,0:T(8,128)(2,1)S(1)}, u32[]{:S(2)}, u32[]{:S(2)}) collective-permute-start(bf16[270,128]{1,0:T(8,128)(2,1)S(1)} %dynamic-slice_bitcast_fusion.4), channel_id=1, source_target_pairs={{0,8},{1,9},{2,10},{3,11},{4,12},{5,13},{6,14},{7,15},{8,0},{9,1},... | collective-permute-start | bytes 207368 | tf_op jit(solution)/shard_map/ppermute | solution.py:605
